TPU v7x, 32 devices: a whole 2x2x4 slice. The times are simulated.
32 devices in a mesh: dp: 8 (over y, x, core), tensor: 4 (over z).
Axes of the slice: x: 2, y: 2, z: 4, core: 2. Of those that a mesh axis runs over, the one named last changes fastest.
Arguments:
- tokens: bfloat16 [8192, 1600], P(('dp', 'tensor')), may hold values from -6 to 6
- segment_ids: int32 [8192], P('dp'), may hold values from 0 to 15, never falling along the last dimension, each value on 1 to 1024 neighbouring positions
- out_grad: bfloat16 [8192, 1600], P(('dp', 'tensor')), may hold values from -6 to 6
- w_query: bfloat16 [1600, 1600], P('dp'), may hold values from -0.15625 to 0.15625
- w_keyval: bfloat16 [2, 1600, 320], P(None, 'dp'), may hold values from -0.15625 to 0.15625
- w_output: bfloat16 [1600, 1600], P('dp'), may hold values from -0.15625 to 0.15625
- meta_tokens: bfloat16 [128, 1600], P('dp'), may hold values from -6 to 6
- norm_gains: bfloat16 [4, 1600], P(None, 'dp'), may hold values from 0.5 to 1.5
- in_proj: bfloat16 [2, 1600, 3200], P(None, 'dp', 'tensor'), may hold values from -0.15625 to 0.15625
- x_proj: bfloat16 [4, 800, 132], P('tensor', 'dp'), may hold values from -0.109375 to 0.109375
- dt_proj: bfloat16 [100, 4, 800], P(None, 'tensor', 'dp'), may hold values from -0.625 to 0.625
- conv_weight: bfloat16 [4, 4, 800], P(None, 'tensor', 'dp'), may hold values from -3 to 3
- conv_bias: bfloat16 [4, 800], P('tensor', 'dp'), may hold values from -3 to 3
- dt_bias: bfloat16 [4, 800], P('tensor', 'dp'), may hold values from -4.59375 to -2.296875
- a_log: bfloat16 [16, 4, 800], P(None, 'tensor', 'dp'), may hold values from 0 to 2.765625
- skip_gain: bfloat16 [4, 800], P('tensor', 'dp'), may hold values from 0.5 to 1.5
- out_proj: bfloat16 [3200, 1600], P('tensor', 'dp'), may hold values from -0.109375 to 0.109375
- gate_up: bfloat16 [2, 1600, 5504], P(None, 'dp', 'tensor'), may hold values from -0.15625 to 0.15625
- w_down: bfloat16 [5504, 1600], P('tensor', 'dp'), may hold values from -0.078125 to 0.078125
Outputs:
- block_out: bfloat16 [8192, 1600], P(('dp', 'tensor'))
- tokens_grad: float32 [8192, 1600], P(('dp', 'tensor'))
- query_grad: float32 [1600, 1600], P('dp')
- keyval_grad: float32 [2, 1600, 320], P(None, 'dp')
- output_grad: float32 [1600, 1600], P('dp')
- meta_grad: float32 [128, 1600], P('dp')
- gains_grad: float32 [4, 1600], P(None, 'dp')
- inproj_grad: float32 [2, 1600, 3200], P(None, 'dp', 'tensor')
- xproj_grad: float32 [4, 800, 132], P('tensor', 'dp')
- dtproj_grad: float32 [100, 4, 800], P(None, 'tensor', 'dp')
- conv_grad: float32 [4, 4, 800], P(None, 'tensor', 'dp')
- convbias_grad: float32 [4, 800], P('tensor', 'dp')
- dtbias_grad: float32 [4, 800], P('tensor', 'dp')
- alog_grad: float32 [16, 4, 800], P(None, 'tensor', 'dp')
- skip_grad: float32 [4, 800], P('tensor', 'dp')
- outproj_grad: float32 [3200, 1600], P('tensor', 'dp')
- gateup_grad: float32 [2, 1600, 5504], P(None, 'dp', 'tensor')
- down_grad: float32 [5504, 1600], P('tensor', 'dp')
Inputs may be any that keep to these rules, and one draw needn't show every extreme that they name: `segment_ids`: segment numbers never fall along the whole array; each number covers 1 to 1024 consecutive positions and one covers exactly 1024.
All inputs are finite; a program needn't handle non-finite values.
Results may differ from a plain program's by a relative error of at most 0.018.
Values may be sent and summed in bfloat16 or wider, within the bound.
A program may use at most 384 MiB of HBM per device.

v0:
```python
import math

import jax
import jax.numpy as jnp
from jax import lax
from jax.sharding import PartitionSpec as P

HEADS = 25
KV_HEADS = 5
HEAD_DIM = 64
META = 128
STATE = 16
CONV = 4
DTR = 100
SEQ_LEN = 256
SCAN_BLOCK = 16


EPSILON = 1e-05
ROPE_BASE = 10000.0
NEG_FILL = -1e30


def plain_dot(former, latter):
    return jnp.dot(former, latter, preferred_element_type=jnp.float32)


def contract_rows(former, latter):
    return lax.dot_general(
        former, latter, (((0,), (0,)), ((), ())), preferred_element_type=jnp.float32
    )


def contract_cols(former, latter):
    return lax.dot_general(
        former, latter, (((1,), (1,)), ((), ())), preferred_element_type=jnp.float32
    )


def contract_rows_exact(former, latter):
    return lax.dot_general(
        former,
        latter,
        (((0,), (0,)), ((), ())),
        precision=lax.Precision.HIGHEST,
        preferred_element_type=jnp.float32,
    )


def contract_cols_exact(former, latter):
    return lax.dot_general(
        former,
        latter,
        (((1,), (1,)), ((), ())),
        precision=lax.Precision.HIGHEST,
        preferred_element_type=jnp.float32,
    )


def mix_sum(pattern, former, latter):
    return jnp.einsum(pattern, former, latter, preferred_element_type=jnp.float32)


def inverse_rms(operand):
    return lax.rsqrt(jnp.mean(operand * operand, axis=-1, keepdims=True) + EPSILON)


def norm_backward(cotangent, normed, scaling):
    return scaling * (cotangent - normed * jnp.mean(cotangent * normed, axis=-1, keepdims=True))


def swish_slope(operand):
    sigmoid = jax.nn.sigmoid(operand)
    return sigmoid * (1.0 + operand * (1.0 - sigmoid))


def rotary_tables(row_count):
    places = (jnp.arange(row_count, dtype=jnp.int32) % SEQ_LEN).astype(jnp.float32)
    powers = jnp.arange(HEAD_DIM // 2, dtype=jnp.int32).astype(jnp.float32) * (2.0 / HEAD_DIM)
    angles = places[:, None] * jnp.power(ROPE_BASE, -powers)[None, :]
    return (jnp.cos(angles)[:, None, :], jnp.sin(angles)[:, None, :])


def rotate_pairs(operand, cosine_table, sine_table):
    half_dim = operand.shape[-1] // 2
    leading = operand[..., :half_dim]
    trailing = operand[..., half_dim:]
    return jnp.concatenate(
        [
            leading * cosine_table - trailing * sine_table,
            leading * sine_table + trailing * cosine_table,
        ],
        axis=-1,
    )


def segment_mask(segments):
    per_sequence = segments.reshape(-1, SEQ_LEN)
    places = jnp.arange(SEQ_LEN, dtype=jnp.int32)
    return (per_sequence[:, :, None] == per_sequence[:, None, :]) & (
        places[:, None] >= places[None, :]
    )


def segment_offsets(segments):
    places = jnp.arange(segments.shape[0], dtype=jnp.int32)
    before = jnp.concatenate([segments[:1] - 1, segments[:-1]])
    fresh = (places % SEQ_LEN == 0) | (segments != before)
    begins = lax.cummax(jnp.where(fresh, places, 0), axis=0)
    return places - begins


def attention_inputs(
    normed_low, meta_low, query_weight, key_weight, value_weight, cosine_table, sine_table
):
    row_count = normed_low.shape[0]
    seq_count = row_count // SEQ_LEN
    groups = HEADS // KV_HEADS
    queries = rotate_pairs(
        plain_dot(normed_low, query_weight).reshape(row_count, HEADS, HEAD_DIM),
        cosine_table,
        sine_table,
    )
    keys_rot = rotate_pairs(
        plain_dot(normed_low, key_weight).reshape(row_count, KV_HEADS, HEAD_DIM),
        cosine_table,
        sine_table,
    )
    query_low = queries.astype(jnp.bfloat16).reshape(seq_count, SEQ_LEN, KV_HEADS, groups, HEAD_DIM)
    key_low = keys_rot.astype(jnp.bfloat16).reshape(seq_count, SEQ_LEN, KV_HEADS, HEAD_DIM)
    value_low = (
        plain_dot(normed_low, value_weight)
        .astype(jnp.bfloat16)
        .reshape(seq_count, SEQ_LEN, KV_HEADS, HEAD_DIM)
    )
    meta_keys = (
        plain_dot(meta_low, key_weight).astype(jnp.bfloat16).reshape(META, KV_HEADS, HEAD_DIM)
    )
    meta_values = (
        plain_dot(meta_low, value_weight).astype(jnp.bfloat16).reshape(META, KV_HEADS, HEAD_DIM)
    )
    return (query_low, key_low, value_low, meta_keys, meta_values)


def attention_scores(query_low, key_low, meta_keys, allowed):
    score_scale = 1.0 / math.sqrt(HEAD_DIM)
    meta_scores = mix_sum("slkgd,nkd->skgln", query_low, meta_keys) * score_scale
    own_scores = mix_sum("slkgd,smkd->skglm", query_low, key_low) * score_scale
    own_scores = jnp.where(allowed[:, None, None], own_scores, NEG_FILL)
    return (meta_scores, own_scores)


def attention_forward(query_low, key_low, value_low, meta_keys, meta_values, allowed):
    meta_scores, own_scores = attention_scores(query_low, key_low, meta_keys, allowed)
    highest = jnp.maximum(jnp.max(meta_scores, axis=-1), jnp.max(own_scores, axis=-1))
    totals = jnp.sum(jnp.exp(meta_scores - highest[..., None]), axis=-1) + jnp.sum(
        jnp.exp(own_scores - highest[..., None]), axis=-1
    )
    log_total = highest + jnp.log(totals)
    meta_probs = jnp.exp(meta_scores - log_total[..., None]).astype(jnp.bfloat16)
    own_probs = jnp.exp(own_scores - log_total[..., None]).astype(jnp.bfloat16)
    mixed_heads = mix_sum("skgln,nkd->slkgd", meta_probs, meta_values) + mix_sum(
        "skglm,smkd->slkgd", own_probs, value_low
    )
    row_count = query_low.shape[0] * SEQ_LEN
    return (mixed_heads.reshape(row_count, HEADS * HEAD_DIM).astype(jnp.bfloat16), log_total)


def attention_backward(
    cotangent_low,
    query_low,
    key_low,
    value_low,
    meta_keys,
    meta_values,
    allowed,
    log_total,
    cosine_table,
    sine_table,
):
    row_count = query_low.shape[0] * SEQ_LEN
    score_scale = 1.0 / math.sqrt(HEAD_DIM)
    cotangent_low = cotangent_low.reshape(query_low.shape)
    meta_scores, own_scores = attention_scores(query_low, key_low, meta_keys, allowed)
    meta_probs = jnp.exp(meta_scores - log_total[..., None])
    own_probs = jnp.exp(own_scores - log_total[..., None])
    meta_dprob = mix_sum("slkgd,nkd->skgln", cotangent_low, meta_values)
    own_dprob = mix_sum("slkgd,smkd->skglm", cotangent_low, value_low)
    row_delta = jnp.sum(meta_probs * meta_dprob, axis=-1) + jnp.sum(own_probs * own_dprob, axis=-1)
    meta_dscore = (meta_probs * (meta_dprob - row_delta[..., None]) * score_scale).astype(
        jnp.bfloat16
    )
    own_dscore = (own_probs * (own_dprob - row_delta[..., None]) * score_scale).astype(jnp.bfloat16)
    back_query = mix_sum("skgln,nkd->slkgd", meta_dscore, meta_keys) + mix_sum(
        "skglm,smkd->slkgd", own_dscore, key_low
    )
    back_query = (
        rotate_pairs(back_query.reshape(row_count, HEADS, HEAD_DIM), cosine_table, -sine_table)
        .reshape(row_count, -1)
        .astype(jnp.bfloat16)
    )
    back_key = mix_sum("skglm,slkgd->smkd", own_dscore, query_low)
    back_key = (
        rotate_pairs(back_key.reshape(row_count, KV_HEADS, HEAD_DIM), cosine_table, -sine_table)
        .reshape(row_count, -1)
        .astype(jnp.bfloat16)
    )
    back_value = (
        mix_sum("skglm,slkgd->smkd", own_probs.astype(jnp.bfloat16), cotangent_low)
        .reshape(row_count, -1)
        .astype(jnp.bfloat16)
    )
    back_meta_key = mix_sum("skgln,slkgd->nkd", meta_dscore, query_low).reshape(META, -1)
    back_meta_value = mix_sum(
        "skgln,slkgd->nkd", meta_probs.astype(jnp.bfloat16), cotangent_low
    ).reshape(META, -1)
    return (back_query, back_key, back_value, back_meta_key, back_meta_value)


def causal_conv(mamba_in, conv_taps, conv_shift, offsets):
    totals = conv_shift[None] + conv_taps[0][None] * mamba_in
    for lag_count in range(1, CONV):
        lagged = jnp.concatenate(
            [jnp.zeros((lag_count, mamba_in.shape[1]), mamba_in.dtype), mamba_in[:-lag_count]]
        )
        totals = totals + jnp.where(
            (offsets >= lag_count)[:, None], conv_taps[lag_count][None] * lagged, 0.0
        )
    return totals


def causal_conv_grad(cotangent, mamba_in, conv_taps, offsets):
    back_input = conv_taps[0][None] * cotangent
    tap_grads = [jnp.sum(cotangent * mamba_in, axis=0)]
    for lag_count in range(1, CONV):
        masked = jnp.where((offsets >= lag_count)[:, None], cotangent, 0.0)
        padding = jnp.zeros((lag_count, mamba_in.shape[1]), mamba_in.dtype)
        lagged = jnp.concatenate([padding, mamba_in[:-lag_count]])
        tap_grads.append(jnp.sum(masked * lagged, axis=0))
        back_input = back_input + conv_taps[lag_count][None] * jnp.concatenate(
            [masked[lag_count:], padding]
        )
    return (back_input, jnp.stack(tap_grads), jnp.sum(cotangent, axis=0))


def into_blocks(operand):
    seq_count = operand.shape[0] // SEQ_LEN
    shaped = operand.reshape((seq_count, SEQ_LEN // SCAN_BLOCK, SCAN_BLOCK) + operand.shape[1:])
    return jnp.swapaxes(shaped, 0, 1)


def out_of_blocks(operand):
    return jnp.swapaxes(operand, 0, 1).reshape((-1,) + operand.shape[3:])


def scan_step(running, feed_block, step_block, input_block, keep_block, offset, decay_rate):
    decays = (
        jnp.exp(step_block[:, offset, None, :] * decay_rate[None])
        * keep_block[:, offset, None, None]
    )
    driven = step_block[:, offset] * feed_block[:, offset]
    return (decays * running + driven[:, None, :] * input_block[:, offset, :, None], decays)


def selective_scan(feed_rows, step_size, input_mat, output_mat, decay_rate, keep_state):
    seq_count = feed_rows.shape[0] // SEQ_LEN
    initial = jnp.zeros((seq_count, decay_rate.shape[0], feed_rows.shape[1]), feed_rows.dtype)

    def advance(running, pieces):
        feed_block, step_block, input_block, output_block, keep_block = pieces
        entering = running
        outputs = []
        for offset in range(SCAN_BLOCK):
            running, decays = scan_step(
                running, feed_block, step_block, input_block, keep_block, offset, decay_rate
            )
            outputs.append(jnp.sum(output_block[:, offset, :, None] * running, axis=1))
        return (running, (entering, jnp.stack(outputs, axis=1)))

    pieces = tuple(
        (
            into_blocks(operand)
            for operand in (feed_rows, step_size, input_mat, output_mat, keep_state)
        )
    )
    finished, (starts, outputs) = lax.scan(advance, initial, pieces)
    return (out_of_blocks(outputs), starts)


def selective_scan_grad(
    cotangent, feed_rows, step_size, input_mat, output_mat, decay_rate, keep_state, starts
):
    seq_count = feed_rows.shape[0] // SEQ_LEN

    def retreat(carried, pieces):
        back_state, back_rate = carried
        back_block, feed_block, step_block, input_block, output_block, keep_block, entering = pieces
        states = [entering]
        decay_list = []
        running = entering
        for offset in range(SCAN_BLOCK):
            running, decays = scan_step(
                running, feed_block, step_block, input_block, keep_block, offset, decay_rate
            )
            states.append(running)
            decay_list.append(decays)
        back_feed = [None] * SCAN_BLOCK
        back_step = [None] * SCAN_BLOCK
        back_input = [None] * SCAN_BLOCK
        back_output = [None] * SCAN_BLOCK
        for offset in reversed(range(SCAN_BLOCK)):
            back_state = (
                back_state + output_block[:, offset, :, None] * back_block[:, offset, None, :]
            )
            back_output[offset] = jnp.sum(
                back_block[:, offset, None, :] * states[offset + 1], axis=2
            )
            driven = step_block[:, offset] * feed_block[:, offset]
            back_input[offset] = jnp.sum(back_state * driven[:, None, :], axis=2)
            back_driven = jnp.sum(back_state * input_block[:, offset, :, None], axis=1)
            through = back_state * decay_list[offset] * states[offset]
            back_feed[offset] = back_driven * step_block[:, offset]
            back_step[offset] = back_driven * feed_block[:, offset] + jnp.sum(
                through * decay_rate[None], axis=1
            )
            back_rate = back_rate + jnp.sum(through * step_block[:, offset, None, :], axis=0)
            back_state = back_state * decay_list[offset]
        return (
            (back_state, back_rate),
            (
                jnp.stack(back_feed, axis=1),
                jnp.stack(back_step, axis=1),
                jnp.stack(back_input, axis=1),
                jnp.stack(back_output, axis=1),
            ),
        )

    initial = (
        jnp.zeros((seq_count, decay_rate.shape[0], feed_rows.shape[1]), feed_rows.dtype),
        jnp.zeros(decay_rate.shape, feed_rows.dtype),
    )
    pieces = tuple(
        (
            into_blocks(operand)
            for operand in (cotangent, feed_rows, step_size, input_mat, output_mat, keep_state)
        )
    ) + (starts,)
    (back_state, back_rate), (back_feed, back_step, back_input, back_output) = lax.scan(
        retreat, initial, pieces, reverse=True
    )
    return (
        out_of_blocks(back_feed),
        out_of_blocks(back_step),
        out_of_blocks(back_input),
        out_of_blocks(back_output),
        back_rate,
    )


def prepare(gathered):
    (
        query_weight,
        keyval_weight,
        output_weight,
        meta_rows,
        gain_rows,
        inproj_weight,
        xproj_weight,
        dtproj_weight,
        conv_taps,
        conv_shift,
        dt_shift,
        decay_log,
        skip_weight,
        outproj_weight,
        gateup_weight,
        down_weight,
    ) = gathered
    return (
        query_weight,
        keyval_weight,
        output_weight,
        meta_rows,
        gain_rows.astype(jnp.float32),
        inproj_weight,
        xproj_weight[0],
        dtproj_weight[:, 0],
        conv_taps[:, 0].astype(jnp.float32),
        conv_shift[0].astype(jnp.float32),
        dt_shift[0].astype(jnp.float32),
        -jnp.exp(decay_log[:, 0].astype(jnp.float32)),
        skip_weight[0].astype(jnp.float32),
        outproj_weight,
        gateup_weight,
        down_weight,
    )


def per_device(
    tokens,
    segment_ids,
    out_grad,
    w_query,
    w_keyval,
    w_output,
    meta_tokens,
    norm_gains,
    in_proj,
    x_proj,
    dt_proj,
    conv_weight,
    conv_bias,
    dt_bias,
    a_log,
    skip_gain,
    out_proj,
    gate_up,
    w_down,
):
    local = prepare(
        (
            lax.all_gather(w_query, "dp", axis=0, tiled=True),
            lax.all_gather(w_keyval, "dp", axis=1, tiled=True),
            lax.all_gather(w_output, "dp", axis=0, tiled=True),
            lax.all_gather(meta_tokens, "dp", axis=0, tiled=True),
            lax.all_gather(norm_gains, "dp", axis=1, tiled=True),
            lax.all_gather(in_proj, "dp", axis=1, tiled=True),
            lax.all_gather(x_proj, "dp", axis=1, tiled=True),
            lax.all_gather(dt_proj, "dp", axis=2, tiled=True),
            lax.all_gather(conv_weight, "dp", axis=2, tiled=True),
            lax.all_gather(conv_bias, "dp", axis=1, tiled=True),
            lax.all_gather(dt_bias, "dp", axis=1, tiled=True),
            lax.all_gather(a_log, "dp", axis=2, tiled=True),
            lax.all_gather(skip_gain, "dp", axis=1, tiled=True),
            lax.all_gather(out_proj, "dp", axis=1, tiled=True),
            lax.all_gather(gate_up, "dp", axis=1, tiled=True),
            lax.all_gather(w_down, "dp", axis=1, tiled=True),
        )
    )
    (
        query_weight,
        keyval_weight,
        output_weight,
        meta_rows,
        gain_rows,
        inproj_weight,
        xproj_weight,
        dtproj_weight,
        conv_taps,
        conv_shift,
        dt_shift,
        decay_rate,
        skip_weight,
        outproj_weight,
        gateup_weight,
        down_weight,
    ) = local
    token_count = tokens.shape[0]
    member = lax.axis_index("tensor")
    own_segments = lax.dynamic_slice_in_dim(segment_ids, member * token_count, token_count)
    residual = tokens.astype(jnp.float32)
    scale_one = inverse_rms(residual)
    normed_one = residual * scale_one
    normed_low = (normed_one * gain_rows[0]).astype(jnp.bfloat16)
    meta_float = meta_rows.astype(jnp.float32)
    meta_scale = inverse_rms(meta_float)
    meta_normed = meta_float * meta_scale
    meta_low = (meta_normed * gain_rows[0]).astype(jnp.bfloat16)
    cosine_table, sine_table = rotary_tables(token_count)
    allowed = segment_mask(own_segments)
    query_low, key_low, value_low, meta_keys, meta_values = attention_inputs(
        normed_low,
        meta_low,
        query_weight,
        keyval_weight[0],
        keyval_weight[1],
        cosine_table,
        sine_table,
    )
    attended, log_total = attention_forward(
        query_low, key_low, value_low, meta_keys, meta_values, allowed
    )
    attn_out = plain_dot(attended, output_weight)
    normed_all, grad_all = (
        lax.all_gather(normed_low, "tensor", axis=0, tiled=True),
        lax.all_gather(out_grad, "tensor", axis=0, tiled=True),
    )
    offsets = segment_offsets(segment_ids)
    mamba_in = plain_dot(normed_all, inproj_weight[0])
    gate_raw = plain_dot(normed_all, inproj_weight[1])
    conv_raw = causal_conv(mamba_in, conv_taps, conv_shift, offsets)
    feed_rows = jax.nn.silu(conv_raw)
    feed_low = feed_rows.astype(jnp.bfloat16)
    projected = lax.psum(plain_dot(feed_low, xproj_weight), "tensor")
    rank_low = projected[:, :DTR].astype(jnp.bfloat16)
    step_raw = plain_dot(rank_low, dtproj_weight) + dt_shift
    step_size = jax.nn.softplus(step_raw)
    input_mat = projected[:, DTR : DTR + STATE]
    output_mat = projected[:, DTR + STATE :]
    keep_state = (offsets > 0).astype(jnp.float32)
    scanned, starts = selective_scan(
        feed_rows, step_size, input_mat, output_mat, decay_rate, keep_state
    )
    combined = scanned + skip_weight * feed_rows
    gate_act = jax.nn.silu(gate_raw)
    mamba_low = (combined * gate_act).astype(jnp.bfloat16)
    mamba_out = lax.psum_scatter(
        plain_dot(mamba_low, outproj_weight), "tensor", scatter_dimension=0, tiled=True
    )
    attn_scale = inverse_rms(attn_out)
    attn_normed = attn_out * attn_scale
    mamba_scale = inverse_rms(mamba_out)
    mamba_normed = mamba_out * mamba_scale
    mixed_rows = residual + 0.5 * (attn_normed * gain_rows[1] + mamba_normed * gain_rows[2])
    scale_two = inverse_rms(mixed_rows)
    normed_two = mixed_rows * scale_two
    ffn_low = (normed_two * gain_rows[3]).astype(jnp.bfloat16)
    ffn_all = lax.all_gather(ffn_low, "tensor", axis=0, tiled=True)
    gate_pre = plain_dot(ffn_all, gateup_weight[0])
    up_pre = plain_dot(ffn_all, gateup_weight[1])
    gate_swish = jax.nn.silu(gate_pre)
    hidden_low = (gate_swish * up_pre).astype(jnp.bfloat16)
    ffn_out = lax.psum_scatter(
        plain_dot(hidden_low, down_weight).astype(jnp.bfloat16),
        "tensor",
        scatter_dimension=0,
        tiled=True,
    ).astype(jnp.float32)
    block_out = (mixed_rows + ffn_out).astype(jnp.bfloat16)
    local = prepare(
        (
            lax.all_gather(w_query, "dp", axis=0, tiled=True),
            lax.all_gather(w_keyval, "dp", axis=1, tiled=True),
            lax.all_gather(w_output, "dp", axis=0, tiled=True),
            lax.all_gather(meta_tokens, "dp", axis=0, tiled=True),
            lax.all_gather(norm_gains, "dp", axis=1, tiled=True),
            lax.all_gather(in_proj, "dp", axis=1, tiled=True),
            lax.all_gather(x_proj, "dp", axis=1, tiled=True),
            lax.all_gather(dt_proj, "dp", axis=2, tiled=True),
            lax.all_gather(conv_weight, "dp", axis=2, tiled=True),
            lax.all_gather(conv_bias, "dp", axis=1, tiled=True),
            lax.all_gather(dt_bias, "dp", axis=1, tiled=True),
            lax.all_gather(a_log, "dp", axis=2, tiled=True),
            lax.all_gather(skip_gain, "dp", axis=1, tiled=True),
            lax.all_gather(out_proj, "dp", axis=1, tiled=True),
            lax.all_gather(gate_up, "dp", axis=1, tiled=True),
            lax.all_gather(w_down, "dp", axis=1, tiled=True),
        )
    )
    (
        query_weight,
        keyval_weight,
        output_weight,
        meta_rows,
        gain_rows,
        inproj_weight,
        xproj_weight,
        dtproj_weight,
        conv_taps,
        conv_shift,
        dt_shift,
        decay_rate,
        skip_weight,
        outproj_weight,
        gateup_weight,
        down_weight,
    ) = local
    grad_float = out_grad.astype(jnp.float32)
    g_down = contract_rows(hidden_low, grad_all)
    g_hidden = contract_cols(grad_all, down_weight)
    g_gate_low = (g_hidden * up_pre * swish_slope(gate_pre)).astype(jnp.bfloat16)
    g_up_low = (g_hidden * gate_swish).astype(jnp.bfloat16)
    g_gateup = jnp.stack([contract_rows(ffn_all, g_gate_low), contract_rows(ffn_all, g_up_low)])
    g_ffn_in = lax.psum_scatter(
        contract_cols(g_gate_low, gateup_weight[0]) + contract_cols(g_up_low, gateup_weight[1]),
        "tensor",
        scatter_dimension=0,
        tiled=True,
    )
    g_gain_ffn = jnp.sum(g_ffn_in * normed_two, axis=0)
    g_mixed = grad_float + norm_backward(g_ffn_in * gain_rows[3], normed_two, scale_two)
    half_grad = 0.5 * g_mixed
    g_gain_attn = jnp.sum(half_grad * attn_normed, axis=0)
    g_attn = norm_backward(half_grad * gain_rows[1], attn_normed, attn_scale)
    g_gain_mamba = jnp.sum(half_grad * mamba_normed, axis=0)
    g_mamba = norm_backward(half_grad * gain_rows[2], mamba_normed, mamba_scale)
    g_mamba_all = lax.all_gather(g_mamba.astype(jnp.bfloat16), "tensor", axis=0, tiled=True)
    g_outproj = contract_rows(mamba_low, g_mamba_all)
    g_gated = contract_cols(g_mamba_all, outproj_weight)
    g_combined = g_gated * gate_act
    g_skip = jnp.sum(g_combined * feed_rows, axis=0)
    g_gate_raw = g_gated * combined * swish_slope(gate_raw)
    g_feed_scan, g_step, g_input_mat, g_output_mat, g_rate = selective_scan_grad(
        g_combined, feed_rows, step_size, input_mat, output_mat, decay_rate, keep_state, starts
    )
    g_step_raw = g_step * jax.nn.sigmoid(step_raw)
    g_dt_shift = jnp.sum(g_step_raw, axis=0)
    g_step_low = g_step_raw.astype(jnp.bfloat16)
    g_dtproj = contract_rows(rank_low, g_step_low)
    g_projected = lax.psum(
        jnp.concatenate(
            [contract_cols(g_step_low, dtproj_weight), g_input_mat, g_output_mat], axis=1
        ),
        "tensor",
    )
    g_projected_low = g_projected.astype(jnp.bfloat16)
    g_xproj = contract_rows(feed_low, g_projected_low)
    g_feed = g_combined * skip_weight + g_feed_scan + contract_cols(g_projected_low, xproj_weight)
    g_conv_raw = g_feed * swish_slope(conv_raw)
    g_mamba_in, g_conv_taps, g_conv_shift = causal_conv_grad(
        g_conv_raw, mamba_in, conv_taps, offsets
    )
    g_in_low = g_mamba_in.astype(jnp.bfloat16)
    g_gate_raw_low = g_gate_raw.astype(jnp.bfloat16)
    g_inproj = jnp.stack(
        [contract_rows(normed_all, g_in_low), contract_rows(normed_all, g_gate_raw_low)]
    )
    g_normed = lax.psum_scatter(
        (
            contract_cols(g_in_low, inproj_weight[0])
            + contract_cols(g_gate_raw_low, inproj_weight[1])
        ).astype(jnp.bfloat16),
        "tensor",
        scatter_dimension=0,
        tiled=True,
    ).astype(jnp.float32)
    g_attn_low = g_attn.astype(jnp.bfloat16)
    g_output = contract_rows(attended, g_attn_low)
    g_attended = contract_cols(g_attn_low, output_weight).astype(jnp.bfloat16)
    g_query_low, g_key_low, g_value_low, g_meta_key, g_meta_value = attention_backward(
        g_attended,
        query_low,
        key_low,
        value_low,
        meta_keys,
        meta_values,
        allowed,
        log_total,
        cosine_table,
        sine_table,
    )
    meta_exact = meta_low.astype(jnp.float32)
    key_float = keyval_weight[0].astype(jnp.float32)
    value_float = keyval_weight[1].astype(jnp.float32)
    g_query = contract_rows(normed_low, g_query_low)
    g_keyval = jnp.stack(
        [
            contract_rows(normed_low, g_key_low) + contract_rows_exact(meta_exact, g_meta_key),
            contract_rows(normed_low, g_value_low) + contract_rows_exact(meta_exact, g_meta_value),
        ]
    )
    g_normed = (
        g_normed
        + contract_cols(g_query_low, query_weight)
        + contract_cols(g_key_low, keyval_weight[0])
        + contract_cols(g_value_low, keyval_weight[1])
    )
    g_meta_normed = contract_cols_exact(g_meta_key, key_float) + contract_cols_exact(
        g_meta_value, value_float
    )
    g_gain_in = jnp.sum(g_normed * normed_one, axis=0) + jnp.sum(
        g_meta_normed * meta_normed, axis=0
    )
    tokens_grad = g_mixed + norm_backward(g_normed * gain_rows[0], normed_one, scale_one)
    g_meta = norm_backward(g_meta_normed * gain_rows[0], meta_normed, meta_scale)
    g_gains = jnp.stack([g_gain_in, g_gain_attn, g_gain_mamba, g_gain_ffn])
    reduced = (
        lax.psum_scatter(g_query, "dp", scatter_dimension=0, tiled=True),
        lax.psum_scatter(g_keyval, "dp", scatter_dimension=1, tiled=True),
        lax.psum_scatter(g_output, "dp", scatter_dimension=0, tiled=True),
        lax.psum_scatter(g_meta, "dp", scatter_dimension=0, tiled=True),
        lax.psum_scatter(g_gains, "dp", scatter_dimension=1, tiled=True),
        lax.psum_scatter(g_inproj, "dp", scatter_dimension=1, tiled=True),
        lax.psum_scatter(g_xproj[None], "dp", scatter_dimension=1, tiled=True),
        lax.psum_scatter(g_dtproj[:, None], "dp", scatter_dimension=2, tiled=True),
        lax.psum_scatter(g_conv_taps[:, None], "dp", scatter_dimension=2, tiled=True),
        lax.psum_scatter(g_conv_shift[None], "dp", scatter_dimension=1, tiled=True),
        lax.psum_scatter(g_dt_shift[None], "dp", scatter_dimension=1, tiled=True),
        lax.psum_scatter((g_rate * decay_rate)[:, None], "dp", scatter_dimension=2, tiled=True),
        lax.psum_scatter(g_skip[None], "dp", scatter_dimension=1, tiled=True),
        lax.psum_scatter(g_outproj, "dp", scatter_dimension=1, tiled=True),
        lax.psum_scatter(g_gateup, "dp", scatter_dimension=1, tiled=True),
        lax.psum_scatter(g_down, "dp", scatter_dimension=1, tiled=True),
    )
    shared = (
        lax.psum(reduced[0].astype(jnp.bfloat16), "tensor").astype(jnp.float32),
        lax.psum(reduced[1].astype(jnp.bfloat16), "tensor").astype(jnp.float32),
        lax.psum(reduced[2].astype(jnp.bfloat16), "tensor").astype(jnp.float32),
        lax.psum(reduced[3].astype(jnp.bfloat16), "tensor").astype(jnp.float32),
        lax.psum(reduced[4].astype(jnp.bfloat16), "tensor").astype(jnp.float32),
    )
    return (
        block_out,
        tokens_grad,
        shared[0],
        shared[1],
        shared[2],
        shared[3],
        shared[4],
        reduced[5],
        reduced[6],
        reduced[7],
        reduced[8],
        reduced[9],
        reduced[10],
        reduced[11],
        reduced[12],
        reduced[13],
        reduced[14],
        reduced[15],
    )


def solution(mesh):
    in_specs = (
        P(("dp", "tensor"), None),
        P("dp"),
        P(("dp", "tensor"), None),
        P("dp", None),
        P(None, "dp", None),
        P("dp", None),
        P("dp", None),
        P(None, "dp"),
        P(None, "dp", "tensor"),
        P("tensor", "dp", None),
        P(None, "tensor", "dp"),
        P(None, "tensor", "dp"),
        P("tensor", "dp"),
        P("tensor", "dp"),
        P(None, "tensor", "dp"),
        P("tensor", "dp"),
        P("tensor", "dp"),
        P(None, "dp", "tensor"),
        P("tensor", "dp"),
    )
    out_specs = (
        P(("dp", "tensor"), None),
        P(("dp", "tensor"), None),
        P("dp", None),
        P(None, "dp", None),
        P("dp", None),
        P("dp", None),
        P(None, "dp"),
        P(None, "dp", "tensor"),
        P("tensor", "dp", None),
        P(None, "tensor", "dp"),
        P(None, "tensor", "dp"),
        P("tensor", "dp"),
        P("tensor", "dp"),
        P(None, "tensor", "dp"),
        P("tensor", "dp"),
        P("tensor", "dp"),
        P(None, "dp", "tensor"),
        P("tensor", "dp"),
    )
    return jax.shard_map(
        per_device, mesh=mesh, in_specs=in_specs, out_specs=out_specs, check_vma=False
    )
```

profile of v0, /device:TPU:0, one launch (start us, length us, event | category | flops | bytes accessed | tf_op | source)
XLA Modules:
  0.0 2667.7 jit_solution(4306622983411048931)
XLA Ops:
  7.3 10.7 all-gather
  23.5 9.5 all_gather.79
  37.0 14.2 all-reduce.25
  51.4 9.7 all_gather.82
  63.8 12.4 slice_reduce_fusion.35
  76.3 12.2 all-gather.19.cloned.1.call-done
  88.5 43.2 %all-gather.21.cloned.1.call-done = bf16[2,1600,800]{2,1,0:T(8,128)(2,1)} async-done(((bf16[2,200,800]{2,1,0:T(8,128)(2,1)}), bf16[2,1600,800]{2,1,0:T(8,128)(2,1)}) %all-gather.21.cloned.1.call-update) | async-done | bytes 5120016 | tf_op jit(solution)/shard_map/all_gather | solution.py:427
  131.6 6.3 fusion.88
  147.8 10.6 all_gather.83
  159.9 8.7 all_gather.85
  176.6 6.2 copy.225
  183.4 5.7 compare_select_fusion
  189.1 4.9 copy.214
  194.0 6.3 copy.223
  207.6 395.9 %while.40 = (s32[]{:T(128)}, f32[4,16,800]{2,1,0:T(8,128)}, f32[16,4,16,800]{3,2,1,0:T(8,128)}, f32[16,4,16,800]{3,2,1,0:T(8,128)}, f32[16,4,16,800]{3,1,2,0:T(4...) while((s32[]{:T(128)}, f32[4,16,800]{2,1,0:T(8,128)}, ...), condition=%wide.region_27.28_spmd.clone, body=%wide.region_10.27_spmd.clone.sunk | while | flops 8192003 | bytes 9039557 | solution.py:286
  607.6 5.0 copy.227
  612.6 10.0 multiply_convert_fusion.4
  622.6 8.5 fusion.192
  632.0 10.8 all_gather.73
  659.6 5.1 fusion.184
  672.6 6.7 multiply_reduce_fusion.109
  679.3 67.3 %reduce-scatter.28.cloned.1.call-done = f32[256,1600]{0,1:T(8,128)} async-done(((f32[1024,1600]{0,1:T(8,128)}), f32[256,1600]{0,1:T(8,128)}) %reduce-scatter.28.cloned.1.call-update) | async-done | bytes 1638416 | tf_op jit(solution)/shard_map/reduce_scatter | solution.py:507
  754.6 51.3 %all-gather.27.cloned.1.call-done = bf16[2,1600,1376]{2,1,0:T(8,128)(2,1)} async-done(((bf16[2,200,1376]{2,1,0:T(8,128)(2,1)}), bf16[2,1600,1376]{2,1,0:T(8,128)(2,1)}) %all-gather.27.cloned.1.call-update) | async-done | bytes 8806416 | tf_op jit(solution)/shard_map/all_gather | solution.py:436
  805.9 67.6 %all-gather.25.cloned.1.call-done = bf16[1024,1600]{0,1:T(8,128)(2,1)} async-done(((bf16[256,1600]{0,1:T(8,128)(2,1)}), bf16[1024,1600]{0,1:T(8,128)(2,1)}) %all-gather.25.cloned.1.call-update) | async-done | bytes 3276816 | tf_op jit(solution)/shard_map/all_gather | solution.py:518
  873.5 10.3 fusion.71
  883.8 7.2 fusion.72
  890.9 47.9 %all-gather.31.cloned.1.call-done = bf16[1024,1600]{0,1:T(8,128)(2,1)} async-done(((bf16[256,1600]{0,1:T(8,128)(2,1)}), bf16[1024,1600]{0,1:T(8,128)(2,1)}) %all-gather.31.cloned.1.call-update) | async-done | bytes 3276816 | tf_op jit(solution)/shard_map/all_gather | solution.py:486
  938.8 37.8 %all-gather.29.cloned.1.call-done = bf16[1376,1600]{0,1:T(8,128)(2,1)} async-done(((bf16[1376,200]{0,1:T(8,128)(2,1)}), bf16[1376,1600]{0,1:T(8,128)(2,1)}) %all-gather.29.cloned.1.call-update) | async-done | bytes 4403216 | tf_op jit(solution)/shard_map/all_gather | solution.py:437
  976.7 15.2 multiply_convert_fusion
  991.9 8.1 fusion.70
  1000.0 7.4 convolution_add_fusion
  1007.4 9.1 convolution_convert_fusion
  1016.6 106.0 %reduce-scatter.32.cloned.1.call-done = f32[256,1600]{0,1:T(8,128)} async-done(((f32[1024,1600]{0,1:T(8,128)}), f32[256,1600]{0,1:T(8,128)}) %reduce-scatter.32.cloned.1.call-update) | async-done | bytes 1638416 | tf_op jit(solution)/shard_map/reduce_scatter | solution.py:574
  1125.7 62.0 %reduce-scatter.30.cloned.1.call-done = bf16[256,1600]{0,1:T(8,128)(2,1)} async-done(((bf16[1024,1600]{0,1:T(8,128)(2,1)}), bf16[256,1600]{0,1:T(8,128)(2,1)}) %reduce-scatter.30.cloned.1.call-update) | async-done | bytes 819216 | tf_op jit(solution)/shard_map/reduce_scatter | solution.py:523
  1187.7 6.3 multiply_reduce_fusion.103
  1196.1 65.6 %all-gather.33.cloned.1.call-done = bf16[1024,1600]{0,1:T(8,128)(2,1)} async-done(((bf16[256,1600]{0,1:T(8,128)(2,1)}), bf16[1024,1600]{0,1:T(8,128)(2,1)}) %all-gather.33.cloned.1.call-update) | async-done | bytes 3276816 | tf_op jit(solution)/shard_map/all_gather | solution.py:587
  1261.7 12.2 multiply_reduce_fusion.96
  1273.9 5.1 copy.228
  1286.1 429.2 %while.41 = (s32[]{:T(128)}, f32[4,16,800]{2,1,0:T(8,128)S(1)}, f32[16,800]{1,0:T(8,128)S(1)}, f32[16,4,16,800]{3,1,2,0:T(4,128)}, f32[16,4,16,800]{3,1,2,0:T(4,...) while((s32[]{:T(128)}, f32[4,16,800]{2,1,0:T(8,128)S(1)}, ...), condition=%wide.region_116.117_spmd.clone, body=%wide.region_35.116_spmd.clone.sunk | while | flops 21258756 | bytes 17864676 | solution.py:348
  1732.2 28.6 %all-reduce.39 = bf16[1024,132]{0,1:T(8,128)(2,1)} all-reduce(f32[1024,132]{0,1:T(8,128)S(1)} %pad_maximum_fusion.5), channel_id=1, replica_groups=mesh['dp'=8,'tensor'=4] {'tensor'}, use_global_device_ids=true, to_apply=%region_117.118 | all-reduce | flops 135168 | bytes 811008 | tf_op jit(solution)/shard_map/psum | solution.py:600
  1764.9 5.1 copy.234
  1770.0 10.9 fusion.178
  1791.6 5.0 add_convert_fusion
  1802.7 5.5 fusion.64
  1814.8 5.6 fusion.186
  1820.6 7.1 fusion.189
  1841.9 5.2 fusion.110
  1847.2 5.2 convolution_bitcast_fusion.2
  1860.3 21.3 copy.246
  1892.5 9.5 copy.245
  1906.1 4.8 convolution_add_fusion.5
  1914.1 147.8 %all-reduce.40 = (bf16[2,1600,320]{2,0,1:T(2,128)(2,1)S(1)}, bf16[4,1600]{1,0:T(4,128)(2,1)S(1)}, f32[4,1,800]{2,1,0:T(1,128)S(1)}, f32[1,800]{1,0:T(1,128)S(1)}...) all-reduce(f32[2,1600,320]{2,0,1:T(2,128)} %copy.245, ...), channel_id=7, replica_groups=mesh['dp'=8,'tensor'=4] {'dp'}, use_global_device_ids=true, to_apply=%region_125.126.clone | all-reduce | flops 1048800 | bytes 6329600
  2065.1 17.9 reduce-scatter.42.cloned.1.call-done
  2085.3 9.9 fusion.191
  2096.6 7.5 fusion.190
  2104.3 8.4 convolution_bitcast_fusion
  2112.8 5.4 convolution_bitcast_fusion.1
  2118.2 6.5 pad_maximum_fusion
  2126.5 170.2 %all-reduce.36.cloned.1.call-done = (f32[2,1600,800]{2,0,1:T(2,128)}, f32[1,800,132]{1,2,0:T(8,128)}, f32[100,1,800]{0,1,2:T(1,128)}) async-done(((f32[2,1600,800]{2,0,1:T(2,128)}, f32[1,800,132]{1,2,0:T(8,128)}, f32[100,1,800]{0,1,2:T(1,128)}), (f32[2,1600,800]{2,0,1:T(2,128)}, f32[1,800,132]{1,2,0:T(8,128)}, f32[100,1,800]{0,1,2:T(1,128)})) %all-reduce.36.cloned.1.call-update) | async-done | bytes 10982416
  2303.2 39.4 %all-reduce.26 = (bf16[16,1600]{0,1:T(8,128)(2,1)S(1)}, bf16[4,200]{1,0:T(4,128)(2,1)S(1)}) all-reduce(bf16[16,1600]{0,1:T(8,128)(2,1)S(1)} %copy.273, bf16[4,200]{1,0:T(4,128)(2,1)S(1)} %dynamic-slice_convert_fusion.1), channel_id=1, replica_groups=mesh['dp'=8,'tensor'=4] {'tensor'}, use_global_device_ids=true, to_apply=%region_131.132 | all-reduce | flops 26400 | bytes 105600 | tf_op jit(solution)/shard_map/psum | solution.py:689
  2350.2 34.4 %all-reduce.38.cloned.1.call-done = (bf16[2,200,320]{2,0,1:T(2,128)(2,1)}, bf16[200,1600]{1,0:T(8,128)(2,1)}, bf16[200,1600]{1,0:T(8,128)(2,1)}) async-done(((bf16[2,200,320]{2,0,1:T(2,128)(2,1)}, bf16[200,1600]{1,0:T(8,128)(2,1)}, bf16[200,1600]{1,0:T(8,128)(2,1)}), (bf16[2,200,320]{2,0,1:T(2,128)(2,1)}, bf16[200,1600]{1,0:T(8,128)(2,1)}, bf16[200,1600]{1,0:T(8,128)(2,1)})) %all-reduce.38.cloned.1.call-update) | async-done | bytes 1536016 | tf_op jit(solution)/shard_map/psum | solution.py:687
  2390.0 75.2 %reduce-scatter.46.cloned.1.call-done = f32[1376,200]{0,1:T(8,128)} async-done(((f32[1376,1600]{0,1:T(8,128)}), f32[1376,200]{0,1:T(8,128)}) %reduce-scatter.46.cloned.1.call-update) | async-done | bytes 1100816
  2465.2 64.7 %reduce-scatter.44.cloned.1.call-done = f32[800,200]{0,1:T(8,128)} async-done(((f32[800,1600]{0,1:T(8,128)}), f32[800,200]{0,1:T(8,128)}) %reduce-scatter.44.cloned.1.call-update) | async-done | bytes 640016
  2529.9 130.8 %reduce-scatter.36.cloned.1.call-done = f32[2,200,1376]{2,1,0:T(8,128)} async-done(((f32[2,1600,1376]{2,1,0:T(8,128)}), f32[2,200,1376]{2,1,0:T(8,128)}) %reduce-scatter.36.cloned.1.call-update) | async-done | bytes 2201616 | tf_op jit(solution)/shard_map/reduce_scatter | solution.py:682
  (2958 shorter events, 1013.1 us)
Async XLA Ops:
  7.2 27.8 %copy-start.137 = (u32[32]{0:T(128)S(1)}, u32[32]{0:T(128)}, u32[]{:S(2)}) copy-start(u32[32]{0:T(128)} %constant.188) | copy-start | bytes 388
  7.2 16.1 copy-start.138
  7.2 26.2 copy-start.110
  7.2 29.1 %copy-start.143 = (bf16[1,100]{1,0:T(2,128)(2,1)S(1)}, bf16[1,100]{1,0:T(2,128)(2,1)}, u32[]{:S(2)}) copy-start(bf16[1,100]{1,0:T(2,128)(2,1)} %param.35) | copy-start | bytes 604
  7.2 29.3 %copy-start.144 = (bf16[1,100]{1,0:T(2,128)(2,1)S(1)}, bf16[1,100]{1,0:T(2,128)(2,1)}, u32[]{:S(2)}) copy-start(bf16[1,100]{1,0:T(2,128)(2,1)} %param.36) | copy-start | bytes 604
  7.2 29.5 %copy-start.145 = (bf16[1,100]{1,0:T(2,128)(2,1)S(1)}, bf16[1,100]{1,0:T(2,128)(2,1)}, u32[]{:S(2)}) copy-start(bf16[1,100]{1,0:T(2,128)(2,1)} %param.38) | copy-start | bytes 604
  7.3 44.0 %copy-start.103 = (bf16[1,100,132]{1,2,0:T(8,128)(2,1)S(1)}, bf16[1,100,132]{1,2,0:T(8,128)(2,1)}, u32[]{:S(2)}) copy-start(bf16[1,100,132]{1,2,0:T(8,128)(2,1)} %param.32) | copy-start | bytes 79204
  7.3 81.2 %all-gather.19.cloned.1.call-start = ((), (), s32[]{:S(2)}) async-start(), calls=%async_computation.13 | async-start | bytes 4096000 | tf_op jit(solution)/shard_map/all_gather | solution.py:485
  18.7 638.1 %copy-start.59 = (f32[1600]{0:T(1024)}, f32[1600]{0:T(1024)S(1)}, u32[]{:S(2)}) copy-start(f32[1600]{0:T(1024)S(1)} %get-tuple-element.824) | copy-start | bytes 19204
  22.5 109.1 %all-gather.21.cloned.1.call-start = ((), (), s32[]{:S(2)}) async-start(), calls=%async_computation.14 | async-start | bytes 6451200 | tf_op jit(solution)/shard_map/all_gather | solution.py:427
  23.2 160.1 %all-reduce.34.cloned.1.call-start = ((), (), s32[]{:S(2)}) async-start(), calls=%async_computation.15 | async-start | bytes 1114112 | tf_op jit(solution)/shard_map/psum | solution.py:494
  63.8 74.1 %copy-start.126 = (pred[1024]{0:T(1024)(128)(4,1)}, pred[1024]{0:T(1024)(128)(4,1)S(1)}, u32[]{:S(2)}) copy-start(pred[1024]{0:T(1024)(128)(4,1)S(1)} %get-tuple-element.1136) | copy-start | bytes 3076
  63.8 74.1 %copy-start.128 = (pred[1024]{0:T(1024)(128)(4,1)}, pred[1024]{0:T(1024)(128)(4,1)S(1)}, u32[]{:S(2)}) copy-start(pred[1024]{0:T(1024)(128)(4,1)S(1)} %get-tuple-element.1137) | copy-start | bytes 3076
  63.8 74.1 %copy-start.130 = (pred[1024]{0:T(1024)(128)(4,1)}, pred[1024]{0:T(1024)(128)(4,1)S(1)}, u32[]{:S(2)}) copy-start(pred[1024]{0:T(1024)(128)(4,1)S(1)} %get-tuple-element.1138) | copy-start | bytes 3076
  76.2 61.7 %copy-start.95 = (f32[800]{0:T(1024)}, f32[800]{0:T(1024)S(1)}, u32[]{:S(2)}) copy-start(f32[800]{0:T(1024)S(1)} %get-tuple-element.817) | copy-start | bytes 9604
  76.2 61.7 %copy-start.97 = (f32[800]{0:T(1024)}, f32[800]{0:T(1024)S(1)}, u32[]{:S(2)}) copy-start(f32[800]{0:T(1024)S(1)} %get-tuple-element.818) | copy-start | bytes 9604
  76.3 61.7 %copy-start.99 = (f32[800]{0:T(1024)}, f32[800]{0:T(1024)S(1)}, u32[]{:S(2)}) copy-start(f32[800]{0:T(1024)S(1)} %get-tuple-element.819) | copy-start | bytes 9604
  76.3 61.7 %copy-start.101 = (f32[800]{0:T(1024)}, f32[800]{0:T(1024)S(1)}, u32[]{:S(2)}) copy-start(f32[800]{0:T(1024)S(1)} %get-tuple-element.820) | copy-start | bytes 9604
  142.6 1119.1 %copy-start.6 = (f32[1024,800]{0,1:T(8,128)}, f32[1024,800]{0,1:T(8,128)S(1)}, u32[]{:S(2)}) copy-start(f32[1024,800]{0,1:T(8,128)S(1)} %get-tuple-element.929) | copy-start | bytes 9830404
  142.6 17.2 copy-start.135
  144.3 478.3 %all-gather.23.cloned.1.call-start = ((), (), s32[]{:S(2)}) async-start(), calls=%async_computation.16 | async-start | bytes 3225600 | tf_op jit(solution)/shard_map/all_gather | solution.py:435
  144.9 503.2 %all-gather.13.cloned.1.call-start = ((), (), s32[]{:S(2)}) async-start(), calls=%async_computation.10 | async-start | bytes 2764800 | tf_op jit(solution)/shard_map/all_gather | solution.py:423
  145.5 514.1 %all-gather.15.cloned.1.call-start = ((), (), s32[]{:S(2)}) async-start(), calls=%async_computation.11 | async-start | bytes 5990400 | tf_op jit(solution)/shard_map/all_gather | solution.py:422
  146.1 526.5 %all-gather.17.cloned.1.call-start = ((), (), s32[]{:S(2)}) async-start(), calls=%async_computation.12 | async-start | bytes 5990400 | tf_op jit(solution)/shard_map/all_gather | solution.py:424
  146.8 599.7 %reduce-scatter.28.cloned.1.call-start = ((), (), s32[]{:S(2)}) async-start(), calls=%async_computation.17 | async-start | bytes 8192000 | tf_op jit(solution)/shard_map/reduce_scatter | solution.py:507
  147.7 35.7 %copy-start.113 = (f32[800]{0:T(1024)}, f32[800]{0:T(1024)S(1)}, u32[]{:S(2)}) copy-start(f32[800]{0:T(1024)S(1)} %add.1067) | copy-start | bytes 9604
  159.8 23.6 copy-start.49
  631.2 174.7 %all-gather.27.cloned.1.call-start = ((), (), s32[]{:S(2)}) async-start(), calls=%async_computation.19 | async-start | bytes 10137600 | tf_op jit(solution)/shard_map/all_gather | solution.py:436
  631.9 241.5 %all-gather.25.cloned.1.call-start = ((), (), s32[]{:S(2)}) async-start(), calls=%async_computation.18 | async-start | bytes 4096000 | tf_op jit(solution)/shard_map/all_gather | solution.py:518
  647.3 22.4 copy-start.41
  648.1 16.6 copy-start.47
  672.6 75.6 %copy-start.91 = (f32[1600]{0:T(1024)S(1)}, f32[1600]{0:T(1024)}, u32[]{:S(2)}) copy-start(f32[1600]{0:T(1024)} %get-tuple-element.822) | copy-start | bytes 19204
  672.6 75.6 %copy-start.92 = (f32[1600]{0:T(1024)S(1)}, f32[1600]{0:T(1024)}, u32[]{:S(2)}) copy-start(f32[1600]{0:T(1024)} %get-tuple-element.823) | copy-start | bytes 19204
  753.3 185.5 %all-gather.31.cloned.1.call-start = ((), (), s32[]{:S(2)}) async-start(), calls=%async_computation.22 | async-start | bytes 4096000 | tf_op jit(solution)/shard_map/all_gather | solution.py:486
  754.0 222.6 %all-gather.29.cloned.1.call-start = ((), (), s32[]{:S(2)}) async-start(), calls=%async_computation.20 | async-start | bytes 5068800 | tf_op jit(solution)/shard_map/all_gather | solution.py:437
  754.6 368.0 %reduce-scatter.32.cloned.1.call-start = ((), (), s32[]{:S(2)}) async-start(), calls=%async_computation.23 | async-start | bytes 8192000 | tf_op jit(solution)/shard_map/reduce_scatter | solution.py:574
  976.6 23.3 slice-start.2
  976.6 23.3 slice-start.3
  1007.4 180.3 %reduce-scatter.30.cloned.1.call-start = ((), (), s32[]{:S(2)}) async-start(), calls=%async_computation.21 | async-start | bytes 4096000 | tf_op jit(solution)/shard_map/reduce_scatter | solution.py:523
  1016.5 245.2 %all-gather.33.cloned.1.call-start = ((), (), s32[]{:S(2)}) async-start(), calls=%async_computation.24 | async-start | bytes 4096000 | tf_op jit(solution)/shard_map/all_gather | solution.py:587
  1194.1 67.6 %copy-start.112 = (f32[800]{0:T(1024)S(1)}, f32[800]{0:T(1024)}, u32[]{:S(2)}) copy-start(f32[800]{0:T(1024)} %mul.6158) | copy-start | bytes 9604
  1196.0 710.1 %reduce-scatter.34.cloned.1.call-start = ((), (), s32[]{:S(2)}) async-start(), calls=%async_computation.25 | async-start | bytes 4096000 | tf_op jit(solution)/shard_map/reduce_scatter | solution.py:618
  1314.7 12.7 copy-start.8
  1368.3 12.7 copy-start.8
  1395.2 12.7 copy-start.8
  1422.0 12.7 copy-start.8
  1448.9 12.7 copy-start.8
  1475.7 12.7 copy-start.8
  1502.5 12.7 copy-start.8
  1529.3 12.7 copy-start.8
  1609.8 12.7 copy-start.8
  1663.4 12.7 copy-start.8
  1796.6 266.2 %reduce-scatter.40.cloned.1.call-start = ((), (), s32[]{:S(2)}) async-start(), calls=%async_computation.28 | async-start | bytes 11980800
  1820.5 262.5 %reduce-scatter.42.cloned.1.call-start = ((), (), s32[]{:S(2)}) async-start(), calls=%async_computation.29 | async-start | bytes 11980800
  1827.7 297.7 %reduce-scatter.38.cloned.1.call-start = ((), (), s32[]{:S(2)}) async-start(), calls=%async_computation.27 | async-start | bytes 958464
  1847.1 449.7 %all-reduce.36.cloned.1.call-start = ((), (), s32[]{:S(2)}) async-start(), calls=%async_computation.32 | async-start | bytes 24731648
  1860.2 21.3 copy-start.7
  1885.6 499.1 %all-reduce.38.cloned.1.call-start = ((), (), s32[]{:S(2)}) async-start(), calls=%async_computation.33 | async-start | bytes 3276800 | tf_op jit(solution)/shard_map/psum | solution.py:687
  1892.5 12.8 copy-start.36
  1892.5 13.0 copy-start.136
  2085.2 379.9 %reduce-scatter.46.cloned.1.call-start = ((), (), s32[]{:S(2)}) async-start(), calls=%async_computation.31 | async-start | bytes 10137600
  2095.2 434.7 %reduce-scatter.44.cloned.1.call-start = ((), (), s32[]{:S(2)}) async-start(), calls=%async_computation.30 | async-start | bytes 6451200
  2104.1 556.6 %reduce-scatter.36.cloned.1.call-start = ((), (), s32[]{:S(2)}) async-start(), calls=%async_computation.26 | async-start | bytes 20275200 | tf_op jit(solution)/shard_map/reduce_scatter | solution.py:682
  2296.8 50.4 %copy-start.27 = (f32[256,1600]{0,1:T(8,128)S(1)}, f32[256,1600]{0,1:T(8,128)}, u32[]{:S(2)}) copy-start(f32[256,1600]{0,1:T(8,128)} %copy-done.26) | copy-start | bytes 4915204
  (433 other events, 2988.3 us)
Sparse Core Ops, SparseCore 0:
  22.6 65.7 all-gather.18
  90.4 41.2 all-gather.20
  144.5 38.8 all-reduce.33
  185.1 30.8 all-gather.22
  217.8 29.2 all-gather.12
  248.8 41.3 all-gather.14
  292.1 41.3 all-gather.16
  631.3 115.2 reduce-scatter.27
  748.5 57.4 all-gather.26
  807.9 65.5 all-gather.24
  875.0 63.7 all-gather.30
  940.5 36.0 all-gather.28
  1007.5 115.0 reduce-scatter.31
  1124.8 62.9 reduce-scatter.29
  1196.1 65.5 all-gather.32
  1796.7 61.4 reduce-scatter.33
  1861.7 103.0 reduce-scatter.39
  1968.2 114.6 reduce-scatter.41
  2086.7 35.2 reduce-scatter.37
  2126.4 170.2 all-reduce.35
  2299.9 84.7 all-reduce.37
  2388.8 76.3 reduce-scatter.45
  2469.2 60.5 reduce-scatter.43
  2533.9 126.6 reduce-scatter.35
where the time goes:
time: 2720 us; the launch traced here: 2670 us
  waiting for transfers between devices  1060 us (39%)
  other arithmetic  540 us (20%)
  local copies, waits for them, and re-layouts  509 us (19%)
  blocking collectives  290 us (11%)
  matrix products  236 us (9%)
    unnamed x30, waiting for transfers between devices  333 us
    unnamed x2, blocking collectives  162 us
    while x240, other arithmetic  157 us
    squeeze x160, local copies, waits for them, and re-layouts, selective_scan(): finished, (starts, outputs) = lax.scan(advance, initial, pieces)  133 us
    reduce_scatter x1, waiting for transfers between devices, per_device(): lax.psum_scatter(g_gateup, 'dp', scatter_dimension=1, tiled=True)  131 us
    reduce_sum x96, other arithmetic, advance(): outputs.append(jnp.sum(output_block[:, offset, :, None] * running, axis=1))  113 us
    reduce_scatter x1, waiting for transfers between devices, per_device(): lax.psum_scatter(contract_cols(g_gate_low, gateup_weight[0]) + contract_c...  106 us
    reduce_sum x128, other arithmetic, retreat(): jnp.sum(through * decay_rate[None], axis=1)  84 us
  transfers between devices with their start and end apart: 24, of which 17 were waited for; matrix products, arithmetic and copies ran while one was open for 27% of the time, Pallas kernels for 0%

commit v1 on v0

v1 whole, which is shorter than its diff:
```python
import functools
import math

import jax
import jax.numpy as jnp
from jax import lax
from jax.experimental import pallas as pl
from jax.experimental.pallas import tpu as pltpu
from jax.sharding import PartitionSpec as P

HEADS = 25
KV_HEADS = 5
HEAD_DIM = 64
META = 128
STATE = 16
CONV = 4
DTR = 100
SEQ_LEN = 256

EPSILON = 1e-05
ROPE_BASE = 10000.0
NEG_FILL = -1e30


def plain_dot(former, latter):
    return jnp.dot(former, latter, preferred_element_type=jnp.float32)


def contract_rows(former, latter):
    return lax.dot_general(
        former, latter, (((0,), (0,)), ((), ())), preferred_element_type=jnp.float32
    )


def contract_cols(former, latter):
    return lax.dot_general(
        former, latter, (((1,), (1,)), ((), ())), preferred_element_type=jnp.float32
    )


def contract_rows_exact(former, latter):
    return lax.dot_general(
        former,
        latter,
        (((0,), (0,)), ((), ())),
        precision=lax.Precision.HIGHEST,
        preferred_element_type=jnp.float32,
    )


def contract_cols_exact(former, latter):
    return lax.dot_general(
        former,
        latter,
        (((1,), (1,)), ((), ())),
        precision=lax.Precision.HIGHEST,
        preferred_element_type=jnp.float32,
    )


def mix_sum(pattern, former, latter):
    return jnp.einsum(pattern, former, latter, preferred_element_type=jnp.float32)


def inverse_rms(operand):
    return lax.rsqrt(jnp.mean(operand * operand, axis=-1, keepdims=True) + EPSILON)


def norm_backward(cotangent, normed, scaling):
    return scaling * (cotangent - normed * jnp.mean(cotangent * normed, axis=-1, keepdims=True))


def swish_slope(operand):
    sigmoid = jax.nn.sigmoid(operand)
    return sigmoid * (1.0 + operand * (1.0 - sigmoid))


def rotary_tables(row_count):
    places = (jnp.arange(row_count, dtype=jnp.int32) % SEQ_LEN).astype(jnp.float32)
    powers = jnp.arange(HEAD_DIM // 2, dtype=jnp.int32).astype(jnp.float32) * (2.0 / HEAD_DIM)
    angles = places[:, None] * jnp.power(ROPE_BASE, -powers)[None, :]
    return (jnp.cos(angles)[:, None, :], jnp.sin(angles)[:, None, :])


def rotate_pairs(operand, cosine_table, sine_table):
    half_dim = operand.shape[-1] // 2
    leading = operand[..., :half_dim]
    trailing = operand[..., half_dim:]
    return jnp.concatenate(
        [
            leading * cosine_table - trailing * sine_table,
            leading * sine_table + trailing * cosine_table,
        ],
        axis=-1,
    )


def segment_mask(segments):
    per_sequence = segments.reshape(-1, SEQ_LEN)
    places = jnp.arange(SEQ_LEN, dtype=jnp.int32)
    return (per_sequence[:, :, None] == per_sequence[:, None, :]) & (
        places[:, None] >= places[None, :]
    )


def attention_inputs(
    normed_low, meta_low, query_weight, key_weight, value_weight, cosine_table, sine_table
):
    row_count = normed_low.shape[0]
    seq_count = row_count // SEQ_LEN
    groups = HEADS // KV_HEADS
    queries = rotate_pairs(
        plain_dot(normed_low, query_weight).reshape(row_count, HEADS, HEAD_DIM),
        cosine_table,
        sine_table,
    )
    keys_rot = rotate_pairs(
        plain_dot(normed_low, key_weight).reshape(row_count, KV_HEADS, HEAD_DIM),
        cosine_table,
        sine_table,
    )
    query_low = queries.astype(jnp.bfloat16).reshape(seq_count, SEQ_LEN, KV_HEADS, groups, HEAD_DIM)
    key_low = keys_rot.astype(jnp.bfloat16).reshape(seq_count, SEQ_LEN, KV_HEADS, HEAD_DIM)
    value_low = (
        plain_dot(normed_low, value_weight)
        .astype(jnp.bfloat16)
        .reshape(seq_count, SEQ_LEN, KV_HEADS, HEAD_DIM)
    )
    meta_keys = (
        plain_dot(meta_low, key_weight).astype(jnp.bfloat16).reshape(META, KV_HEADS, HEAD_DIM)
    )
    meta_values = (
        plain_dot(meta_low, value_weight).astype(jnp.bfloat16).reshape(META, KV_HEADS, HEAD_DIM)
    )
    return (query_low, key_low, value_low, meta_keys, meta_values)


def attention_scores(query_low, key_low, meta_keys, allowed):
    score_scale = 1.0 / math.sqrt(HEAD_DIM)
    meta_scores = mix_sum("slkgd,nkd->skgln", query_low, meta_keys) * score_scale
    own_scores = mix_sum("slkgd,smkd->skglm", query_low, key_low) * score_scale
    own_scores = jnp.where(allowed[:, None, None], own_scores, NEG_FILL)
    return (meta_scores, own_scores)


def attention_forward(query_low, key_low, value_low, meta_keys, meta_values, allowed):
    meta_scores, own_scores = attention_scores(query_low, key_low, meta_keys, allowed)
    highest = jnp.maximum(jnp.max(meta_scores, axis=-1), jnp.max(own_scores, axis=-1))
    totals = jnp.sum(jnp.exp(meta_scores - highest[..., None]), axis=-1) + jnp.sum(
        jnp.exp(own_scores - highest[..., None]), axis=-1
    )
    log_total = highest + jnp.log(totals)
    meta_probs = jnp.exp(meta_scores - log_total[..., None]).astype(jnp.bfloat16)
    own_probs = jnp.exp(own_scores - log_total[..., None]).astype(jnp.bfloat16)
    mixed_heads = mix_sum("skgln,nkd->slkgd", meta_probs, meta_values) + mix_sum(
        "skglm,smkd->slkgd", own_probs, value_low
    )
    row_count = query_low.shape[0] * SEQ_LEN
    return (mixed_heads.reshape(row_count, HEADS * HEAD_DIM).astype(jnp.bfloat16), log_total)


def attention_backward(
    cotangent_low,
    query_low,
    key_low,
    value_low,
    meta_keys,
    meta_values,
    allowed,
    log_total,
    cosine_table,
    sine_table,
):
    row_count = query_low.shape[0] * SEQ_LEN
    score_scale = 1.0 / math.sqrt(HEAD_DIM)
    cotangent_low = cotangent_low.reshape(query_low.shape)
    meta_scores, own_scores = attention_scores(query_low, key_low, meta_keys, allowed)
    meta_probs = jnp.exp(meta_scores - log_total[..., None])
    own_probs = jnp.exp(own_scores - log_total[..., None])
    meta_dprob = mix_sum("slkgd,nkd->skgln", cotangent_low, meta_values)
    own_dprob = mix_sum("slkgd,smkd->skglm", cotangent_low, value_low)
    row_delta = jnp.sum(meta_probs * meta_dprob, axis=-1) + jnp.sum(own_probs * own_dprob, axis=-1)
    meta_dscore = (meta_probs * (meta_dprob - row_delta[..., None]) * score_scale).astype(
        jnp.bfloat16
    )
    own_dscore = (own_probs * (own_dprob - row_delta[..., None]) * score_scale).astype(jnp.bfloat16)
    back_query = mix_sum("skgln,nkd->slkgd", meta_dscore, meta_keys) + mix_sum(
        "skglm,smkd->slkgd", own_dscore, key_low
    )
    back_query = (
        rotate_pairs(back_query.reshape(row_count, HEADS, HEAD_DIM), cosine_table, -sine_table)
        .reshape(row_count, -1)
        .astype(jnp.bfloat16)
    )
    back_key = mix_sum("skglm,slkgd->smkd", own_dscore, query_low)
    back_key = (
        rotate_pairs(back_key.reshape(row_count, KV_HEADS, HEAD_DIM), cosine_table, -sine_table)
        .reshape(row_count, -1)
        .astype(jnp.bfloat16)
    )
    back_value = (
        mix_sum("skglm,slkgd->smkd", own_probs.astype(jnp.bfloat16), cotangent_low)
        .reshape(row_count, -1)
        .astype(jnp.bfloat16)
    )
    back_meta_key = mix_sum("skgln,slkgd->nkd", meta_dscore, query_low).reshape(META, -1)
    back_meta_value = mix_sum(
        "skgln,slkgd->nkd", meta_probs.astype(jnp.bfloat16), cotangent_low
    ).reshape(META, -1)
    return (back_query, back_key, back_value, back_meta_key, back_meta_value)


LOG2E = 1.4426950408889634
FAR = 1e6
BLK = 16

def _softplus(v):
    return jnp.maximum(v, 0.0) + jnp.log1p(jnp.exp(-jnp.abs(v)))

def _sigmoid(v):
    return 1.0 / (1.0 + jnp.exp(-v))

def scan_fwd_kernel(feed_ref, sraw_ref, gate_ref, keep_ref, b_ref, c_ref, rate_ref, skip_ref,
                    low_ref, comb_ref, starts_ref, h_scr, y_scr):
    blocks = feed_ref.shape[0] // BLK
    rate2 = rate_ref[...] * LOG2E
    h_scr[...] = jnp.zeros_like(h_scr)

    def body(n, carry):
        rows = pl.ds(pl.multiple_of(n * BLK, BLK), BLK)
        feed = feed_ref[rows, :]
        step = _softplus(sraw_ref[rows, :])
        reach = jnp.where(keep_ref[rows, :] > 0.0, step, FAR)
        drive = step * feed
        bm = b_ref[0, n]
        cm = c_ref[0, n]
        h = h_scr[...]
        starts_ref[0, n] = h
        for j in range(BLK):
            a = jnp.exp2(reach[j:j + 1, :] * rate2)
            h = a * h + drive[j:j + 1, :] * bm[:, j:j + 1]
            y_scr[j:j + 1, :] = jnp.sum(h * cm[:, j:j + 1], axis=0, keepdims=True)
        h_scr[...] = h
        combined = y_scr[...] + skip_ref[...] * feed
        comb_ref[rows, :] = combined
        gate = gate_ref[rows, :]
        low_ref[rows, :] = (combined * (gate * _sigmoid(gate))).astype(low_ref.dtype)
        return carry

    lax.fori_loop(0, blocks, body, 0)

def scan_bwd_kernel(gg_ref, gate_ref, comb_ref, feed_ref, sraw_ref, keep_ref, b_ref, c_ref, starts_ref, rate_ref, skip_ref,
                    ggate_ref, gfeed_ref, gstep_ref, db_ref, dc_ref, drate_ref, dskip_ref, dbias_ref,
                    dh_scr, h_scr, a_scr, du_scr, ds_scr):
    blocks = feed_ref.shape[0] // BLK
    rate = rate_ref[...]
    rate2 = rate * LOG2E
    lane = lax.broadcasted_iota(jnp.int32, (b_ref.shape[2], BLK), 1)

    @pl.when(pl.program_id(0) == 0)
    def _():
        drate_ref[...] = jnp.zeros_like(drate_ref)
        dskip_ref[...] = jnp.zeros_like(dskip_ref)
        dbias_ref[...] = jnp.zeros_like(dbias_ref)

    dh_scr[...] = jnp.zeros_like(dh_scr)

    def body(i, carry):
        n = blocks - 1 - i
        rows = pl.ds(pl.multiple_of(n * BLK, BLK), BLK)
        feed = feed_ref[rows, :]
        sraw = sraw_ref[rows, :]
        step = _softplus(sraw)
        reach = jnp.where(keep_ref[rows, :] > 0.0, step, FAR)
        drive = step * feed
        gate = gate_ref[rows, :]
        sig = _sigmoid(gate)
        gg = gg_ref[rows, :]
        gcomb = gg * (gate * sig)
        ggate_ref[rows, :] = (gg * comb_ref[rows, :] * (sig * (1.0 + gate * (1.0 - sig)))).astype(ggate_ref.dtype)
        dskip_ref[...] += jnp.sum(gcomb * feed, axis=0, keepdims=True)
        bm = b_ref[0, n]
        cm = c_ref[0, n]
        h = starts_ref[0, n]
        for j in range(BLK):
            h_scr[j] = h
            a = jnp.exp2(reach[j:j + 1, :] * rate2)
            a_scr[j] = a
            h = a * h + drive[j:j + 1, :] * bm[:, j:j + 1]
        dh = dh_scr[...]
        drate = drate_ref[...]
        dbm = jnp.zeros(bm.shape, jnp.float32)
        dcm = jnp.zeros(bm.shape, jnp.float32)
        for j in reversed(range(BLK)):
            gy = gcomb[j:j + 1, :]
            dh = dh + cm[:, j:j + 1] * gy
            dcm = jnp.where(lane == j, jnp.sum(gy * h, axis=1, keepdims=True), dcm)
            dbm = jnp.where(lane == j, jnp.sum(dh * drive[j:j + 1, :], axis=1, keepdims=True), dbm)
            du_scr[j:j + 1, :] = jnp.sum(dh * bm[:, j:j + 1], axis=0, keepdims=True)
            dh = dh * a_scr[j]
            h = h_scr[j]
            thru = dh * h
            ds_scr[j:j + 1, :] = jnp.sum(thru * rate, axis=0, keepdims=True)
            drate = drate + thru * step[j:j + 1, :]
        dh_scr[...] = dh
        drate_ref[...] = drate
        db_ref[0, n] = dbm
        dc_ref[0, n] = dcm
        du = du_scr[...]
        gfeed_ref[rows, :] = gcomb * skip_ref[...] + du * step
        gsraw = (du * feed + ds_scr[...]) * _sigmoid(sraw)
        dbias_ref[...] += jnp.sum(gsraw, axis=0, keepdims=True)
        gstep_ref[rows, :] = gsraw.astype(gstep_ref.dtype)
        return carry

    lax.fori_loop(0, blocks, body, 0)

def to_cols(mat, seq_len):
    rows, states = mat.shape
    return jnp.swapaxes(mat.reshape(rows // seq_len, seq_len // BLK, BLK, states), 2, 3)

def from_cols(cols):
    return jnp.swapaxes(cols, 2, 3).reshape(-1, cols.shape[2])

def scan_fwd(feed, sraw, gate, keep, bcols, ccols, rate, skip, seq_len):
    rows, width = feed.shape
    seqs = rows // seq_len
    states = rate.shape[0]
    nb = seq_len // BLK
    wide = pl.BlockSpec((seq_len, width), lambda s: (s, 0))
    cols = pl.BlockSpec((1, nb, states, BLK), lambda s: (s, 0, 0, 0))
    f32 = jnp.float32
    return pl.pallas_call(
        scan_fwd_kernel,
        grid=(seqs,),
        in_specs=[wide, wide, wide, pl.BlockSpec((seq_len, 1), lambda s: (s, 0)), cols, cols,
                  pl.BlockSpec((states, width), lambda s: (0, 0)), pl.BlockSpec((1, width), lambda s: (0, 0))],
        out_specs=[wide, wide, pl.BlockSpec((1, nb, states, width), lambda s: (s, 0, 0, 0))],
        out_shape=[jax.ShapeDtypeStruct((rows, width), jnp.bfloat16), jax.ShapeDtypeStruct((rows, width), f32),
                   jax.ShapeDtypeStruct((seqs, nb, states, width), f32)],
        scratch_shapes=[pltpu.VMEM((states, width), f32), pltpu.VMEM((BLK, width), f32)],
        name="scan_forward",
    )(feed, sraw, gate, keep, bcols, ccols, rate, skip)

def scan_bwd(gg, gate, comb, feed, sraw, keep, bcols, ccols, starts, rate, skip, seq_len):
    rows, width = feed.shape
    seqs = rows // seq_len
    states = rate.shape[0]
    nb = seq_len // BLK
    wide = pl.BlockSpec((seq_len, width), lambda s: (s, 0))
    cols = pl.BlockSpec((1, nb, states, BLK), lambda s: (s, 0, 0, 0))
    par = pl.BlockSpec((states, width), lambda s: (0, 0))
    row = pl.BlockSpec((1, width), lambda s: (0, 0))
    f32 = jnp.float32
    return pl.pallas_call(
        scan_bwd_kernel,
        grid=(seqs,),
        in_specs=[wide, wide, wide, wide, wide, pl.BlockSpec((seq_len, 1), lambda s: (s, 0)), cols, cols,
                  pl.BlockSpec((1, nb, states, width), lambda s: (s, 0, 0, 0)), par, row],
        out_specs=[wide, wide, wide, cols, cols, par, row, row],
        out_shape=[jax.ShapeDtypeStruct((rows, width), jnp.bfloat16), jax.ShapeDtypeStruct((rows, width), f32),
                   jax.ShapeDtypeStruct((rows, width), jnp.bfloat16),
                   jax.ShapeDtypeStruct((seqs, nb, states, BLK), f32), jax.ShapeDtypeStruct((seqs, nb, states, BLK), f32),
                   jax.ShapeDtypeStruct((states, width), f32), jax.ShapeDtypeStruct((1, width), f32), jax.ShapeDtypeStruct((1, width), f32)],
        scratch_shapes=[pltpu.VMEM((states, width), f32), pltpu.VMEM((BLK, states, width), f32), pltpu.VMEM((BLK, states, width), f32),
                        pltpu.VMEM((BLK, width), f32), pltpu.VMEM((BLK, width), f32)],
        name="scan_backward",
    )(gg, gate, comb, feed, sraw, keep, bcols, ccols, starts, rate, skip)


def lag_masks(segments):
    places = jnp.arange(segments.shape[0], dtype=jnp.int32) % SEQ_LEN
    masks = []
    for lag in range(1, CONV):
        before = jnp.concatenate([segments[:lag], segments[:-lag]])
        masks.append(((places >= lag) & (segments == before))[:, None])
    return masks


def causal_conv(mamba_in, conv_taps, conv_shift, masks):
    totals = conv_shift[None] + conv_taps[0][None] * mamba_in
    for lag in range(1, CONV):
        lagged = jnp.concatenate([jnp.zeros((lag, mamba_in.shape[1]), mamba_in.dtype), mamba_in[:-lag]])
        totals = totals + jnp.where(masks[lag - 1], conv_taps[lag][None] * lagged, 0.0)
    return totals


def causal_conv_grad(cotangent, mamba_in, conv_taps, masks):
    back_input = conv_taps[0][None] * cotangent
    tap_grads = [jnp.sum(cotangent * mamba_in, axis=0)]
    for lag in range(1, CONV):
        masked = jnp.where(masks[lag - 1], cotangent, 0.0)
        padding = jnp.zeros((lag, mamba_in.shape[1]), mamba_in.dtype)
        lagged = jnp.concatenate([padding, mamba_in[:-lag]])
        tap_grads.append(jnp.sum(masked * lagged, axis=0))
        back_input = back_input + conv_taps[lag][None] * jnp.concatenate([masked[lag:], padding])
    return back_input, jnp.stack(tap_grads), jnp.sum(cotangent, axis=0)


def pack(pieces):
    return jnp.concatenate([piece.reshape(-1) for piece in pieces])


def gather_small(pieces, dims):
    packed = lax.all_gather(pack(pieces), "dp", axis=0, tiled=False)
    wholes, start = [], 0
    for piece, dim in zip(pieces, dims):
        part = packed[:, start : start + piece.size].reshape((packed.shape[0],) + piece.shape)
        start += piece.size
        part = jnp.moveaxis(part, 0, dim)
        wholes.append(part.reshape(piece.shape[:dim] + (-1,) + piece.shape[dim + 1 :]))
    return wholes


def scatter_small(totals, dims, count):
    shares, shapes = [], []
    for total, dim in zip(totals, dims):
        shape = total.shape[:dim] + (total.shape[dim] // count,) + total.shape[dim + 1 :]
        split = total.reshape(total.shape[:dim] + (count, shape[dim]) + total.shape[dim + 1 :])
        shares.append(jnp.moveaxis(split, dim, 0).reshape(count, -1))
        shapes.append(shape)
    packed = jnp.concatenate(shares, axis=1).astype(jnp.bfloat16)
    own = lax.psum_scatter(packed, "dp", scatter_dimension=0, tiled=True).reshape(-1)
    pieces, start = [], 0
    for shape in shapes:
        size = math.prod(shape)
        pieces.append(own[start : start + size].reshape(shape))
        start += size
    return pieces


def gather_rows(shards):
    return [lax.all_gather(shard, "dp", axis=0, tiled=True) for shard in shards]


def scatter_rows(totals):
    return [lax.psum_scatter(total, "dp", scatter_dimension=0, tiled=True) for total in totals]


def low_rows(former, latter):
    return contract_rows(former, latter).astype(jnp.bfloat16)


def per_device(
    tokens,
    segment_ids,
    out_grad,
    w_query,
    w_keyval,
    w_output,
    meta_tokens,
    norm_gains,
    in_proj,
    x_proj,
    dt_proj,
    conv_weight,
    conv_bias,
    dt_bias,
    a_log,
    skip_gain,
    out_proj,
    gate_up,
    w_down,
):
    dp_count = lax.axis_size("dp")
    small_dims = (0, 1, 0, 1, 1, 0, 0, 1, 0)
    meta_rows, gain_rows, xproj_weight, dtproj_weight, conv_taps, conv_shift, dt_shift, decay_log, skip_weight = gather_small(
        (
            meta_tokens,
            norm_gains,
            x_proj[0],
            dt_proj[:, 0],
            conv_weight[:, 0],
            conv_bias[0],
            dt_bias[0],
            a_log[:, 0],
            skip_gain[0],
        ),
        small_dims,
    )
    gain_rows = gain_rows.astype(jnp.float32)
    conv_taps = conv_taps.astype(jnp.float32)
    conv_shift = conv_shift.astype(jnp.float32)
    dt_shift = dt_shift.astype(jnp.float32)
    decay_rate = -jnp.exp(decay_log.astype(jnp.float32))
    skip_weight = skip_weight.astype(jnp.float32)

    token_count = tokens.shape[0]
    member = lax.axis_index("tensor")
    own_segments = lax.dynamic_slice_in_dim(segment_ids, member * token_count, token_count)
    residual = tokens.astype(jnp.float32)
    scale_one = inverse_rms(residual)
    normed_one = residual * scale_one
    normed_low = (normed_one * gain_rows[0]).astype(jnp.bfloat16)
    normed_all = lax.all_gather(normed_low, "tensor", axis=0, tiled=True)
    in_first, in_second = gather_rows((in_proj[0], in_proj[1]))
    query_weight, key_weight, value_weight, output_weight = gather_rows((w_query, w_keyval[0], w_keyval[1], w_output))
    (out_turned,) = gather_rows((out_proj.T,))
    gate_weight, up_weight = gather_rows((gate_up[0], gate_up[1]))
    grad_all = lax.all_gather(out_grad, "tensor", axis=0, tiled=True)
    (down_turned,) = gather_rows((w_down.T,))

    meta_float = meta_rows.astype(jnp.float32)
    meta_scale = inverse_rms(meta_float)
    meta_normed = meta_float * meta_scale
    meta_low = (meta_normed * gain_rows[0]).astype(jnp.bfloat16)
    cosine_table, sine_table = rotary_tables(token_count)
    allowed = segment_mask(own_segments)

    masks = lag_masks(segment_ids)
    keep_state = masks[0].astype(jnp.float32)
    mamba_in = plain_dot(normed_all, in_first)
    gate_raw = plain_dot(normed_all, in_second)
    conv_raw = causal_conv(mamba_in, conv_taps, conv_shift, masks)
    feed_rows = jax.nn.silu(conv_raw)
    feed_low = feed_rows.astype(jnp.bfloat16)
    projected = lax.psum(plain_dot(feed_low, xproj_weight), "tensor")

    query_low, key_low, value_low, meta_keys, meta_values = attention_inputs(
        normed_low, meta_low, query_weight, key_weight, value_weight, cosine_table, sine_table
    )
    attended, log_total = attention_forward(query_low, key_low, value_low, meta_keys, meta_values, allowed)
    attn_out = plain_dot(attended, output_weight)

    rank_low = projected[:, :DTR].astype(jnp.bfloat16)
    step_raw = plain_dot(rank_low, dtproj_weight) + dt_shift
    input_cols = to_cols(projected[:, DTR : DTR + STATE], SEQ_LEN)
    output_cols = to_cols(projected[:, DTR + STATE :], SEQ_LEN)
    mamba_low, combined, starts = scan_fwd(
        feed_rows, step_raw, gate_raw, keep_state, input_cols, output_cols, decay_rate, skip_weight[None], SEQ_LEN
    )
    mamba_out = lax.psum_scatter(
        contract_cols(mamba_low, out_turned).astype(jnp.bfloat16), "tensor", scatter_dimension=0, tiled=True
    ).astype(jnp.float32)
    attn_scale = inverse_rms(attn_out)
    attn_normed = attn_out * attn_scale
    mamba_scale = inverse_rms(mamba_out)
    mamba_normed = mamba_out * mamba_scale
    mixed_rows = residual + 0.5 * (attn_normed * gain_rows[1] + mamba_normed * gain_rows[2])
    scale_two = inverse_rms(mixed_rows)
    normed_two = mixed_rows * scale_two
    ffn_low = (normed_two * gain_rows[3]).astype(jnp.bfloat16)
    ffn_all = lax.all_gather(ffn_low, "tensor", axis=0, tiled=True)
    gate_pre = plain_dot(ffn_all, gate_weight)
    up_pre = plain_dot(ffn_all, up_weight)
    gate_swish = jax.nn.silu(gate_pre)
    hidden_low = (gate_swish * up_pre).astype(jnp.bfloat16)
    g_hidden = plain_dot(grad_all, down_turned)
    g_gate_low = (g_hidden * up_pre * swish_slope(gate_pre)).astype(jnp.bfloat16)
    g_up_low = (g_hidden * gate_swish).astype(jnp.bfloat16)
    g_ffn_in = lax.psum_scatter(
        (contract_cols(g_gate_low, gate_weight) + contract_cols(g_up_low, up_weight)).astype(jnp.bfloat16),
        "tensor",
        scatter_dimension=0,
        tiled=True,
    ).astype(jnp.float32)
    ffn_out = lax.psum_scatter(
        contract_cols(hidden_low, down_turned).astype(jnp.bfloat16), "tensor", scatter_dimension=0, tiled=True
    ).astype(jnp.float32)
    block_out = (mixed_rows + ffn_out).astype(jnp.bfloat16)

    grad_float = out_grad.astype(jnp.float32)
    g_gain_ffn = jnp.sum(g_ffn_in * normed_two, axis=0)
    g_mixed = grad_float + norm_backward(g_ffn_in * gain_rows[3], normed_two, scale_two)
    half_grad = 0.5 * g_mixed
    g_gain_attn = jnp.sum(half_grad * attn_normed, axis=0)
    g_attn_low = norm_backward(half_grad * gain_rows[1], attn_normed, attn_scale).astype(jnp.bfloat16)
    g_gain_mamba = jnp.sum(half_grad * mamba_normed, axis=0)
    g_mamba_low = norm_backward(half_grad * gain_rows[2], mamba_normed, mamba_scale).astype(jnp.bfloat16)
    g_mamba_all = lax.all_gather(g_mamba_low, "tensor", axis=0, tiled=True)
    r_gate, r_up, r_down = scatter_rows(
        (low_rows(ffn_all, g_gate_low), low_rows(ffn_all, g_up_low), low_rows(grad_all, hidden_low))
    )

    g_attended = contract_cols(g_attn_low, output_weight).astype(jnp.bfloat16)
    g_query_low, g_key_low, g_value_low, g_meta_key, g_meta_value = attention_backward(
        g_attended,
        query_low,
        key_low,
        value_low,
        meta_keys,
        meta_values,
        allowed,
        log_total,
        cosine_table,
        sine_table,
    )
    meta_exact = meta_low.astype(jnp.float32)
    g_query = low_rows(normed_low, g_query_low)
    g_output = low_rows(attended, g_attn_low)
    g_key = contract_rows(normed_low, g_key_low) + contract_rows_exact(meta_exact, g_meta_key)
    g_value = contract_rows(normed_low, g_value_low) + contract_rows_exact(meta_exact, g_meta_value)
    r_query, r_output, r_key, r_value = scatter_rows(
        (g_query, g_output, g_key.astype(jnp.bfloat16), g_value.astype(jnp.bfloat16))
    )

    g_gated = plain_dot(g_mamba_all, out_turned)
    g_gate_raw_low, g_feed_part, g_step_low, g_input_cols, g_output_cols, g_rate, g_skip, g_dt_shift = scan_bwd(
        g_gated,
        gate_raw,
        combined,
        feed_rows,
        step_raw,
        keep_state,
        input_cols,
        output_cols,
        starts,
        decay_rate,
        skip_weight[None],
        SEQ_LEN,
    )
    g_projected = lax.psum(
        jnp.concatenate(
            [contract_cols(g_step_low, dtproj_weight), from_cols(g_input_cols), from_cols(g_output_cols)], axis=1
        ),
        "tensor",
    )
    (r_out,) = scatter_rows((low_rows(g_mamba_all, mamba_low),))
    g_dtproj = contract_rows(rank_low, g_step_low)
    g_projected_low = g_projected.astype(jnp.bfloat16)
    g_feed = g_feed_part + contract_cols(g_projected_low, xproj_weight)
    g_conv_raw = g_feed * swish_slope(conv_raw)
    g_mamba_in, g_conv_taps, g_conv_shift = causal_conv_grad(g_conv_raw, mamba_in, conv_taps, masks)
    g_in_low = g_mamba_in.astype(jnp.bfloat16)
    g_normed = lax.psum_scatter(
        (contract_cols(g_in_low, in_first) + contract_cols(g_gate_raw_low, in_second)).astype(jnp.bfloat16),
        "tensor",
        scatter_dimension=0,
        tiled=True,
    ).astype(jnp.float32)
    r_in_first, r_in_second = scatter_rows((low_rows(normed_all, g_in_low), low_rows(normed_all, g_gate_raw_low)))
    g_xproj = contract_rows(feed_low, g_projected_low)

    key_float = key_weight.astype(jnp.float32)
    value_float = value_weight.astype(jnp.float32)
    g_normed = (
        g_normed
        + contract_cols(g_query_low, query_weight)
        + contract_cols(g_key_low, key_weight)
        + contract_cols(g_value_low, value_weight)
    )
    g_meta_normed = contract_cols_exact(g_meta_key, key_float) + contract_cols_exact(g_meta_value, value_float)
    g_gain_in = jnp.sum(g_normed * normed_one, axis=0) + jnp.sum(g_meta_normed * meta_normed, axis=0)
    tokens_grad = g_mixed + norm_backward(g_normed * gain_rows[0], normed_one, scale_one)
    g_meta = norm_backward(g_meta_normed * gain_rows[0], meta_normed, meta_scale)
    g_gains = jnp.stack([g_gain_in, g_gain_attn, g_gain_mamba, g_gain_ffn])
    r_meta, r_gains, r_xproj, r_dtproj, r_conv, r_convbias, r_dtbias, r_alog, r_skip = scatter_small(
        (
            g_meta,
            g_gains,
            g_xproj,
            g_dtproj,
            g_conv_taps,
            g_conv_shift,
            g_dt_shift[0],
            g_rate * decay_rate,
            g_skip[0],
        ),
        small_dims,
        dp_count,
    )
    shared = lax.psum((r_query, r_key, r_value, r_output, r_meta, r_gains), "tensor")
    s_query, s_key, s_value, s_output, s_meta, s_gains = [item.astype(jnp.float32) for item in shared]
    wide = lambda item: item.astype(jnp.float32)
    return (
        block_out,
        tokens_grad,
        s_query,
        jnp.stack([s_key, s_value]),
        s_output,
        s_meta,
        s_gains,
        jnp.stack([wide(r_in_first), wide(r_in_second)]),
        wide(r_xproj)[None],
        wide(r_dtproj)[:, None],
        wide(r_conv)[:, None],
        wide(r_convbias)[None],
        wide(r_dtbias)[None],
        wide(r_alog)[:, None],
        wide(r_skip)[None],
        wide(r_out).T,
        jnp.stack([wide(r_gate), wide(r_up)]),
        wide(r_down).T,
    )


IN_SPECS = (
    P(("dp", "tensor"), None),
    P("dp"),
    P(("dp", "tensor"), None),
    P("dp", None),
    P(None, "dp", None),
    P("dp", None),
    P("dp", None),
    P(None, "dp"),
    P(None, "dp", "tensor"),
    P("tensor", "dp", None),
    P(None, "tensor", "dp"),
    P(None, "tensor", "dp"),
    P("tensor", "dp"),
    P("tensor", "dp"),
    P(None, "tensor", "dp"),
    P("tensor", "dp"),
    P("tensor", "dp"),
    P(None, "dp", "tensor"),
    P("tensor", "dp"),
)
OUT_SPECS = IN_SPECS[:1] + (P(("dp", "tensor"), None),) + IN_SPECS[3:]


def solution(mesh):
    return jax.shard_map(per_device, mesh=mesh, in_specs=IN_SPECS, out_specs=OUT_SPECS, check_vma=False)
```

time: 2720 us -> 1730 us (0.64); the launches traced: 2670 us -> 1720 us
  other arithmetic: 540 us -> 70 us
  local copies, waits for them, and re-layouts: 509 us -> 91.6 us
  blocking collectives: 290 us -> 80.5 us
  Pallas kernels: 0 us -> 140 us
  waiting for transfers between devices: 1060 us -> 1090 us
    reduce_sum x241 -> x0, other arithmetic: 218 us -> none  [the longest x96 113 us: advance(): outputs.append(jnp.sum(output_block[:, offset, :, None] * running, axis=1))]
    unnamed x2 -> x0, blocking collectives: 162 us -> none
    while x240 -> x0, other arithmetic: 157 us -> none
    reduce_scatter x5 -> x4, waiting for transfers between devices: 366 us -> 224 us  [the longest x1 61.1 us: per_device(): lax.psum_scatter(contract_cols(hidden_low, down_turned).astype(jnp.bfloat...]
    pallas_call x0 -> x2, Pallas kernels: none -> 140 us  [the longest x1 105 us: scan_bwd(): pl.pallas_call(scan_bwd_kernel, grid=(seqs,), in_specs=[wide, wide, wide,...]
    squeeze x160 -> x0, local copies, waits for them, and re-layouts: 133 us -> none  [selective_scan(): finished, (starts, outputs) = lax.scan(advance, initial, pieces)]
    another operation x314 -> x11, local copies, waits for them, and re-layouts: 119 us -> 8.12 us  [the longest x4 2.62 us: pack(): return jnp.concatenate([piece.reshape(-1) for piece in pieces])]
    unnamed x30 -> x42, waiting for transfers between devices: 333 us -> 416 us
  transfers between devices with their start and end apart: 24 -> 30, of which waited for: 17 -> 24; matrix products, arithmetic and copies ran while one was open for 27% -> 17% of each run, Pallas kernels for 0% -> 8%
where the time goes in v1:
time: 1730 us; the launch traced here: 1720 us
  waiting for transfers between devices  1090 us (63%)
  matrix products  235 us (14%)
  Pallas kernels  140 us (8%)
  local copies, waits for them, and re-layouts  91.6 us (5%)
  blocking collectives  80.5 us (5%)
  other arithmetic  70 us (4%)
  between operations  17.3 us (1%)
    unnamed x42, waiting for transfers between devices  416 us
    all_gather x8, waiting for transfers between devices, gather_rows(): return [lax.all_gather(shard, 'dp', axis=0, tiled=True) for shard in shards]  148 us
    pallas_call x1, Pallas kernels, scan_bwd(): pl.pallas_call(scan_bwd_kernel, grid=(seqs,), in_specs=[wide, wide, wide,...  105 us
    dot_general x14, matrix products, plain_dot(): return jnp.dot(former, latter, preferred_element_type=jnp.float32)  77.6 us
    psum x1, waiting for transfers between devices, per_device(): lax.psum((r_query, r_key, r_value, r_output, r_meta, r_gains), 'tensor')  72 us
    all_gather x1, waiting for transfers between devices, per_device(): normed_all = lax.all_gather(normed_low, 'tensor', axis=0, tiled=True)  67.7 us
    all_gather x1, waiting for transfers between devices, per_device(): ffn_all = lax.all_gather(ffn_low, 'tensor', axis=0, tiled=True)  67.7 us
    dot_general x12, matrix products, contract_cols(): lax.dot_general(former, latter, (((1,), (1,)), ((), ())), preferred_eleme...  67 us
  transfers between devices with their start and end apart: 30, of which 24 were waited for; matrix products, arithmetic and copies ran while one was open for 17% of the time, Pallas kernels for 8%

profile of v1, /device:TPU:0, one launch (start us, length us, event | category | flops | bytes accessed | tf_op | source)
XLA Modules:
  0.0 1724.5 jit_solution(12895867359389860418)
XLA Ops:
  14.5 3.6 concatenate.72
  22.6 56.4 %all-reduce.28.cloned.1.call-done = bf16[415200]{0:T(1024)(128)(2,1)} async-done(((bf16[415200]{0:T(1024)(128)(2,1)}), bf16[415200]{0:T(1024)(128)(2,1)}) %all-reduce.28.cloned.1.call-update) | async-done | bytes 830416
  85.9 26.0 %all-gather.36.cloned.1.call-done = bf16[1,1600,800]{2,1,0:T(8,128)(2,1)} async-done(((bf16[1,200,800]{2,1,0:T(8,128)(2,1)}), bf16[1,1600,800]{2,1,0:T(8,128)(2,1)}) %all-gather.36.cloned.1.call-update) | async-done | bytes 2560016 | tf_op jit(solution)/shard_map/all_gather | solution.py:433
  111.8 67.7 %all-gather.24.cloned.1.call-done = bf16[1024,1600]{0,1:T(8,128)(2,1)} async-done(((bf16[256,1600]{0,1:T(8,128)(2,1)}), bf16[1024,1600]{0,1:T(8,128)(2,1)}) %all-gather.24.cloned.1.call-update) | async-done | bytes 3276816 | tf_op jit(solution)/shard_map/all_gather | solution.py:495
  179.6 6.9 fusion.33
  186.5 5.2 fusion.15
  200.9 10.2 all-gather.38.cloned.1.call-done
  211.1 8.6 fusion.29.gate_ref
  219.7 33.0 %all-reduce.26.cloned.1.call-done = f32[1024,132]{0,1:T(8,128)} async-done(((f32[1024,132]{0,1:T(8,128)}), f32[1024,132]{0,1:T(8,128)}) %all-reduce.26.cloned.1.call-update) | async-done | bytes 540688 | tf_op jit(solution)/shard_map/psum | solution.py:517
  258.3 35.7 %scan_forward.1 = (bf16[1024,800]{1,0:T(8,128)(2,1)}, f32[1024,800]{1,0:T(8,128)}, f32[4,16,16,800]{3,2,1,0:T(8,128)}) custom-call(f32[1024,800]{1,0:T(8,128)} %copy-done.2, f32[1024,800]{1,0:T(8,128)} %convolution_add_fusion.6.sraw_ref, f32[1024,800]{1,0:T(8,128)} %fusion.29.gate_ref, f32[1024,1]{1,0:T(8,128)} %copy.148.keep_ref, ...), custom_call_target="tpu_custom_call" | custom-call | tf_op jit(solution)/shard_map/scan_forward/pallas_call | solution.py:333
  294.1 8.0 convolution_convert_fusion.6
  304.9 15.6 all-gather.2
  320.5 15.7 all-gather.1
  348.8 4.8 fusion.140
  358.8 2.8 fusion.69
  361.6 14.6 all-gather.22.cloned.1.call-done
  376.2 6.2 multiply_reduce_fusion.7
  383.0 58.0 %reduce-scatter.35.cloned.1.call-done = bf16[256,1600]{0,1:T(8,128)(2,1)} async-done(((bf16[1024,1600]{0,1:T(8,128)(2,1)}), bf16[256,1600]{0,1:T(8,128)(2,1)}) %reduce-scatter.35.cloned.1.call-update) | async-done | bytes 819216 | tf_op jit(solution)/shard_map/reduce_scatter | solution.py:532
  448.2 59.8 %all-gather.32.cloned.1.call-done = bf16[1024,1600]{0,1:T(8,128)(2,1)} async-done(((bf16[256,1600]{0,1:T(8,128)(2,1)}), bf16[1024,1600]{0,1:T(8,128)(2,1)}) %all-gather.32.cloned.1.call-update) | async-done | bytes 3276816 | tf_op jit(solution)/shard_map/all_gather | solution.py:500
  508.0 38.0 %all-gather.30.cloned.1.call-done = bf16[1600,1376]{1,0:T(8,128)(2,1)} async-done(((bf16[200,1376]{1,0:T(8,128)(2,1)}), bf16[1600,1376]{1,0:T(8,128)(2,1)}) %all-gather.30.cloned.1.call-update) | async-done | bytes 4403216 | tf_op jit(solution)/shard_map/all_gather | solution.py:433
  546.0 9.9 fusion.141
  555.9 30.3 %all-gather.42.cloned.1.call-done = bf16[1,1600,1376]{2,1,0:T(8,128)(2,1)} async-done(((bf16[1,200,1376]{2,1,0:T(8,128)(2,1)}), bf16[1,1600,1376]{2,1,0:T(8,128)(2,1)}) %all-gather.42.cloned.1.call-update) | async-done | bytes 4403216 | tf_op jit(solution)/shard_map/all_gather | solution.py:433
  586.2 67.7 %all-gather.28.cloned.1.call-done = bf16[1024,1600]{0,1:T(8,128)(2,1)} async-done(((bf16[256,1600]{0,1:T(8,128)(2,1)}), bf16[1024,1600]{0,1:T(8,128)(2,1)}) %all-gather.28.cloned.1.call-update) | async-done | bytes 3276816 | tf_op jit(solution)/shard_map/all_gather | solution.py:543
  653.9 10.0 fusion.9
  663.9 28.4 %all-gather.40.cloned.1.call-done = bf16[1,1600,1376]{2,1,0:T(8,128)(2,1)} async-done(((bf16[1,200,1376]{2,1,0:T(8,128)(2,1)}), bf16[1,1600,1376]{2,1,0:T(8,128)(2,1)}) %all-gather.40.cloned.1.call-update) | async-done | bytes 4403216 | tf_op jit(solution)/shard_map/all_gather | solution.py:433
  692.3 15.2 multiply_convert_fusion.1
  707.5 8.3 fusion.7
  715.8 6.6 add_convert_fusion.1
  722.6 9.1 convolution_convert_fusion.5
  738.9 46.2 %reduce-scatter.39.cloned.1.call-done = bf16[256,1600]{0,1:T(8,128)(2,1)} async-done(((bf16[1024,1600]{0,1:T(8,128)(2,1)}), bf16[256,1600]{0,1:T(8,128)(2,1)}) %reduce-scatter.39.cloned.1.call-update) | async-done | bytes 819216 | tf_op jit(solution)/shard_map/reduce_scatter | solution.py:551
  785.1 3.0 fusion.59
  788.7 61.1 %reduce-scatter.37.cloned.1.call-done = bf16[256,1600]{0,1:T(8,128)(2,1)} async-done(((bf16[1024,1600]{0,1:T(8,128)(2,1)}), bf16[256,1600]{0,1:T(8,128)(2,1)}) %reduce-scatter.37.cloned.1.call-update) | async-done | bytes 819216 | tf_op jit(solution)/shard_map/reduce_scatter | solution.py:557
  849.8 6.0 multiply_reduce_fusion.4
  862.4 4.6 convolution_convert_fusion.10
  869.6 5.1 fusion
  886.1 3.0 fusion.68
  894.1 4.1 convolution_convert_fusion.3
  903.5 4.1 convolution_convert_fusion.4
  909.5 8.7 convolution_convert_fusion.1
  918.7 8.7 convolution_convert_fusion.2
  929.3 8.7 fusion.4
  939.8 7.7 fusion.142.gg_ref
  947.6 104.6 %scan_backward.1 = (bf16[1024,800]{1,0:T(8,128)(2,1)}, f32[1024,800]{1,0:T(8,128)}, bf16[1024,800]{1,0:T(8,128)(2,1)}, f32[4,16,16,16]{3,2,1,0:T(8,128)}, f32[4,...) custom-call(f32[1024,800]{1,0:T(8,128)} %fusion.142.gg_ref, ...), custom_call_target="tpu_custom_call" | custom-call | tf_op jit(solution)/shard_map/scan_backward/pallas_call | solution.py:355
  1052.2 7.7 convolution_convert_fusion.8
  1062.9 29.6 %all-reduce.33 = bf16[1024,132]{0,1:T(8,128)(2,1)S(1)} all-reduce(f32[1024,132]{0,1:T(8,128)S(1)} %pad_maximum_fusion.2), channel_id=1, replica_groups=mesh['dp'=8,'tensor'=4] {'tensor'}, use_global_device_ids=true, to_apply=%region_15.16 | all-reduce | flops 135168 | bytes 811008 | tf_op jit(solution)/shard_map/psum | solution.py:612
  1092.5 11.9 fusion.131
  1107.9 7.0 convolution_convert_fusion.9
  1115.1 6.9 convolution_convert_fusion.7
  1124.2 9.0 reduce-scatter.43.cloned.1.call-done
  1133.3 5.7 fusion.31
  1139.0 5.0 add_convert_fusion
  1147.9 3.0 multiply_reduce_fusion.9
  1156.2 37.8 %reduce-scatter.59.cloned.1.call-done = bf16[200,1376]{1,0:T(8,128)(2,1)} async-done(((bf16[1600,1376]{1,0:T(8,128)(2,1)}), bf16[200,1376]{1,0:T(8,128)(2,1)}) %reduce-scatter.59.cloned.1.call-update) | async-done | bytes 550416
  1193.9 60.7 %reduce-scatter.57.cloned.1.call-done = bf16[200,1376]{1,0:T(8,128)(2,1)} async-done(((bf16[1600,1376]{1,0:T(8,128)(2,1)}), bf16[200,1376]{1,0:T(8,128)(2,1)}) %reduce-scatter.57.cloned.1.call-update) | async-done | bytes 550416
  1257.4 57.8 %reduce-scatter.61.cloned.1.call-done = bf16[200,1376]{1,0:T(8,128)(2,1)} async-done(((bf16[1600,1376]{1,0:T(8,128)(2,1)}), bf16[200,1376]{1,0:T(8,128)(2,1)}) %reduce-scatter.61.cloned.1.call-update) | async-done | bytes 550416
  1327.4 38.4 %reduce-scatter.53.cloned.1.call-done = bf16[200,800]{1,0:T(8,128)(2,1)} async-done(((bf16[1600,800]{1,0:T(8,128)(2,1)}), bf16[200,800]{1,0:T(8,128)(2,1)}) %reduce-scatter.53.cloned.1.call-update) | async-done | bytes 320016
  1365.8 50.4 %reduce-scatter.51.cloned.1.call-done = bf16[200,800]{1,0:T(8,128)(2,1)} async-done(((bf16[1600,800]{1,0:T(8,128)(2,1)}), bf16[200,800]{1,0:T(8,128)(2,1)}) %reduce-scatter.51.cloned.1.call-update) | async-done | bytes 320016
  1418.6 48.1 %reduce-scatter.55.cloned.1.call-done = bf16[200,800]{1,0:T(8,128)(2,1)} async-done(((bf16[1600,800]{1,0:T(8,128)(2,1)}), bf16[200,800]{1,0:T(8,128)(2,1)}) %reduce-scatter.55.cloned.1.call-update) | async-done | bytes 320016
  1468.6 72.0 %all-reduce.32.cloned.1.call-done = (bf16[200,1600]{1,0:T(8,128)(2,1)}, bf16[1,200,320]{2,1,0:T(8,128)(2,1)}, bf16[1,200,320]{2,1,0:T(8,128)(2,1)}, bf16[200,1600]{1,0:T(8,128)(2,1)}) async-done(((bf16[200,1600]{1,0:T(8,128)(2,1)}, bf16[1,200,320]{2,1,0:T(8,128)(2,1)}, bf16[1,200,320]{2,1,0:T(8,128)(2,1)}, bf16[200,1600]{1,0:T(8,128)(2,1)}), (bf16[200,1600]{1,0:T(8,128)(2,1)}, ...) | async-done | bytes 1536016 | tf_op jit(solution)/shard_map/psum | solution.py:662
  1546.0 58.4 %reduce-scatter.41.cloned.1.call-done = bf16[256,1600]{0,1:T(8,128)(2,1)} async-done(((bf16[1024,1600]{0,1:T(8,128)(2,1)}), bf16[256,1600]{0,1:T(8,128)(2,1)}) %reduce-scatter.41.cloned.1.call-update) | async-done | bytes 819216 | tf_op jit(solution)/shard_map/reduce_scatter | solution.py:625
  1604.4 4.4 convolution_add_fusion.4
  1625.4 3.5 fusion.65
  1628.9 52.6 %all-reduce.30.cloned.1.call-done = bf16[8,51900]{1,0:T(8,128)(2,1)} async-done(((bf16[8,51900]{1,0:T(8,128)(2,1)}), bf16[8,51900]{1,0:T(8,128)(2,1)}) %all-reduce.30.cloned.1.call-update) | async-done | bytes 830416
  1691.9 19.6 %all-reduce.18 = (bf16[16,1600]{1,0:T(8,128)(2,1)S(1)}, bf16[4,200]{1,0:T(4,128)(2,1)S(1)}) all-reduce(bf16[16,1600]{1,0:T(8,128)(2,1)S(1)} %reshape.703, bf16[4,200]{1,0:T(4,128)(2,1)S(1)} %reshape.704), channel_id=1, replica_groups=mesh['dp'=8,'tensor'=4] {'tensor'}, use_global_device_ids=true, to_apply=%region_41.42 | all-reduce | flops 26400 | bytes 105600 | tf_op jit(solution)/shard_map/psum | solution.py:662
  (510 shorter events, 179.6 us)
Async XLA Ops:
  7.2 15.2 copy-start.11
  7.2 71.8 %all-reduce.28.cloned.1.call-start = ((), (), s32[]{:S(2)}) async-start(), calls=%async_computation.31 | async-start | bytes 1662976
  20.2 91.6 %all-gather.36.cloned.1.call-start = ((), (), s32[]{:S(2)}) async-start(), calls=%async_computation.27 | async-start | bytes 3225600 | tf_op jit(solution)/shard_map/all_gather | solution.py:433
  22.3 61.0 %copy-start.71 = (s32[1024]{0:T(1024)S(1)}, s32[1024]{0:T(1024)}, u32[]{:S(2)}) copy-start(s32[1024]{0:T(1024)} %param.20) | copy-start | bytes 12292
  22.3 157.3 %all-gather.24.cloned.1.call-start = ((), (), s32[]{:S(2)}) async-start(), calls=%async_computation.16 | async-start | bytes 4096000 | tf_op jit(solution)/shard_map/all_gather | solution.py:495
  22.6 62.3 %copy-start.93 = (f32[256]{0:T(256)}, f32[256]{0:T(256)S(1)}, u32[]{:S(2)}) copy-start(f32[256]{0:T(256)S(1)} %add_rsqrt_fusion.3) | copy-start | bytes 3076
  81.2 255.3 %copy-start.24 = (bf16[8,51900]{1,0:T(8,128)(2,1)}, bf16[8,51900]{1,0:T(8,128)(2,1)S(1)}, u32[]{:S(2)}) copy-start(bf16[8,51900]{1,0:T(8,128)(2,1)S(1)} %reshape.717) | copy-start | bytes 2491204
  81.5 650.9 %copy-start.53 = (f32[1600]{0:T(1024)}, f32[1600]{0:T(1024)S(1)}, u32[]{:S(2)}) copy-start(f32[1600]{0:T(1024)S(1)} %mul.706) | copy-start | bytes 19204
  82.7 128.4 %all-gather.38.cloned.1.call-start = ((), (), s32[]{:S(2)}) async-start(), calls=%async_computation.28 | async-start | bytes 3225600 | tf_op jit(solution)/shard_map/all_gather | solution.py:433
  83.3 169.5 %all-reduce.26.cloned.1.call-start = ((), (), s32[]{:S(2)}) async-start(), calls=%async_computation.17 | async-start | bytes 1114112 | tf_op jit(solution)/shard_map/psum | solution.py:517
  84.6 101.9 %copy-start.98 = (pred[1024]{0:T(1024)(128)(4,1)}, pred[1024]{0:T(1024)(128)(4,1)S(1)}, u32[]{:S(2)}) copy-start(pred[1024]{0:T(1024)(128)(4,1)S(1)} %get-tuple-element.132) | copy-start | bytes 3076
  84.6 101.9 %copy-start.100 = (pred[1024]{0:T(1024)(128)(4,1)}, pred[1024]{0:T(1024)(128)(4,1)S(1)}, u32[]{:S(2)}) copy-start(pred[1024]{0:T(1024)(128)(4,1)S(1)} %get-tuple-element.169) | copy-start | bytes 3076
  84.6 101.9 %copy-start.102 = (pred[1024]{0:T(1024)(128)(4,1)}, pred[1024]{0:T(1024)(128)(4,1)S(1)}, u32[]{:S(2)}) copy-start(pred[1024]{0:T(1024)(128)(4,1)S(1)} %get-tuple-element.170) | copy-start | bytes 3076
  85.2 101.4 %copy-start.74 = (f32[800]{0:T(1024)}, f32[800]{0:T(1024)S(1)}, u32[]{:S(2)}) copy-start(f32[800]{0:T(1024)S(1)} %mul.744) | copy-start | bytes 9604
  85.2 101.3 %copy-start.76 = (f32[800]{0:T(1024)}, f32[800]{0:T(1024)S(1)}, u32[]{:S(2)}) copy-start(f32[800]{0:T(1024)S(1)} %mul.753) | copy-start | bytes 9604
  85.3 101.2 %copy-start.78 = (f32[800]{0:T(1024)}, f32[800]{0:T(1024)S(1)}, u32[]{:S(2)}) copy-start(f32[800]{0:T(1024)S(1)} %mul.750) | copy-start | bytes 9604
  85.4 101.2 %copy-start.80 = (f32[800]{0:T(1024)}, f32[800]{0:T(1024)S(1)}, u32[]{:S(2)}) copy-start(f32[800]{0:T(1024)S(1)} %mul.747) | copy-start | bytes 9604
  85.9 105.9 %copy-start.33 = (bf16[800,132]{1,0:T(8,128)(2,1)}, bf16[800,132]{1,0:T(8,128)(2,1)S(1)}, u32[]{:S(2)}) copy-start(bf16[800,132]{1,0:T(8,128)(2,1)S(1)} %reshape_reshape.12) | copy-start | bytes 633604
  195.2 98.9 %all-gather.26.cloned.1.call-start = ((), (), s32[]{:S(2)}) async-start(), calls=%async_computation.18 | async-start | bytes 3225600 | tf_op jit(solution)/shard_map/all_gather | solution.py:433
  195.8 153.0 %all-gather.20.cloned.1.call-start = ((), (), s32[]{:S(2)}) async-start(), calls=%async_computation.14 | async-start | bytes 5990400 | tf_op jit(solution)/shard_map/all_gather | solution.py:433
  196.5 179.7 %all-gather.22.cloned.1.call-start = ((), (), s32[]{:S(2)}) async-start(), calls=%async_computation.15 | async-start | bytes 5990400 | tf_op jit(solution)/shard_map/all_gather | solution.py:433
  197.3 243.7 %reduce-scatter.35.cloned.1.call-start = ((), (), s32[]{:S(2)}) async-start(), calls=%async_computation.19 | async-start | bytes 4096000 | tf_op jit(solution)/shard_map/reduce_scatter | solution.py:532
  200.9 55.0 %copy-start.43 = (bf16[100,800]{1,0:T(8,128)(2,1)}, bf16[100,800]{1,0:T(8,128)(2,1)S(1)}, u32[]{:S(2)}) copy-start(bf16[100,800]{1,0:T(8,128)(2,1)S(1)} %reshape.684) | copy-start | bytes 480004
  302.1 205.8 %all-gather.32.cloned.1.call-start = ((), (), s32[]{:S(2)}) async-start(), calls=%async_computation.23 | async-start | bytes 4096000 | tf_op jit(solution)/shard_map/all_gather | solution.py:500
  302.7 243.2 %all-gather.30.cloned.1.call-start = ((), (), s32[]{:S(2)}) async-start(), calls=%async_computation.21 | async-start | bytes 5068800 | tf_op jit(solution)/shard_map/all_gather | solution.py:433
  303.5 282.7 %all-gather.42.cloned.1.call-start = ((), (), s32[]{:S(2)}) async-start(), calls=%async_computation.30 | async-start | bytes 5068800 | tf_op jit(solution)/shard_map/all_gather | solution.py:433
  304.6 349.3 %all-gather.28.cloned.1.call-start = ((), (), s32[]{:S(2)}) async-start(), calls=%async_computation.20 | async-start | bytes 4096000 | tf_op jit(solution)/shard_map/all_gather | solution.py:543
  320.5 24.6 %copy-start.6 = (bf16[1,1600,320]{2,1,0:T(8,128)(2,1)}, bf16[1,1600,320]{2,1,0:T(8,128)(2,1)S(1)}, u32[]{:S(2)}) copy-start(bf16[1,1600,320]{2,1,0:T(8,128)(2,1)S(1)} %all-gather.2) | copy-start | bytes 3072004
  320.5 23.3 %copy-start.3 = (bf16[256,1600]{0,1:T(8,128)(2,1)S(1)}, bf16[256,1600]{0,1:T(8,128)(2,1)}, u32[]{:S(2)}) copy-start(bf16[256,1600]{0,1:T(8,128)(2,1)} %fusion.61) | copy-start | bytes 2457604
  337.6 104.8 %copy-start.72 = (f32[1600]{0:T(1024)}, f32[1600]{0:T(1024)S(1)}, u32[]{:S(2)}) copy-start(f32[1600]{0:T(1024)S(1)} %mul.760) | copy-start | bytes 19204
  447.5 244.8 %all-gather.40.cloned.1.call-start = ((), (), s32[]{:S(2)}) async-start(), calls=%async_computation.29 | async-start | bytes 5068800 | tf_op jit(solution)/shard_map/all_gather | solution.py:433
  448.1 337.0 %reduce-scatter.39.cloned.1.call-start = ((), (), s32[]{:S(2)}) async-start(), calls=%async_computation.24 | async-start | bytes 4096000 | tf_op jit(solution)/shard_map/reduce_scatter | solution.py:551
  692.3 15.2 copy-start.113
  722.5 127.2 %reduce-scatter.37.cloned.1.call-start = ((), (), s32[]{:S(2)}) async-start(), calls=%async_computation.22 | async-start | bytes 4096000 | tf_op jit(solution)/shard_map/reduce_scatter | solution.py:557
  731.7 206.5 %all-gather.34.cloned.1.call-start = ((), (), s32[]{:S(2)}) async-start(), calls=%async_computation.25 | async-start | bytes 4096000 | tf_op jit(solution)/shard_map/all_gather | solution.py:570
  857.7 266.5 %reduce-scatter.47.cloned.1.call-start = ((), (), s32[]{:S(2)}) async-start(), calls=%async_computation.35 | async-start | bytes 1382400
  884.8 239.4 %reduce-scatter.45.cloned.1.call-start = ((), (), s32[]{:S(2)}) async-start(), calls=%async_computation.34 | async-start | bytes 1382400
  894.0 230.1 %reduce-scatter.49.cloned.1.call-start = ((), (), s32[]{:S(2)}) async-start(), calls=%async_computation.36 | async-start | bytes 5990400
  898.2 235.0 %reduce-scatter.43.cloned.1.call-start = ((), (), s32[]{:S(2)}) async-start(), calls=%async_computation.33 | async-start | bytes 5990400
  907.6 286.3 %reduce-scatter.59.cloned.1.call-start = ((), (), s32[]{:S(2)}) async-start(), calls=%async_computation.41 | async-start | bytes 5068800
  918.3 336.4 %reduce-scatter.57.cloned.1.call-start = ((), (), s32[]{:S(2)}) async-start(), calls=%async_computation.40 | async-start | bytes 5068800
  927.4 387.8 %reduce-scatter.61.cloned.1.call-start = ((), (), s32[]{:S(2)}) async-start(), calls=%async_computation.42 | async-start | bytes 5068800
  938.1 427.8 %reduce-scatter.53.cloned.1.call-start = ((), (), s32[]{:S(2)}) async-start(), calls=%async_computation.38 | async-start | bytes 3225600
  1059.9 356.4 %reduce-scatter.51.cloned.1.call-start = ((), (), s32[]{:S(2)}) async-start(), calls=%async_computation.37 | async-start | bytes 3225600
  1060.1 32.4 %copy-start.34 = (bf16[800,132]{1,0:T(8,128)(2,1)S(1)}, bf16[800,132]{1,0:T(8,128)(2,1)}, u32[]{:S(2)}) copy-start(bf16[800,132]{1,0:T(8,128)(2,1)} %copy-done.33) | copy-start | bytes 633604
  1060.1 32.4 %copy-start.99 = (pred[1024]{0:T(1024)(128)(4,1)S(1)}, pred[1024]{0:T(1024)(128)(4,1)}, u32[]{:S(2)}) copy-start(pred[1024]{0:T(1024)(128)(4,1)} %copy-done.98) | copy-start | bytes 3076
  1060.1 32.4 %copy-start.101 = (pred[1024]{0:T(1024)(128)(4,1)S(1)}, pred[1024]{0:T(1024)(128)(4,1)}, u32[]{:S(2)}) copy-start(pred[1024]{0:T(1024)(128)(4,1)} %copy-done.100) | copy-start | bytes 3076
  1060.1 32.4 %copy-start.103 = (pred[1024]{0:T(1024)(128)(4,1)S(1)}, pred[1024]{0:T(1024)(128)(4,1)}, u32[]{:S(2)}) copy-start(pred[1024]{0:T(1024)(128)(4,1)} %copy-done.102) | copy-start | bytes 3076
  1115.0 8.5 copy-start.88
  1115.0 351.7 %reduce-scatter.55.cloned.1.call-start = ((), (), s32[]{:S(2)}) async-start(), calls=%async_computation.39 | async-start | bytes 3225600
  1122.0 11.3 copy-start.40
  1122.0 418.5 %all-reduce.32.cloned.1.call-start = ((), (), s32[]{:S(2)}) async-start(), calls=%async_computation.43 | async-start | bytes 3276800 | tf_op jit(solution)/shard_map/psum | solution.py:662
  1133.2 471.2 %reduce-scatter.41.cloned.1.call-start = ((), (), s32[]{:S(2)}) async-start(), calls=%async_computation.26 | async-start | bytes 4096000 | tf_op jit(solution)/shard_map/reduce_scatter | solution.py:625
  1144.0 537.4 %all-reduce.30.cloned.1.call-start = ((), (), s32[]{:S(2)}) async-start(), calls=%async_computation.32 | async-start | bytes 1662976
  1153.1 164.2 %copy-start.112 = (f32[1,800]{1,0:T(1,128)S(1)}, f32[1,800]{1,0:T(1,128)}, u32[]{:S(2)}) copy-start(f32[1,800]{1,0:T(1,128)} %get-tuple-element.37) | copy-start | bytes 9604
  1153.1 164.9 %copy-start.111 = (f32[1,800]{1,0:T(1,128)S(1)}, f32[1,800]{1,0:T(1,128)}, u32[]{:S(2)}) copy-start(f32[1,800]{1,0:T(1,128)} %get-tuple-element.39) | copy-start | bytes 9604
  1153.1 165.6 %copy-start.49 = (f32[16,800]{1,0:T(8,128)S(1)}, f32[16,800]{1,0:T(8,128)}, u32[]{:S(2)}) copy-start(f32[16,800]{1,0:T(8,128)} %neg.73.rate_ref) | copy-start | bytes 153604
  1153.2 165.6 %copy-start.73 = (f32[16,800]{1,0:T(8,128)S(1)}, f32[16,800]{1,0:T(8,128)}, u32[]{:S(2)}) copy-start(f32[16,800]{1,0:T(8,128)} %get-tuple-element.38) | copy-start | bytes 153604
  1154.3 165.3 %copy-start.42 = (f32[1024,132]{0,1:T(8,128)S(1)}, f32[1024,132]{0,1:T(8,128)}, u32[]{:S(2)}) copy-start(f32[1024,132]{0,1:T(8,128)} %all-reduce.26.cloned.1.call-done) | copy-start | bytes 1622020
  1418.6 185.8 %copy-start.38 = (bf16[256,25,64]{0,2,1:T(8,128)(2,1)S(1)}, bf16[256,25,64]{0,2,1:T(8,128)(2,1)}, u32[]{:S(2)}) copy-start(bf16[256,25,64]{0,2,1:T(8,128)(2,1)} %copy-done.37) | copy-start | bytes 2457604
  1546.0 62.9 %copy-start.47 = (bf16[256,5,64]{0,2,1:T(8,128)(2,1)S(1)}, bf16[256,5,64]{0,2,1:T(8,128)(2,1)}, u32[]{:S(2)}) copy-start(bf16[256,5,64]{0,2,1:T(8,128)(2,1)} %copy-done.46) | copy-start | bytes 491524
  1610.1 10.9 copy-start.110
  1610.1 12.3 copy-start.70
  1610.1 13.9 copy-start.109
  (90 other events, 290.8 us)
Sparse Core Ops, SparseCore 0:
  20.3 58.6 all-reduce.27
  81.4 30.3 all-gather.35
  114.0 65.5 all-gather.23
  181.9 29.1 all-gather.37
  213.9 38.8 all-reduce.25
  254.5 30.8 all-gather.25
  287.3 46.1 all-gather.19
  335.3 40.8 all-gather.21
  378.5 62.4 reduce-scatter.34
  442.4 65.5 all-gather.31
  509.9 36.0 all-gather.29
  548.3 37.8 all-gather.41
  588.3 65.5 all-gather.27
  656.2 36.0 all-gather.39
  722.6 62.4 reduce-scatter.38
  787.3 62.4 reduce-scatter.36
  857.8 65.5 all-gather.33
  927.1 34.2 reduce-scatter.46
  965.4 36.1 reduce-scatter.44
  1004.8 62.4 reduce-scatter.48
  1070.7 62.4 reduce-scatter.42
  1136.6 57.3 reduce-scatter.58
  1197.3 57.2 reduce-scatter.56
  1257.9 57.2 reduce-scatter.60
  1318.6 47.1 reduce-scatter.52
  1369.1 47.1 reduce-scatter.50
  1419.5 47.1 reduce-scatter.54
  1469.3 71.2 all-reduce.31
  1542.9 61.4 reduce-scatter.40
  1625.5 55.8 all-reduce.29

commit v2 on v1

v2 whole, which is shorter than its diff:
```python
import functools
import math

import jax
import jax.numpy as jnp
from jax import lax
from jax.experimental import pallas as pl
from jax.experimental.pallas import tpu as pltpu
from jax.sharding import PartitionSpec as P

HEADS = 25
KV_HEADS = 5
HEAD_DIM = 64
META = 128
STATE = 16
CONV = 4
DTR = 100
SEQ_LEN = 256

EPSILON = 1e-05
ROPE_BASE = 10000.0
NEG_FILL = -1e30


def plain_dot(former, latter):
    return jnp.dot(former, latter, preferred_element_type=jnp.float32)


def contract_rows(former, latter):
    return lax.dot_general(
        former, latter, (((0,), (0,)), ((), ())), preferred_element_type=jnp.float32
    )


def contract_cols(former, latter):
    return lax.dot_general(
        former, latter, (((1,), (1,)), ((), ())), preferred_element_type=jnp.float32
    )


def contract_rows_exact(former, latter):
    return lax.dot_general(
        former,
        latter,
        (((0,), (0,)), ((), ())),
        precision=lax.Precision.HIGHEST,
        preferred_element_type=jnp.float32,
    )


def contract_cols_exact(former, latter):
    return lax.dot_general(
        former,
        latter,
        (((1,), (1,)), ((), ())),
        precision=lax.Precision.HIGHEST,
        preferred_element_type=jnp.float32,
    )


def mix_sum(pattern, former, latter):
    return jnp.einsum(pattern, former, latter, preferred_element_type=jnp.float32)


def inverse_rms(operand):
    return lax.rsqrt(jnp.mean(operand * operand, axis=-1, keepdims=True) + EPSILON)


def norm_backward(cotangent, normed, scaling):
    return scaling * (cotangent - normed * jnp.mean(cotangent * normed, axis=-1, keepdims=True))


def swish_slope(operand):
    sigmoid = jax.nn.sigmoid(operand)
    return sigmoid * (1.0 + operand * (1.0 - sigmoid))


def rotary_tables(row_count):
    places = (jnp.arange(row_count, dtype=jnp.int32) % SEQ_LEN).astype(jnp.float32)
    powers = jnp.arange(HEAD_DIM // 2, dtype=jnp.int32).astype(jnp.float32) * (2.0 / HEAD_DIM)
    angles = places[:, None] * jnp.power(ROPE_BASE, -powers)[None, :]
    return (jnp.cos(angles)[:, None, :], jnp.sin(angles)[:, None, :])


def rotate_pairs(operand, cosine_table, sine_table):
    half_dim = operand.shape[-1] // 2
    leading = operand[..., :half_dim]
    trailing = operand[..., half_dim:]
    return jnp.concatenate(
        [
            leading * cosine_table - trailing * sine_table,
            leading * sine_table + trailing * cosine_table,
        ],
        axis=-1,
    )


def segment_mask(segments):
    per_sequence = segments.reshape(-1, SEQ_LEN)
    places = jnp.arange(SEQ_LEN, dtype=jnp.int32)
    return (per_sequence[:, :, None] == per_sequence[:, None, :]) & (
        places[:, None] >= places[None, :]
    )


def attention_inputs(
    normed_low, meta_low, query_weight, key_weight, value_weight, cosine_table, sine_table
):
    row_count = normed_low.shape[0]
    seq_count = row_count // SEQ_LEN
    groups = HEADS // KV_HEADS
    queries = rotate_pairs(
        product(normed_low, query_weight, jnp.float32).reshape(row_count, HEADS, HEAD_DIM),
        cosine_table,
        sine_table,
    )
    keys_rot = rotate_pairs(
        plain_dot(normed_low, key_weight).reshape(row_count, KV_HEADS, HEAD_DIM),
        cosine_table,
        sine_table,
    )
    query_low = queries.astype(jnp.bfloat16).reshape(seq_count, SEQ_LEN, KV_HEADS, groups, HEAD_DIM)
    key_low = keys_rot.astype(jnp.bfloat16).reshape(seq_count, SEQ_LEN, KV_HEADS, HEAD_DIM)
    value_low = (
        plain_dot(normed_low, value_weight)
        .astype(jnp.bfloat16)
        .reshape(seq_count, SEQ_LEN, KV_HEADS, HEAD_DIM)
    )
    meta_keys = (
        plain_dot(meta_low, key_weight).astype(jnp.bfloat16).reshape(META, KV_HEADS, HEAD_DIM)
    )
    meta_values = (
        plain_dot(meta_low, value_weight).astype(jnp.bfloat16).reshape(META, KV_HEADS, HEAD_DIM)
    )
    return (query_low, key_low, value_low, meta_keys, meta_values)


def attention_scores(query_low, key_low, meta_keys, allowed):
    score_scale = 1.0 / math.sqrt(HEAD_DIM)
    meta_scores = mix_sum("slkgd,nkd->skgln", query_low, meta_keys) * score_scale
    own_scores = mix_sum("slkgd,smkd->skglm", query_low, key_low) * score_scale
    own_scores = jnp.where(allowed[:, None, None], own_scores, NEG_FILL)
    return (meta_scores, own_scores)


def attention_forward(query_low, key_low, value_low, meta_keys, meta_values, allowed):
    meta_scores, own_scores = attention_scores(query_low, key_low, meta_keys, allowed)
    highest = jnp.maximum(jnp.max(meta_scores, axis=-1), jnp.max(own_scores, axis=-1))
    totals = jnp.sum(jnp.exp(meta_scores - highest[..., None]), axis=-1) + jnp.sum(
        jnp.exp(own_scores - highest[..., None]), axis=-1
    )
    log_total = highest + jnp.log(totals)
    meta_probs = jnp.exp(meta_scores - log_total[..., None]).astype(jnp.bfloat16)
    own_probs = jnp.exp(own_scores - log_total[..., None]).astype(jnp.bfloat16)
    mixed_heads = mix_sum("skgln,nkd->slkgd", meta_probs, meta_values) + mix_sum(
        "skglm,smkd->slkgd", own_probs, value_low
    )
    row_count = query_low.shape[0] * SEQ_LEN
    return (mixed_heads.reshape(row_count, HEADS * HEAD_DIM).astype(jnp.bfloat16), log_total)


def attention_backward(
    cotangent_low,
    query_low,
    key_low,
    value_low,
    meta_keys,
    meta_values,
    allowed,
    log_total,
    cosine_table,
    sine_table,
):
    row_count = query_low.shape[0] * SEQ_LEN
    score_scale = 1.0 / math.sqrt(HEAD_DIM)
    cotangent_low = cotangent_low.reshape(query_low.shape)
    meta_scores, own_scores = attention_scores(query_low, key_low, meta_keys, allowed)
    meta_probs = jnp.exp(meta_scores - log_total[..., None])
    own_probs = jnp.exp(own_scores - log_total[..., None])
    meta_dprob = mix_sum("slkgd,nkd->skgln", cotangent_low, meta_values)
    own_dprob = mix_sum("slkgd,smkd->skglm", cotangent_low, value_low)
    row_delta = jnp.sum(meta_probs * meta_dprob, axis=-1) + jnp.sum(own_probs * own_dprob, axis=-1)
    meta_dscore = (meta_probs * (meta_dprob - row_delta[..., None]) * score_scale).astype(
        jnp.bfloat16
    )
    own_dscore = (own_probs * (own_dprob - row_delta[..., None]) * score_scale).astype(jnp.bfloat16)
    back_query = mix_sum("skgln,nkd->slkgd", meta_dscore, meta_keys) + mix_sum(
        "skglm,smkd->slkgd", own_dscore, key_low
    )
    back_query = (
        rotate_pairs(back_query.reshape(row_count, HEADS, HEAD_DIM), cosine_table, -sine_table)
        .reshape(row_count, -1)
        .astype(jnp.bfloat16)
    )
    back_key = mix_sum("skglm,slkgd->smkd", own_dscore, query_low)
    back_key = (
        rotate_pairs(back_key.reshape(row_count, KV_HEADS, HEAD_DIM), cosine_table, -sine_table)
        .reshape(row_count, -1)
        .astype(jnp.bfloat16)
    )
    back_value = (
        mix_sum("skglm,slkgd->smkd", own_probs.astype(jnp.bfloat16), cotangent_low)
        .reshape(row_count, -1)
        .astype(jnp.bfloat16)
    )
    back_meta_key = mix_sum("skgln,slkgd->nkd", meta_dscore, query_low).reshape(META, -1)
    back_meta_value = mix_sum(
        "skgln,slkgd->nkd", meta_probs.astype(jnp.bfloat16), cotangent_low
    ).reshape(META, -1)
    return (back_query, back_key, back_value, back_meta_key, back_meta_value)


LOG2E = 1.4426950408889634
FAR = 1e6
BLK = 16
CORE, FIRST, SECOND = 1, 2, 4
MESH_ID = pl.DeviceIdType.MESH
LOW = jnp.bfloat16


def greet(peers=False):
    me = lax.axis_index("dp")
    barrier = pltpu.get_barrier_semaphore()
    for bit in (CORE, FIRST, SECOND):
        pl.semaphore_signal(barrier, inc=1, device_id={"dp": jnp.bitwise_xor(me, bit)}, device_id_type=MESH_ID)
    if peers:
        place = lax.axis_index("tensor")
        for k in range(1, 4):
            pl.semaphore_signal(barrier, inc=1, device_id={"tensor": jnp.bitwise_xor(place, k)}, device_id_type=MESH_ID)
    pl.semaphore_wait(barrier, 6 if peers else 3)


def split_rows(rows):
    return rows // 32 * 16 if rows > 128 else rows


class Gather:
    def __init__(self, arrays):
        self.arrays = arrays
        self.views = []
        for a, array in enumerate(arrays):
            subs = [None] if array.ndim == 2 else list(range(array.shape[0]))
            self.views += [(a, sub, array.shape[-2:]) for sub in subs]
        self.count = len(self.views)
        self.in_specs = [pl.BlockSpec(memory_space=pltpu.VMEM)] * len(arrays)
        self.out_specs = [pl.BlockSpec(memory_space=pl.ANY)] * self.count
        self.out_shape = [jax.ShapeDtypeStruct((8,) + shape, LOW) for _, _, shape in self.views]
        sems = pltpu.SemaphoreType.DMA((self.count, 9))
        self.scratch = [sems, sems, pltpu.SemaphoreType.DMA((self.count,))]
        self.sent = sum(math.prod(array.shape) for array in arrays) * 2
        self.results = lambda outs: [out.reshape(-1, out.shape[2]) for out in outs]

    def bind(self, ins, outs, scratch):
        self.shards = [ins[a] if sub is None else ins[a].at[sub] for a, sub, _ in self.views]
        self.wholes = outs
        self.send, self.recv, self.keep = scratch

    def stages(self):
        me = lax.axis_index("dp")

        def remote(i, slot, source, target, bit):
            return pltpu.make_async_remote_copy(
                src_ref=source,
                dst_ref=target,
                send_sem=self.send.at[i, slot],
                recv_sem=self.recv.at[i, slot],
                device_id={"dp": jnp.bitwise_xor(me, bit)},
                device_id_type=MESH_ID,
            )

        def part(ref, half, i):
            rows = self.views[i][2][0]
            cut = split_rows(rows)
            return ref.at[pl.ds(0, cut)] if half == 0 else ref.at[pl.ds(cut, rows - cut)]

        def halves(i):
            rows = self.views[i][2][0]
            return (0, 1) if split_rows(rows) < rows else (0,)

        bits = (FIRST, SECOND, CORE)

        def own(i, k):
            return remote(i, k, self.shards[i], self.wholes[i].at[me], bits[k])

        def local(i):
            return pltpu.make_async_copy(self.shards[i], self.wholes[i].at[me], self.keep.at[i])

        def onward(i, half):
            piece = part(self.wholes[i].at[jnp.bitwise_xor(me, bits[half])], half, i)
            return remote(i, 3 + half, piece, piece, bits[1 - half])

        def across(i, k):
            theirs = self.wholes[i].at[jnp.bitwise_xor(me, bits[k])]
            return remote(i, 5 + k, theirs, theirs, CORE)

        def across_far(i, half):
            piece = part(self.wholes[i].at[jnp.bitwise_xor(me, FIRST + SECOND)], half, i)
            return remote(i, 7 + half, piece, piece, CORE)

        def begin():
            greet()
            for i in range(self.count):
                for k in range(3):
                    own(i, k).start()
                local(i).start()

        def forward(i):
            for k in range(2):
                own(i, k).wait_recv()
                if k in halves(i):
                    onward(i, k).start()
                across(i, k).start()

        def last(i):
            for half in halves(i):
                onward(i, half).wait_recv()
                across_far(i, half).start()

        def finish():
            for i in range(self.count):
                own(i, 2).wait_recv()
                local(i).wait()
                for k in range(2):
                    across(i, k).wait_recv()
                for half in halves(i):
                    across_far(i, half).wait_recv()
            for i in range(self.count):
                for k in range(3):
                    own(i, k).wait_send()
                for k in range(2):
                    across(i, k).wait_send()
                for half in halves(i):
                    onward(i, half).wait_send()
                    across_far(i, half).wait_send()

        return begin, forward, last, finish


class Scatter:
    def __init__(self, groups, shared=0):
        self.totals = []
        self.places = []
        self.out_shape = []
        for o, group in enumerate(groups):
            for k, total in enumerate(group):
                self.totals.append(total.reshape(8, -1, total.shape[-1]))
                self.places.append((o, k if len(group) > 1 else None))
            shape = self.totals[-1].shape[1:]
            self.out_shape.append(jax.ShapeDtypeStruct(((len(group),) + shape) if len(group) > 1 else shape, jnp.float32))
        self.arrays = self.totals
        self.count = len(self.totals)
        self.sizes = [total.shape[1:] for total in self.totals]
        self.in_specs = [pl.BlockSpec(memory_space=pl.ANY)] * self.count
        self.out_specs = [pl.BlockSpec(memory_space=pltpu.VMEM)] * len(self.out_shape)
        self.shared = shared
        vm = pltpu.VMEM
        self.scratch = [vm((4,) + s, LOW) for s in self.sizes] * 1
        self.scratch += [vm((4,) + s, LOW) for s in self.sizes]
        self.scratch += [vm((2, split_rows(s[0]), s[1]), LOW) for s in self.sizes]
        self.scratch += [vm((2, max(s[0] - split_rows(s[0]), 16), s[1]), LOW) for s in self.sizes]
        self.scratch += [vm(s, LOW) for s in self.sizes]
        self.scratch += [vm(s, LOW) for s in self.sizes[:shared]]
        self.scratch += [vm((3,) + s, LOW) for s in self.sizes[:shared]]
        sems = pltpu.SemaphoreType.DMA((self.count, 13))
        self.scratch += [sems, sems, pltpu.SemaphoreType.DMA((self.count, 4))]
        self.sent = sum(math.prod(s) for s in self.sizes) * 2
        self.results = list

    def bind(self, ins, outs, scratch):
        n = self.count
        self.ins = ins
        self.outs = [outs[o] if k is None else outs[o].at[k] for o, k in self.places]
        self.mine, self.crossed, self.firsts, self.seconds, self.lasts = (scratch[k * n : (k + 1) * n] for k in range(5))
        self.sums = scratch[5 * n : 5 * n + self.shared]
        self.peers = scratch[5 * n + self.shared : 5 * n + 2 * self.shared]
        self.send, self.recv, self.keep = scratch[5 * n + 2 * self.shared :]

    def stages(self):
        me = lax.axis_index("dp")
        core = jnp.bitwise_and(me, 1)
        col = jnp.bitwise_and(lax.div(me, 2), 1)
        row = lax.div(me, 4)

        def remote(i, slot, source, target, bit):
            return pltpu.make_async_remote_copy(
                src_ref=source,
                dst_ref=target,
                send_sem=self.send.at[i, slot],
                recv_sem=self.recv.at[i, slot],
                device_id={"dp": jnp.bitwise_xor(me, bit)},
                device_id_type=MESH_ID,
            )

        def add_rows(rows, target, *sources):
            def add(at):
                total = sources[0][at, :].astype(jnp.float32)
                for source in sources[1:]:
                    total = total + source[at, :].astype(jnp.float32)
                target[at, :] = total.astype(target.dtype)

            if rows <= 128:
                add(pl.ds(0, rows))
            else:
                step = 8

                def body(n, carry):
                    add(pl.ds(pl.multiple_of(n * step, step), step))
                    return carry

                lax.fori_loop(0, rows // step, body, 0)

        def cut(half, i):
            rows = self.sizes[i][0]
            first = split_rows(rows)
            return pl.ds(0, first) if half == 0 else pl.ds(first, rows - first)

        def size(half, i):
            first = split_rows(self.sizes[i][0])
            return first if half == 0 else self.sizes[i][0] - first

        def halves(i):
            return (0, 1) if size(1, i) else (0,)

        def cross(i, k):
            return remote(i, k, self.ins[i].at[2 * k + 1 - core], self.crossed[i].at[k], CORE)

        def stay(i, k):
            return pltpu.make_async_copy(self.ins[i].at[2 * k + core], self.mine[i].at[k], self.keep.at[i, k])

        def first(i, half, other):
            if half == 0:
                return remote(i, 4 + other, self.mine[i].at[2 * other + 1 - col, cut(0, i)], self.firsts[i].at[other], FIRST)
            return remote(i, 6 + other, self.mine[i].at[2 * (1 - row) + other, cut(1, i)], self.seconds[i].at[other], SECOND)

        def second(i, half):
            if half == 0:
                return remote(i, 8, self.mine[i].at[2 * (1 - row) + col, cut(0, i)], self.lasts[i].at[cut(0, i)], SECOND)
            return remote(i, 9, self.mine[i].at[2 * row + 1 - col, cut(1, i)], self.lasts[i].at[cut(1, i)], FIRST)

        def begin():
            greet(self.shared > 0)
            for i in range(self.count):
                for k in range(4):
                    cross(i, k).start()
                    stay(i, k).start()

        def forward(i):
            for k in range(4):
                cross(i, k).wait_recv()
                stay(i, k).wait()
                add_rows(self.sizes[i][0], self.mine[i].at[k], self.mine[i].at[k], self.crossed[i].at[k])
            for half in halves(i):
                for other in range(2):
                    first(i, half, other).start()

        def last(i):
            for half in halves(i):
                for other in range(2):
                    first(i, half, other).wait_recv()
                    k = 2 * other + col if half == 0 else 2 * row + other
                    slot = self.mine[i].at[k, cut(half, i)]
                    add_rows(size(half, i), slot, slot, (self.firsts if half == 0 else self.seconds)[i].at[other])
                second(i, half).start()

        def peer(i, k):
            place = lax.axis_index("tensor")
            return pltpu.make_async_remote_copy(
                src_ref=self.sums[i],
                dst_ref=self.peers[i].at[k],
                send_sem=self.send.at[i, 10 + k],
                recv_sem=self.recv.at[i, 10 + k],
                device_id={"tensor": jnp.bitwise_xor(place, k + 1)},
                device_id_type=MESH_ID,
            )

        def finish():
            for i in range(self.count):
                for half in halves(i):
                    second(i, half).wait_recv()
                whole = self.mine[i].at[2 * row + col]
                if i < self.shared:
                    add_rows(self.sizes[i][0], self.sums[i], whole, self.lasts[i])
                    for k in range(3):
                        peer(i, k).start()
                else:
                    add_rows(self.sizes[i][0], self.outs[i], whole, self.lasts[i])
            for i in range(self.shared):
                for k in range(3):
                    peer(i, k).wait_recv()
                add_rows(self.sizes[i][0], self.outs[i], self.sums[i], *[self.peers[i].at[k] for k in range(3)])
            for i in range(self.count):
                for k in range(4):
                    cross(i, k).wait_send()
                for half in halves(i):
                    for other in range(2):
                        first(i, half, other).wait_send()
                    second(i, half).wait_send()
                if i < self.shared:
                    for k in range(3):
                        peer(i, k).wait_send()

        return begin, forward, last, finish


def tie_kernel(*refs):
    pass


def tie(value, *others):
    spec = pl.BlockSpec(memory_space=pl.ANY)
    return pl.pallas_call(
        tie_kernel,
        out_shape=jax.ShapeDtypeStruct(value.shape, value.dtype),
        in_specs=[spec] * (1 + len(others)),
        out_specs=spec,
        input_output_aliases={0: 0},
        name="tie",
    )(value, *others)


def comm_kernel(move, n_others, *refs):
    a = len(move.arrays)
    b = a + n_others
    c = b + len(move.out_shape)
    move.bind(refs[:a], refs[b:c], refs[c:])
    begin, forward, last, finish = move.stages()
    begin()
    for i in range(move.count):
        forward(i)
    for i in range(move.count):
        last(i)
    finish()


def comm_call(move, ident, name, others=()):
    outs = pl.pallas_call(
        functools.partial(comm_kernel, move, len(others)),
        out_shape=move.out_shape,
        in_specs=move.in_specs + [pl.BlockSpec(memory_space=pl.ANY)] * len(others),
        out_specs=move.out_specs,
        scratch_shapes=move.scratch,
        compiler_params=pltpu.CompilerParams(collective_id=ident, has_side_effects=True),
        cost_estimate=pl.CostEstimate(flops=0, bytes_accessed=100 * move.sent, transcendentals=0),
        name=f"{name}_{ident}",
    )(*move.arrays, *others)
    return move.results(outs)


def product_kernel(former_ref, latter_ref, out_ref):
    out_ref[...] = jnp.dot(former_ref[...], latter_ref[...], preferred_element_type=jnp.float32).astype(out_ref.dtype)


def product(former, latter, kind=LOW):
    rows, depth = former.shape
    block = next(size for size in (320, 128, rows) if rows % size == 0)
    return pl.pallas_call(
        product_kernel,
        grid=(rows // block,),
        in_specs=[pl.BlockSpec((block, depth), lambda r: (r, 0)), pl.BlockSpec(latter.shape, lambda r: (0, 0))],
        out_specs=pl.BlockSpec((block, latter.shape[1]), lambda r: (r, 0)),
        out_shape=jax.ShapeDtypeStruct((rows, latter.shape[1]), kind),
        cost_estimate=pl.CostEstimate(flops=2 * rows * depth * latter.shape[1], bytes_accessed=2 * former.size, transcendentals=0),
        name="product",
    )(former, latter)


def softplus(v):
    return jnp.maximum(v, 0.0) + jnp.log1p(jnp.exp(-jnp.abs(v)))


def sigmoid(v):
    return 1.0 / (1.0 + jnp.exp(-v))


def scan_fwd_body(feed_ref, sraw_ref, gate_ref, keep_ref, b_ref, c_ref, rate_ref, skip_ref, low_ref, comb_ref, starts_ref, h_scr, y_scr):
    blocks = feed_ref.shape[0] // BLK
    rate2 = rate_ref[...] * LOG2E

    @pl.when(pl.program_id(1) == 0)
    def _():
        h_scr[...] = jnp.zeros_like(h_scr)

    def body(n, carry):
        rows = pl.ds(pl.multiple_of(n * BLK, BLK), BLK)
        feed = feed_ref[rows, :]
        step = softplus(sraw_ref[rows, :])
        reach = jnp.where(keep_ref[rows, :] > 0.0, step, FAR)
        drive = step * feed
        bm = b_ref[0, n]
        cm = c_ref[0, n]
        h = h_scr[...]
        starts_ref[0, n] = h
        for j in range(BLK):
            a = jnp.exp2(reach[j : j + 1, :] * rate2)
            h = a * h + drive[j : j + 1, :] * bm[:, j : j + 1]
            y_scr[j : j + 1, :] = jnp.sum(h * cm[:, j : j + 1], axis=0, keepdims=True)
        h_scr[...] = h
        combined = y_scr[...] + skip_ref[...] * feed
        comb_ref[rows, :] = combined
        gate = gate_ref[rows, :]
        low_ref[rows, :] = (combined * (gate * sigmoid(gate))).astype(low_ref.dtype)
        return carry

    lax.fori_loop(0, blocks, body, 0)


def scan_bwd_body(
    gg_ref, gate_ref, comb_ref, feed_ref, sraw_ref, keep_ref, b_ref, c_ref, starts_ref, rate_ref, skip_ref,
    ggate_ref, gfeed_ref, gstep_ref, db_ref, dc_ref, drate_ref, dskip_ref, dbias_ref,
    dh_scr, h_scr, a_scr, du_scr, ds_scr,
):
    blocks = feed_ref.shape[0] // BLK
    rate = rate_ref[...]
    rate2 = rate * LOG2E
    lane = lax.broadcasted_iota(jnp.int32, (b_ref.shape[2], BLK), 1)

    @pl.when((pl.program_id(0) == 0) & (pl.program_id(1) == 0))
    def _():
        drate_ref[...] = jnp.zeros_like(drate_ref)
        dskip_ref[...] = jnp.zeros_like(dskip_ref)
        dbias_ref[...] = jnp.zeros_like(dbias_ref)

    @pl.when(pl.program_id(1) == 0)
    def _():
        dh_scr[...] = jnp.zeros_like(dh_scr)

    def body(i, carry):
        n = blocks - 1 - i
        rows = pl.ds(pl.multiple_of(n * BLK, BLK), BLK)
        feed = feed_ref[rows, :]
        sraw = sraw_ref[rows, :]
        step = softplus(sraw)
        reach = jnp.where(keep_ref[rows, :] > 0.0, step, FAR)
        drive = step * feed
        gate = gate_ref[rows, :]
        sig = sigmoid(gate)
        gg = gg_ref[rows, :]
        gcomb = gg * (gate * sig)
        ggate_ref[rows, :] = (gg * comb_ref[rows, :] * (sig * (1.0 + gate * (1.0 - sig)))).astype(ggate_ref.dtype)
        dskip_ref[...] += jnp.sum(gcomb * feed, axis=0, keepdims=True)
        bm = b_ref[0, n]
        cm = c_ref[0, n]
        h = starts_ref[0, n]
        for j in range(BLK):
            h_scr[j] = h
            a = jnp.exp2(reach[j : j + 1, :] * rate2)
            a_scr[j] = a
            h = a * h + drive[j : j + 1, :] * bm[:, j : j + 1]
        dh = dh_scr[...]
        drate = drate_ref[...]
        dbm = jnp.zeros(bm.shape, jnp.float32)
        dcm = jnp.zeros(bm.shape, jnp.float32)
        for j in reversed(range(BLK)):
            gy = gcomb[j : j + 1, :]
            dh = dh + cm[:, j : j + 1] * gy
            dcm = jnp.where(lane == j, jnp.sum(gy * h, axis=1, keepdims=True), dcm)
            dbm = jnp.where(lane == j, jnp.sum(dh * drive[j : j + 1, :], axis=1, keepdims=True), dbm)
            du_scr[j : j + 1, :] = jnp.sum(dh * bm[:, j : j + 1], axis=0, keepdims=True)
            dh = dh * a_scr[j]
            h = h_scr[j]
            thru = dh * h
            ds_scr[j : j + 1, :] = jnp.sum(thru * rate, axis=0, keepdims=True)
            drate = drate + thru * step[j : j + 1, :]
        dh_scr[...] = dh
        drate_ref[...] = drate
        db_ref[0, n] = dbm
        dc_ref[0, n] = dcm
        du = du_scr[...]
        gfeed_ref[rows, :] = gcomb * skip_ref[...] + du * step
        gsraw = (du * feed + ds_scr[...]) * sigmoid(sraw)
        dbias_ref[...] += jnp.sum(gsraw, axis=0, keepdims=True)
        gstep_ref[rows, :] = gsraw.astype(gstep_ref.dtype)
        return carry

    lax.fori_loop(0, blocks, body, 0)


def fused_kernel(body, n_in, n_prior, n_out, n_scr, move, plan, *refs):
    m_in, m_out = (len(move.arrays), len(move.out_shape)) if move else (0, 0)
    a = n_in + n_prior + m_in
    b = a + n_out + m_out
    ins, outs, scr = refs[:n_in], refs[a : a + n_out], refs[b : b + n_scr]
    if move:
        move.bind(refs[n_in + n_prior : a], refs[a + n_out : b], refs[b + n_scr :])
        begin, forward, last, finish = move.stages()
        step = pl.program_id(0) * pl.num_programs(1) + pl.program_id(1)
        for at, acts in plan(move.count):
            def run(acts=acts):
                for act, i in acts:
                    if act == "begin":
                        begin()
                    elif act == "forward":
                        forward(i)
                    else:
                        last(i)

            pl.when(step == at)(run)
    body(*ins, *outs, *scr)
    if move:
        pl.when(step == pl.num_programs(0) * pl.num_programs(1) - 1)(finish)


def scan_pieces(width, states, seq_len, chunk, back, base):
    pieces = seq_len // chunk
    turn = (lambda t: pieces - 1 - t) if back else (lambda t: t)
    wide = pl.BlockSpec((chunk, width), lambda s, t: ((s + base) * pieces + turn(t), 0))
    keep = pl.BlockSpec((chunk, 1), lambda s, t: ((s + base) * pieces + turn(t), 0))
    cols = pl.BlockSpec((1, chunk // BLK, states, BLK), lambda s, t: (s + base, turn(t), 0, 0))
    starts = pl.BlockSpec((1, chunk // BLK, states, width), lambda s, t: (s + base, turn(t), 0, 0))
    par = pl.BlockSpec((states, width), lambda s, t: (0, 0))
    row = pl.BlockSpec((1, width), lambda s, t: (0, 0))
    return wide, keep, cols, starts, par, row


def fused_call(body, operands, in_specs, out_specs, out_shape, scratch, grid, move, plan, ident, name, prior=(), others=()):
    n_in, n_out, n_scr = len(in_specs), len(out_specs), len(scratch)
    params = {}
    aliases = {n_in + k: k for k in range(len(prior))}
    operands = list(operands) + list(prior) + list(others)
    in_specs = in_specs + [pl.BlockSpec(memory_space=pl.ANY)] * (len(prior) + len(others))
    if move:
        operands = operands + list(move.arrays)
        in_specs = in_specs + move.in_specs
        out_specs = out_specs + move.out_specs
        out_shape = out_shape + move.out_shape
        scratch = scratch + move.scratch
        params = dict(collective_id=ident, has_side_effects=True)
    outs = pl.pallas_call(
        functools.partial(fused_kernel, body, n_in, len(prior) + len(others), n_out, n_scr, move, plan),
        grid=grid,
        in_specs=in_specs,
        out_specs=out_specs,
        out_shape=out_shape,
        scratch_shapes=scratch,
        input_output_aliases=aliases,
        compiler_params=pltpu.CompilerParams(**params),
        cost_estimate=pl.CostEstimate(flops=0, bytes_accessed=150_000_000, transcendentals=0),
        name=name,
    )(*operands)
    return outs[:n_out], (move.results(outs[n_out:]) if move else None)


def scan_fwd(feed, sraw, gate, keep, bcols, ccols, rate, skip, seq_len, move=None, plan=None, ident=None, chunk=128):
    rows, width = feed.shape
    seqs, states, nb = rows // seq_len, rate.shape[0], seq_len // BLK
    wide, keeps, cols, starts, par, row = scan_pieces(width, states, seq_len, chunk, False, 0)
    f32 = jnp.float32
    return fused_call(
        scan_fwd_body,
        (feed, sraw, gate, keep, bcols, ccols, rate, skip),
        [wide, wide, wide, keeps, cols, cols, par, row],
        [wide, wide, starts],
        [
            jax.ShapeDtypeStruct((rows, width), LOW),
            jax.ShapeDtypeStruct((rows, width), f32),
            jax.ShapeDtypeStruct((seqs, nb, states, width), f32),
        ],
        [pltpu.VMEM((states, width), f32), pltpu.VMEM((BLK, width), f32)],
        (seqs, seq_len // chunk),
        move,
        plan,
        ident,
        "scan_forward",
    )


def scan_bwd(
    gg, gate, comb, feed, sraw, keep, bcols, ccols, starts, rate, skip, seq_len,
    part=0, parts=1, prior=(), others=(), move=None, plan=None, ident=None, chunk=128,
):
    rows, width = feed.shape
    seqs, states, nb = rows // seq_len, rate.shape[0], seq_len // BLK
    wide, keeps, cols, startb, par, row = scan_pieces(width, states, seq_len, chunk, True, part * (seqs // parts))
    f32 = jnp.float32
    shape = jax.ShapeDtypeStruct
    return fused_call(
        scan_bwd_body,
        (gg, gate, comb, feed, sraw, keep, bcols, ccols, starts, rate, skip),
        [wide, wide, wide, wide, wide, keeps, cols, cols, startb, par, row],
        [wide, wide, wide, cols, cols, par, row, row],
        [
            shape((rows, width), LOW),
            shape((rows, width), f32),
            shape((rows, width), LOW),
            shape((seqs, nb, states, BLK), f32),
            shape((seqs, nb, states, BLK), f32),
            shape((states, width), f32),
            shape((1, width), f32),
            shape((1, width), f32),
        ],
        [
            pltpu.VMEM((states, width), f32),
            pltpu.VMEM((BLK, states, width), f32),
            pltpu.VMEM((BLK, states, width), f32),
            pltpu.VMEM((BLK, width), f32),
            pltpu.VMEM((BLK, width), f32),
        ],
        (seqs // parts, seq_len // chunk),
        move,
        plan,
        ident,
        "scan_backward",
        prior,
        others,
    )


def to_cols(mat, seq_len):
    rows, states = mat.shape
    return jnp.swapaxes(mat.reshape(rows // seq_len, seq_len // BLK, BLK, states), 2, 3)


def from_cols(cols):
    return jnp.swapaxes(cols, 2, 3).reshape(-1, cols.shape[2])


def lag_masks(segments):
    places = jnp.arange(segments.shape[0], dtype=jnp.int32) % SEQ_LEN
    masks = []
    for lag in range(1, CONV):
        before = jnp.concatenate([segments[:lag], segments[:-lag]])
        masks.append(((places >= lag) & (segments == before))[:, None])
    return masks


def causal_conv(mamba_in, conv_taps, conv_shift, masks):
    totals = conv_shift[None] + conv_taps[0][None] * mamba_in
    for lag in range(1, CONV):
        lagged = jnp.concatenate([jnp.zeros((lag, mamba_in.shape[1]), mamba_in.dtype), mamba_in[:-lag]])
        totals = totals + jnp.where(masks[lag - 1], conv_taps[lag][None] * lagged, 0.0)
    return totals


def causal_conv_grad(cotangent, mamba_in, conv_taps, masks):
    back_input = conv_taps[0][None] * cotangent
    tap_grads = [jnp.sum(cotangent * mamba_in, axis=0)]
    for lag in range(1, CONV):
        masked = jnp.where(masks[lag - 1], cotangent, 0.0)
        padding = jnp.zeros((lag, mamba_in.shape[1]), mamba_in.dtype)
        lagged = jnp.concatenate([padding, mamba_in[:-lag]])
        tap_grads.append(jnp.sum(masked * lagged, axis=0))
        back_input = back_input + conv_taps[lag][None] * jnp.concatenate([masked[lag:], padding])
    return back_input, jnp.stack(tap_grads), jnp.sum(cotangent, axis=0)


def fits():
    return lax.axis_size("dp") == 8 and lax.axis_size("tensor") == 4


def gather_rows(shards, ident, *others):
    if fits():
        return comm_call(Gather(shards), ident, "gather", others)
    planes = [plane for shard in shards for plane in ([shard] if shard.ndim == 2 else list(shard))]
    return [lax.all_gather(plane, "dp", axis=0, tiled=True) for plane in planes]


def scatter_plain(groups, shared=0):
    results, seen = [], 0
    for group in groups:
        shares = [lax.psum_scatter(total, "dp", scatter_dimension=0, tiled=True) for total in group]
        shares = [share.reshape(-1, share.shape[-1]) for share in shares]
        if seen < shared:
            shares = [lax.psum(share, "tensor") for share in shares]
        seen += len(group)
        shares = [share.astype(jnp.float32) for share in shares]
        results.append(jnp.stack(shares) if len(shares) > 1 else shares[0])
    return results


def scatter_rows(groups, ident, shared=0):
    if fits():
        return comm_call(Scatter(groups, shared), ident, "scatter")
    return scatter_plain(groups, shared)


def spread(total, dim, count):
    shape = total.shape[:dim] + (count, total.shape[dim] // count) + total.shape[dim + 1 :]
    return jnp.moveaxis(total.reshape(shape), dim, 0)


def join(parts, dim):
    parts = jnp.moveaxis(parts, 0, dim)
    return parts.reshape(parts.shape[:dim] + (-1,) + parts.shape[dim + 2 :])


def gather_plan(count):
    return [(0, [("begin", 0)])] + [(3 + 2 * i, [("forward", i)]) for i in range(count)] + [(7, [("last", i) for i in range(count)])]


def scatter_plan(count):
    return [
        (0, [("begin", 0)]),
        (1, [("forward", i) for i in range(count)]),
        (3, [("last", i) for i in range(count)]),
    ]


def edge(value):
    return value[tuple(slice(0, 8 if axis < value.ndim - 1 else 128) for axis in range(value.ndim))]


def hold(value, *others):
    return tie(value.T, *others).T


def low_rows(former, latter):
    return contract_rows(former, latter).astype(jnp.bfloat16)


def per_device(
    tokens,
    segment_ids,
    out_grad,
    w_query,
    w_keyval,
    w_output,
    meta_tokens,
    norm_gains,
    in_proj,
    x_proj,
    dt_proj,
    conv_weight,
    conv_bias,
    dt_bias,
    a_log,
    skip_gain,
    out_proj,
    gate_up,
    w_down,
):
    dp_count = lax.axis_size("dp")
    vectors = jnp.concatenate([a_log[:, 0], conv_weight[:, 0], conv_bias, dt_bias, skip_gain], axis=0)
    token_count = tokens.shape[0]
    member = lax.axis_index("tensor")
    tokens_all = lax.all_gather(tokens, "tensor", axis=0, tiled=True)
    xproj_weight, dtproj_weight, vectors, meta_rows, gain_rows, in_first, in_second = gather_rows(
        (x_proj[0], dt_proj[:, 0], vectors, meta_tokens, norm_gains, in_proj), 1
    )
    dtproj_weight = join(dtproj_weight.reshape((dp_count,) + dt_proj[:, 0].shape), 1)
    vectors = join(vectors.reshape(dp_count, -1, conv_bias.shape[1]), 1).astype(jnp.float32)
    gain_rows = join(gain_rows.reshape((dp_count,) + norm_gains.shape), 1).astype(jnp.float32)
    states, taps = a_log.shape[0], conv_weight.shape[0]
    decay_rate = -jnp.exp(vectors[:states])
    conv_taps = vectors[states : states + taps]
    conv_shift, dt_shift, skip_weight = (vectors[states + taps + k] for k in range(3))

    own_segments = lax.dynamic_slice_in_dim(segment_ids, member * token_count, token_count)
    residual = tokens.astype(jnp.float32)
    scale_one = inverse_rms(residual)
    normed_one = residual * scale_one
    normed_low = (normed_one * gain_rows[0]).astype(jnp.bfloat16)
    residual_all = tokens_all.astype(jnp.float32)
    scale_all = inverse_rms(residual_all)
    normed_all = (residual_all * scale_all * gain_rows[0]).astype(jnp.bfloat16)

    meta_float = meta_rows.astype(jnp.float32)
    meta_scale = inverse_rms(meta_float)
    meta_normed = meta_float * meta_scale
    meta_low = (meta_normed * gain_rows[0]).astype(jnp.bfloat16)
    cosine_table, sine_table = rotary_tables(token_count)
    allowed = segment_mask(own_segments)

    masks = lag_masks(segment_ids)
    keep_state = masks[0].astype(jnp.float32)
    mamba_in = plain_dot(normed_all, in_first)
    gate_raw = plain_dot(normed_all, in_second)
    conv_raw = causal_conv(mamba_in, conv_taps, conv_shift, masks)
    feed_rows = jax.nn.silu(conv_raw)
    feed_low = feed_rows.astype(jnp.bfloat16)
    projected_part = plain_dot(feed_low, xproj_weight)
    projected = lax.psum(projected_part, "tensor")
    query_weight, key_weight, value_weight = gather_rows((w_query, w_keyval), 2, edge(projected_part))

    query_low, key_low, value_low, meta_keys, meta_values = attention_inputs(
        normed_low, meta_low, query_weight, key_weight, value_weight, cosine_table, sine_table
    )
    attended, log_total = attention_forward(query_low, key_low, value_low, meta_keys, meta_values, allowed)

    projected = hold(projected, edge(attended), edge(gate_raw))
    rank_low = projected[:, :DTR].astype(jnp.bfloat16)
    step_raw = plain_dot(rank_low, dtproj_weight) + dt_shift
    input_cols = to_cols(projected[:, DTR : DTR + STATE], SEQ_LEN)
    output_cols = to_cols(projected[:, DTR + STATE :], SEQ_LEN)
    grad_all = lax.all_gather(tie(out_grad, step_raw), "tensor", axis=0, tiled=True)
    scan_args = (
        feed_rows, step_raw, gate_raw, keep_state, input_cols, output_cols, decay_rate, skip_weight[None], SEQ_LEN
    )
    out_shards = (w_output, out_proj.T)
    if fits():
        (mamba_low, combined, starts), moved = scan_fwd(*scan_args, move=Gather(out_shards), plan=gather_plan, ident=3)
    else:
        (mamba_low, combined, starts), _ = scan_fwd(*scan_args)
        moved = gather_rows(out_shards, 3)
    output_weight, out_turned = moved
    mamba_part = contract_cols(mamba_low, out_turned).astype(jnp.bfloat16)
    mamba_part = hold(mamba_part, edge(grad_all))
    mamba_out = lax.psum_scatter(mamba_part, "tensor", scatter_dimension=0, tiled=True)
    gate_weight, up_weight = gather_rows((gate_up,), 4, edge(mamba_part))
    attn_out = plain_dot(attended, output_weight)
    mamba_out = hold(mamba_out, gate_weight, edge(attn_out)).astype(jnp.float32)
    attn_scale = inverse_rms(attn_out)
    attn_normed = attn_out * attn_scale
    mamba_scale = inverse_rms(mamba_out)
    mamba_normed = mamba_out * mamba_scale
    mixed_rows = residual + 0.5 * (attn_normed * gain_rows[1] + mamba_normed * gain_rows[2])
    scale_two = inverse_rms(mixed_rows)
    normed_two = mixed_rows * scale_two
    ffn_low = (normed_two * gain_rows[3]).astype(jnp.bfloat16)
    ffn_all = lax.all_gather(ffn_low, "tensor", axis=0, tiled=True)
    (down_turned,) = gather_rows((w_down.T,), 5, edge(ffn_low))
    g_hidden = plain_dot(grad_all, down_turned)
    ffn_all = hold(ffn_all, edge(g_hidden))
    gate_pre = plain_dot(ffn_all, gate_weight)
    up_pre = plain_dot(ffn_all, up_weight)
    gate_swish = jax.nn.silu(gate_pre)
    hidden_low = (gate_swish * up_pre).astype(jnp.bfloat16)
    g_gate_low = (g_hidden * up_pre * swish_slope(gate_pre)).astype(jnp.bfloat16)
    g_up_low = (g_hidden * gate_swish).astype(jnp.bfloat16)
    g_ffn_part = (contract_cols(g_gate_low, gate_weight) + contract_cols(g_up_low, up_weight)).astype(jnp.bfloat16)
    g_ffn_in = lax.psum_scatter(g_ffn_part, "tensor", scatter_dimension=0, tiled=True)
    (r_down,) = scatter_rows(([low_rows(grad_all, hidden_low)],), 6)
    ffn_part = contract_cols(hidden_low, down_turned).astype(jnp.bfloat16)
    d_gate, d_up = low_rows(ffn_all, g_gate_low), low_rows(ffn_all, g_up_low)
    g_ffn_in = hold(g_ffn_in, r_down, edge(ffn_part), d_gate, d_up).astype(jnp.float32)

    grad_float = out_grad.astype(jnp.float32)
    g_gain_ffn = jnp.sum(g_ffn_in * normed_two, axis=0)
    g_mixed = grad_float + norm_backward(g_ffn_in * gain_rows[3], normed_two, scale_two)
    half_grad = 0.5 * g_mixed
    g_gain_attn = jnp.sum(half_grad * attn_normed, axis=0)
    g_attn_low = norm_backward(half_grad * gain_rows[1], attn_normed, attn_scale).astype(jnp.bfloat16)
    g_gain_mamba = jnp.sum(half_grad * mamba_normed, axis=0)
    g_mamba_low = norm_backward(half_grad * gain_rows[2], mamba_normed, mamba_scale).astype(jnp.bfloat16)
    g_mamba_all = lax.all_gather(g_mamba_low, "tensor", axis=0, tiled=True)

    g_attended = contract_cols(g_attn_low, output_weight).astype(jnp.bfloat16)
    g_query_low, g_key_low, g_value_low, g_meta_key, g_meta_value = attention_backward(
        g_attended,
        query_low,
        key_low,
        value_low,
        meta_keys,
        meta_values,
        allowed,
        log_total,
        cosine_table,
        sine_table,
    )
    meta_exact = meta_low.astype(jnp.float32)
    g_query = low_rows(normed_low, g_query_low)
    g_output = low_rows(attended, g_attn_low)
    g_key = contract_rows(normed_low, g_key_low) + contract_rows_exact(meta_exact, g_meta_key)
    g_value = contract_rows(normed_low, g_value_low) + contract_rows_exact(meta_exact, g_meta_value)
    query_side = contract_cols(g_query_low, query_weight)
    key_side = contract_cols(g_key_low, key_weight) + contract_cols(g_value_low, value_weight)
    attention_side = query_side + key_side
    g_key, g_value = g_key.astype(jnp.bfloat16), g_value.astype(jnp.bfloat16)
    g_mamba_all = hold(g_mamba_all, g_query, g_output, g_key, g_value, edge(attention_side))
    g_gated = plain_dot(g_mamba_all, out_turned)
    ffn_out = lax.psum_scatter(hold(ffn_part, g_gated), "tensor", scatter_dimension=0, tiled=True)
    block_out = (mixed_rows + ffn_out.astype(jnp.float32)).astype(jnp.bfloat16)
    attention_groups = ([g_query], [g_output], [g_key, g_value])
    ffn_groups = ([d_gate, d_up],)
    scan_args = (
        g_gated,
        gate_raw,
        combined,
        feed_rows,
        step_raw,
        keep_state,
        input_cols,
        output_cols,
        starts,
        decay_rate,
        skip_weight[None],
        SEQ_LEN,
    )
    if fits():
        first, attention_shares = scan_bwd(
            *scan_args, part=0, parts=2, move=Scatter(attention_groups), plan=scatter_plan, ident=7
        )
        second, ffn_shares = scan_bwd(
            *scan_args, part=1, parts=2, prior=first[:5], others=(edge(ffn_out),), move=Scatter(ffn_groups), plan=scatter_plan, ident=8
        )
        g_gate_raw_low, g_feed_part, g_step_low, g_input_cols, g_output_cols = second[:5]
        g_rate, g_skip, g_dt_shift = [former + latter for former, latter in zip(first[5:], second[5:])]
    else:
        (g_gate_raw_low, g_feed_part, g_step_low, g_input_cols, g_output_cols, g_rate, g_skip, g_dt_shift), _ = scan_bwd(
            *scan_args
        )
        attention_shares, ffn_shares = scatter_plain(attention_groups), scatter_plain(ffn_groups)
    s_query, s_output, s_keyval = lax.psum(tuple(item.astype(jnp.bfloat16) for item in attention_shares), "tensor")
    (r_gateup,) = ffn_shares
    g_projected = jnp.concatenate(
        [contract_cols(g_step_low, dtproj_weight), from_cols(g_input_cols), from_cols(g_output_cols)], axis=1
    )
    g_projected = lax.psum(hold(g_projected, s_query), "tensor")
    g_dtproj = low_rows(g_step_low, rank_low)
    g_out = product(g_mamba_all.T, mamba_low)
    g_projected_low = g_projected.astype(jnp.bfloat16)
    g_feed = g_feed_part + contract_cols(g_projected_low, xproj_weight)
    g_conv_raw = g_feed * swish_slope(conv_raw)
    g_mamba_in, g_conv_taps, g_conv_shift = causal_conv_grad(g_conv_raw, mamba_in, conv_taps, masks)
    g_in_low = g_mamba_in.astype(jnp.bfloat16)
    g_normed_part = contract_cols(g_in_low, in_first) + contract_cols(g_gate_raw_low, in_second)
    g_gain_in = jnp.sum(g_normed_part * (residual_all * scale_all), axis=0)
    g_normed_part = g_normed_part.astype(jnp.bfloat16)
    g_normed = lax.psum_scatter(g_normed_part, "tensor", scatter_dimension=0, tiled=True)
    g_xproj = low_rows(feed_low, g_projected_low)
    key_float = key_weight.astype(jnp.float32)
    value_float = value_weight.astype(jnp.float32)
    g_meta_normed = contract_cols_exact(g_meta_key, key_float) + contract_cols_exact(g_meta_value, value_float)
    g_gain_in = (
        g_gain_in + jnp.sum(attention_side * normed_one, axis=0) + jnp.sum(g_meta_normed * meta_normed, axis=0)
    )
    g_meta = norm_backward(g_meta_normed * gain_rows[0], meta_normed, meta_scale)
    g_gains = jnp.stack([g_gain_in, g_gain_attn, g_gain_mamba, g_gain_ffn])
    g_vectors = jnp.concatenate(
        [g_rate * decay_rate, g_conv_taps, g_conv_shift[None], g_dt_shift, g_skip], axis=0
    ).astype(LOW)
    s_meta, s_gains, r_xproj, r_dtproj, r_vectors, r_inproj, r_out = scatter_rows(
        (
            [g_meta.astype(LOW)],
            [spread(g_gains.astype(LOW), 1, dp_count)],
            [g_xproj],
            [g_dtproj],
            [spread(g_vectors, 1, dp_count)],
            [product(normed_all.T, g_in_low), product(normed_all.T, g_gate_raw_low)],
            [g_out],
        ),
        9,
        shared=2,
    )
    r_vectors = r_vectors.reshape(-1, conv_bias.shape[1])
    r_alog, r_conv = r_vectors[:states], r_vectors[states : states + taps]
    r_convbias, r_dtbias, r_skip = (r_vectors[states + taps + k][None] for k in range(3))
    g_normed = hold(g_normed, r_out).astype(jnp.float32) + attention_side
    tokens_grad = g_mixed + norm_backward(g_normed * gain_rows[0], normed_one, scale_one)
    wide = lambda item: item.astype(jnp.float32)
    return (
        block_out,
        tokens_grad,
        wide(s_query),
        wide(s_keyval),
        wide(s_output),
        s_meta,
        s_gains.reshape(norm_gains.shape),
        r_inproj,
        r_xproj[None],
        r_dtproj.T[:, None],
        r_conv[:, None],
        r_convbias,
        r_dtbias,
        r_alog[:, None],
        r_skip,
        r_out.T,
        r_gateup,
        r_down.T,
    )


IN_SPECS = (
    P(("dp", "tensor"), None),
    P("dp"),
    P(("dp", "tensor"), None),
    P("dp", None),
    P(None, "dp", None),
    P("dp", None),
    P("dp", None),
    P(None, "dp"),
    P(None, "dp", "tensor"),
    P("tensor", "dp", None),
    P(None, "tensor", "dp"),
    P(None, "tensor", "dp"),
    P("tensor", "dp"),
    P("tensor", "dp"),
    P(None, "tensor", "dp"),
    P("tensor", "dp"),
    P("tensor", "dp"),
    P(None, "dp", "tensor"),
    P("tensor", "dp"),
)
OUT_SPECS = IN_SPECS[:1] + (P(("dp", "tensor"), None),) + IN_SPECS[3:]


def solution(mesh):
    return jax.shard_map(per_device, mesh=mesh, in_specs=IN_SPECS, out_specs=OUT_SPECS, check_vma=False)
```

time: 1730 us -> 952 us (0.55)
  waiting for transfers between devices: 1090 us -> 116 us
  Pallas kernels: 140 us -> 434 us
  blocking collectives: 80.5 us -> 29.9 us
  matrix products: 235 us -> 198 us
    unnamed x42 -> x10, waiting for transfers between devices: 416 us -> 0.83 us
    pallas_call x2 -> x23, Pallas kernels: 140 us -> 434 us  [the longest x6 225 us: comm_call(): pl.pallas_call(functools.partial(comm_kernel, move, len(others)), out_sha...]
    all_gather x10 -> x2, waiting for transfers between devices: 275 us -> 18.6 us  [the longest x1 10.1 us: per_device(): lax.all_gather(tie(out_grad, step_raw), 'tensor', axis=0, tiled=True)]
    reduce_scatter x4, waiting for transfers between devices: 224 us -> 9.83 us  [the longest x1 9.81 us: per_device(): lax.psum_scatter(mamba_part, 'tensor', scatter_dimension=0, tiled=True)]
    psum x2, waiting for transfers between devices: 105 us -> 28.9 us  [the longest x1 26.4 us: per_device(): projected = lax.psum(projected_part, 'tensor')]
    all_gather x1, waiting for transfers between devices: 67.7 us -> 26 us  [per_device(): ffn_all = lax.all_gather(ffn_low, 'tensor', axis=0, tiled=True)]
    all_gather x1, waiting for transfers between devices: 0.02 us -> 31.7 us  [per_device(): g_mamba_all = lax.all_gather(g_mamba_low, 'tensor', axis=0, tiled=True)]
    all_gather x2 -> x0, blocking collectives: 31.4 us -> none  [gather_rows(): return [lax.all_gather(shard, 'dp', axis=0, tiled=True) for shard in shards]]
  transfers between devices with their start and end apart: 30 -> 10, of which waited for: 24 -> 7; matrix products, arithmetic and copies ran while one was open for 17% -> 18% of each run, Pallas kernels for 8% -> 41%
where the time goes in v2:
time: 952 us; the launch traced here: 942 us
  Pallas kernels  434 us (46%)
  matrix products  198 us (21%)
  waiting for transfers between devices  116 us (12%)
  local copies, waits for them, and re-layouts  89.7 us (9%)
  other arithmetic  57.1 us (6%)
  blocking collectives  29.9 us (3%)
  between operations  16.8 us (2%)
    pallas_call x6, Pallas kernels, comm_call(): pl.pallas_call(functools.partial(comm_kernel, move, len(others)), out_sha...  225 us
    pallas_call x3, Pallas kernels, fused_call(): pl.pallas_call(functools.partial(fused_kernel, body, n_in, len(prior) + l...  180 us
    dot_general x12, matrix products, contract_cols(): lax.dot_general(former, latter, (((1,), (1,)), ((), ())), preferred_eleme...  66.3 us
    dot_general x13, matrix products, plain_dot(): return jnp.dot(former, latter, preferred_element_type=jnp.float32)  65.9 us
    dot_general x9, matrix products, contract_rows(): lax.dot_general(former, latter, (((0,), (0,)), ((), ())), preferred_eleme...  41.1 us
    unnamed x348, local copies, waits for them, and re-layouts  34.4 us
    all_gather x1, waiting for transfers between devices, per_device(): g_mamba_all = lax.all_gather(g_mamba_low, 'tensor', axis=0, tiled=True)  31.7 us
    psum x1, blocking collectives, per_device(): g_projected = lax.psum(hold(g_projected, s_query), 'tensor')  29.9 us
  transfers between devices with their start and end apart: 10, of which 7 were waited for; matrix products, arithmetic and copies ran while one was open for 18% of the time, Pallas kernels for 41%

profile of v2, /device:TPU:0, one launch (start us, length us, event | category | flops | bytes accessed | tf_op | source)
XLA Modules:
  0.0 942.3 jit_solution(12920435169491066547)
XLA Ops:
  12.0 2.6 concatenate.85.refs_2_
  14.6 37.9 %gather_1.1 = (bf16[8,100,132]{2,1,0:T(8,128)(2,1)}, bf16[8,100,100]{2,1,0:T(8,128)(2,1)}, bf16[8,23,100]{2,1,0:T(8,128)(2,1)}, bf16[8,16,1600]{2,1,0:T(8,128)(2...) custom-call(bf16[100,132]{1,0:T(8,128)(2,1)} %bitcast.499, ...), custom_call_target="tpu_custom_call" | custom-call | bytes 74380000 | tf_op jit(solution)/shard_map/gather_1/pallas_call | solution.py:536
  69.4 8.5 all-gather.5.cloned.1.call-done
  77.9 2.8 fusion.4
  80.8 6.2 fusion.101
  87.1 5.2 fusion.11
  96.0 38.1 %gather_2.1 = (bf16[8,200,1600]{2,1,0:T(8,128)(2,1)}, bf16[8,200,320]{2,1,0:T(8,128)(2,1)}, bf16[8,200,320]{2,1,0:T(8,128)(2,1)}) custom-call(bf16[200,1600]{1,0:T(8,128)(2,1)} %refs_0_.3, bf16[2,200,320]{2,1,0:T(8,128)(2,1)} %refs_1_.1, f32[8,128]{1,0:T(8,128)} %copy.204.refs_2_), custom_call_target="tpu_custom_call" | custom-call | bytes 89600000 | tf_op jit(solution)/shard_map/gather_2/pallas_call | solution.py:536
  134.1 5.5 product.4
  139.7 2.7 copy.117
  142.4 2.2 copy.118
  156.4 7.2 fusion.99.refs_2_.refs_1_
  165.9 26.4 %all-reduce.11.cloned.1.call-done.refs_0_ = f32[132,1024]{1,0:T(8,128)} async-done(((f32[132,1024]{1,0:T(8,128)}), f32[132,1024]{1,0:T(8,128)}) %all-reduce.11.cloned.1.call-update) | async-done | bytes 540688 | tf_op jit(solution)/shard_map/psum | solution.py:971
  192.3 3.5 convolution_add_fusion.5.refs_1_.refs_4_
  202.0 43.8 %scan_forward.1 = (bf16[1024,800]{1,0:T(8,128)(2,1)}, f32[1024,800]{1,0:T(8,128)}, f32[4,16,16,800]{3,2,1,0:T(8,128)}, bf16[8,200,1600]{2,1,0:T(8,128)(2,1)}, bf16[8,200,800]{2,1,0:T(8,128)(2,1)}) custom-call(f32[1024,800]{1,0:T(8,128)} %copy-done.1, f32[1024,800]{1,0:T(8,128)} %convolution_add_fusion.5.refs_1_.refs_4_, f32[1024,800]{1,0:T(8,128)} %copy-done.10, ...), custom_call_target="tpu_custom_call" | custom-call | bytes 150000000 | tf_op jit(solution)/shard_map/scan_forward/pallas_call | solution.py:728
  245.8 7.8 convolution_convert_fusion.6.refs_0_
  253.6 10.1 %all-gather.7.cloned.1.call-done = bf16[1024,1600]{1,0:T(8,128)(2,1)} async-done(((bf16[256,1600]{1,0:T(8,128)(2,1)}), bf16[1024,1600]{1,0:T(8,128)(2,1)}) %all-gather.7.cloned.1.call-update) | async-done | bytes 3276816 | tf_op jit(solution)/shard_map/all_gather | solution.py:984
  265.9 4.8 multiply_reduce_fusion.7
  274.0 43.1 %gather_4.1 = (bf16[8,200,1376]{2,1,0:T(8,128)(2,1)}, bf16[8,200,1376]{2,1,0:T(8,128)(2,1)}) custom-call(bf16[2,200,1376]{2,1,0:T(8,128)(2,1)} %refs_0_.4, bf16[8,128]{1,0:T(8,128)(2,1)} %copy.131.refs_1_), custom_call_target="tpu_custom_call" | custom-call | bytes 110080000 | tf_op jit(solution)/shard_map/gather_4/pallas_call | solution.py:536
  317.1 9.8 %reduce-scatter.5.cloned.1.call-done = bf16[256,1600]{0,1:T(8,128)(2,1)} async-done(((bf16[1024,1600]{0,1:T(8,128)(2,1)}), bf16[256,1600]{0,1:T(8,128)(2,1)}) %reduce-scatter.5.cloned.1.call-update) | async-done | bytes 819216 | tf_op jit(solution)/shard_map/reduce_scatter | solution.py:997
  328.3 2.3 multiply_reduce_fusion.6
  333.5 26.1 %gather_5.1 = bf16[8,200,1376]{2,1,0:T(8,128)(2,1)} custom-call(bf16[200,1376]{1,0:T(8,128)(2,1)} %bitcast.496, bf16[8,128]{1,0:T(8,128)(2,1)} %copy.133.refs_1_), custom_call_target="tpu_custom_call" | custom-call | bytes 55040000 | tf_op jit(solution)/shard_map/gather_5/pallas_call | solution.py:536
  359.6 8.9 fusion.109
  368.6 2.5 copy-done.153
  371.7 26.0 %all-gather.9.cloned.1.call-done = bf16[1024,1600]{0,1:T(8,128)(2,1)} async-done(((bf16[256,1600]{0,1:T(8,128)(2,1)}), bf16[1024,1600]{0,1:T(8,128)(2,1)}) %all-gather.9.cloned.1.call-update) | async-done | bytes 3276816 | tf_op jit(solution)/shard_map/all_gather | solution.py:1009
  397.8 10.3 %fusion.110 = f32[1024,1376]{0,1:T(8,128)} fusion(bf16[1600,1024]{1,0:T(8,128)(2,1)} %tie.14, bf16[1600,1376]{1,0:T(8,128)(2,1)} %bitcast.514), kind=kOutput, calls=%fused_computation.232 | convolution fusion | flops 4508876800 | bytes 13316096 | tf_op jit(solution)/shard_map/dot_general | solution.py:26
  408.1 12.8 %multiply_convert_fusion = (bf16[1024,1376]{0,1:T(8,128)(2,1)}, bf16[1024,1376]{0,1:T(8,128)(2,1)}, bf16[1024,1376]{0,1:T(8,128)(2,1)}) fusion(f32[1024,1376]{0,1:T(8,128)} %copy-done.153, f32[1024,1376]{0,1:T(8,128)} %fusion.110, bf16[1600,1024]{1,0:T(8,128)(2,1)S(1)} %copy-done.50, bf16[1600,1376]{1,0:T(8,128)(2,1)S(1)} %bitcast.455), kind=kOutput, calls=%fused_computation.22 | convolution fusion | flops 4530012160 | bytes 27406336 | tf_op jit(solution)/shard_map/dot_general | solution.py:26
  420.9 7.4 fusion.118
  428.3 7.0 add_convert_fusion
  436.0 10.4 %convolution_convert_fusion.2 = bf16[1600,1376]{1,0:T(8,128)(2,1)} fusion(bf16[1024,1600]{1,0:T(8,128)(2,1)} %all-gather.7.cloned.1.call-done, bf16[1024,1376]{0,1:T(8,128)(2,1)} %get-tuple-element.183), kind=kOutput, calls=%fused_computation.6 | convolution fusion | flops 4511078400 | bytes 10498048 | tf_op jit(solution)/shard_map/dot_general | solution.py:30
  446.4 30.6 %scatter_6.1.refs_1_ = f32[200,1376]{1,0:T(8,128)} custom-call(bf16[8,200,1376]{2,1,0:T(8,128)(2,1)} %bitcast.451), custom_call_target="tpu_custom_call" | custom-call | bytes 55040000 | tf_op jit(solution)/shard_map/scatter_6/pallas_call | solution.py:536
  477.0 7.9 convolution_convert_fusion.5
  487.4 9.3 convolution_convert_fusion.refs_4_
  496.7 6.9 convolution_convert_fusion.1.refs_3_
  503.6 2.7 fusion.59
  506.3 3.5 multiply_reduce_fusion.4
  511.9 4.6 convolution_convert_fusion.7
  519.6 2.1 fusion.14
  532.1 4.5 fusion.119
  541.4 2.4 fusion.96
  550.6 4.0 convolution_convert_fusion.3.refs_2_
  554.6 4.2 convolution_convert_fusion.4.refs_1_
  558.8 31.7 %all-gather.11.cloned.1.call-done = bf16[1024,1600]{0,1:T(8,128)(2,1)} async-done(((bf16[256,1600]{0,1:T(8,128)(2,1)}), bf16[1024,1600]{0,1:T(8,128)(2,1)}) %all-gather.11.cloned.1.call-update) | async-done | bytes 3276816 | tf_op jit(solution)/shard_map/all_gather | solution.py:1034
  592.4 7.8 fusion.114.refs_1_.refs_0_
  600.2 76.2 %scan_backward.2 = (bf16[1024,800]{1,0:T(8,128)(2,1)}, f32[1024,800]{1,0:T(8,128)}, bf16[1024,800]{1,0:T(8,128)(2,1)}, f32[4,16,16,16]{3,2,1,0:T(8,128)}, f32[4,...) custom-call(f32[1024,800]{1,0:T(8,128)} %fusion.114.refs_1_.refs_0_,, ...), custom_call_target="tpu_custom_call" | custom-call | bytes 150000000 | tf_op jit(solution)/shard_map/scan_backward/pallas_call | solution.py:728
  676.4 2.3 convert_element_type.393
  678.7 2.2 convert_element_type.407
  683.2 59.9 %scan_backward.3 = (bf16[1024,800]{1,0:T(8,128)(2,1)}, f32[1024,800]{1,0:T(8,128)}, bf16[1024,800]{1,0:T(8,128)(2,1)}, f32[4,16,16,16]{3,2,1,0:T(8,128)}, f32[4,...) custom-call(f32[1024,800]{1,0:T(8,128)} %fusion.114.refs_1_.refs_0_,, ...), custom_call_target="tpu_custom_call", output_to_operand_aliasing={{0}: (11, {}), {1}: (12, {}), {2}: (13, {}), {3}: (14, {}),... | custom-call | bytes 150000000 | tf_op jit(solution)/shard_map/scan_backward/pallas_call | solution.py:728
  748.0 2.5 all-reduce.13.cloned.1.call-done
  750.5 29.9 %all-reduce.14 = bf16[1024,132]{0,1:T(8,128)(2,1)S(1)} all-reduce(f32[1024,132]{0,1:T(8,128)} %bitcast.448), channel_id=1, replica_groups=mesh['dp'=8,'tensor'=4] {'tensor'}, use_global_device_ids=true, to_apply=%region_20.21 | all-reduce | flops 135168 | bytes 811008 | tf_op jit(solution)/shard_map/psum | solution.py:1097
  780.4 13.4 %fusion.103 = (bf16[800]{0:T(1024)(128)(2,1)}, bf16[800]{0:T(1024)(128)(2,1)}, bf16[800]{0:T(1024)(128)(2,1)}, f32[1024,800]{1,0:T(8,128)S(1)}, bf16[800]{0:T(10...) fusion(f32[1024,800]{1,0:T(8,128)} %copy-done, ...), kind=kOutput, calls=%fused_computation.227 | convolution fusion | flops 233468000 | bytes 33241408 | tf_op jit(solution)/shard_map/dot_general | solution.py:36
  793.8 2.0 slice.276
  795.8 2.0 slice.277
  797.8 2.1 slice.278
  802.3 4.9 add_convert_fusion.1.latter_ref
  807.3 3.6 fusion.116
  811.3 7.5 fusion.3
  822.9 2.2 fusion.117
  825.1 3.6 multiply_reduce_fusion.9
  829.9 7.8 product.7
  839.0 2.3 convert_element_type.408
  845.5 2.5 convolution_convert_fusion.8
  851.4 7.7 product.6
  859.1 7.7 product.5
  866.8 49.4 %scatter_9.1 = (f32[16,1600]{1,0:T(8,128)}, f32[4,200]{1,0:T(4,128)}, f32[100,132]{1,0:T(8,128)}, f32[100,100]{1,0:T(8,128)}, f32[23,100]{1,0:T(8,128)}, /*index=5*/f32[2,200,800]{2,1,0:T(8,128)}, f32[200,800]{1,0:T(8,128)}) custom-call(bf16[8,16,1600]{2,1,0:T(8,128)(2,1)} %bitcast.480, bf16[8,4,200]{2,1,0:T(4,128)(2,1)} %maximum_bitcast_fusion.4.refs_1_, ...), custom_call_target="tpu_custom_call" | custom-call | bytes 106380000 | tf_op jit(solution)/shard_map/scatter_9/pallas_call | solution.py:536
  (533 shorter events, 129.7 us)
Async XLA Ops:
  7.2 53.1 %copy-start.7 = (bf16[256,1600]{0,1:T(8,128)(2,1)S(1)}, bf16[256,1600]{0,1:T(8,128)(2,1)}, u32[]{:S(2)}) copy-start(bf16[256,1600]{0,1:T(8,128)(2,1)} %param.19) | copy-start | bytes 2457604
  7.2 70.7 %all-gather.5.cloned.1.call-start = ((), (), s32[]{:S(2)}) async-start(), calls=%async_computation.4 | async-start | bytes 4096000 | tf_op jit(solution)/shard_map/all_gather | solution.py:935
  14.6 47.6 %copy-start.97 = (s32[1024]{0:T(1024)S(1)}, s32[1024]{0:T(1024)}, u32[]{:S(2)}) copy-start(s32[1024]{0:T(1024)} %param.20) | copy-start | bytes 12292
  53.2 11.6 %copy-start.52 = (bf16[256,1600]{0,1:T(8,128)(2,1)S(1)}, bf16[256,1600]{0,1:T(8,128)(2,1)}, u32[]{:S(2)}) copy-start(bf16[256,1600]{0,1:T(8,128)(2,1)} %param.21) | copy-start | bytes 2457604
  53.9 102.4 %copy-start.85 = (f32[1600]{0:T(1024)}, f32[1600]{0:T(1024)S(1)}, u32[]{:S(2)}) copy-start(f32[1600]{0:T(1024)S(1)} %mul.735) | copy-start | bytes 19204
  60.3 32.1 %copy-start.64 = (bf16[800,132]{0,1:T(8,128)(2,1)}, bf16[800,132]{0,1:T(8,128)(2,1)S(1)}, u32[]{:S(2)}) copy-start(bf16[800,132]{0,1:T(8,128)(2,1)S(1)} %reshape.682) | copy-start | bytes 633604
  60.3 5.9 copy-start.42
  60.8 86.0 %copy-start.11 = (bf16[256,1600]{0,1:T(8,128)(2,1)}, bf16[256,1600]{0,1:T(8,128)(2,1)S(1)}, u32[]{:S(2)}) copy-start(bf16[256,1600]{0,1:T(8,128)(2,1)S(1)} %fusion.44) | copy-start | bytes 2457604
  66.3 20.6 %copy-start.102 = (f32[8,16]{1,0:T(8,128)}, f32[8,16]{1,0:T(8,128)S(1)}, u32[]{:S(2)}) copy-start(f32[8,16]{1,0:T(8,128)S(1)} %add_rsqrt_fusion.1) | copy-start | bytes 1540
  67.6 19.3 %copy-start.135 = (pred[1024]{0:T(1024)(128)(4,1)}, pred[1024]{0:T(1024)(128)(4,1)S(1)}, u32[]{:S(2)}) copy-start(pred[1024]{0:T(1024)(128)(4,1)S(1)} %get-tuple-element.178) | copy-start | bytes 3076
  67.6 19.4 %copy-start.137 = (pred[1024]{0:T(1024)(128)(4,1)}, pred[1024]{0:T(1024)(128)(4,1)S(1)}, u32[]{:S(2)}) copy-start(pred[1024]{0:T(1024)(128)(4,1)S(1)} %get-tuple-element.208) | copy-start | bytes 3076
  67.6 19.4 %copy-start.139 = (pred[1024]{0:T(1024)(128)(4,1)}, pred[1024]{0:T(1024)(128)(4,1)S(1)}, u32[]{:S(2)}) copy-start(pred[1024]{0:T(1024)(128)(4,1)S(1)} %get-tuple-element.209) | copy-start | bytes 3076
  69.4 78.7 %copy-start.29 = (bf16[8,16,1600]{2,1,0:T(8,128)(2,1)}, bf16[8,16,1600]{2,1,0:T(8,128)(2,1)S(1)}, u32[]{:S(2)}) copy-start(bf16[8,16,1600]{2,1,0:T(8,128)(2,1)S(1)} %multiply_convert_fusion.5) | copy-start | bytes 1228804
  80.7 6.3 copy-start.147
  80.8 6.2 copy-start.104
  80.8 6.3 copy-start.106
  80.8 6.3 copy-start.108
  80.8 6.3 copy-start.110
  80.8 6.3 copy-start.132
  95.0 39.1 %copy-start.62 = (f32[1024,132]{0,1:T(8,128)}, f32[1024,132]{0,1:T(8,128)S(1)}, u32[]{:S(2)}) copy-start(f32[1024,132]{0,1:T(8,128)S(1)} %fusion.62) | copy-start | bytes 1622020
  95.1 97.3 %all-reduce.11.cloned.1.call-start = ((), (), s32[]{:S(2)}) async-start(), calls=%async_computation.5 | async-start | bytes 1114112 | tf_op jit(solution)/shard_map/psum | solution.py:971
  155.1 110.8 %copy-start.39 = (bf16[1,256,5,5,64]{1,4,3,2,0:T(8,128)(2,1)}, bf16[1,256,5,5,64]{1,4,3,2,0:T(8,128)(2,1)S(1)}, u32[]{:S(2)}) copy-start(bf16[1,256,5,5,64]{1,4,3,2,0:T(8,128)(2,1)S(1)} %fusion.52) | copy-start | bytes 2457604
  155.9 107.8 %all-gather.7.cloned.1.call-start = ((), (), s32[]{:S(2)}) async-start(), calls=%async_computation.6 | async-start | bytes 4259840 | tf_op jit(solution)/shard_map/all_gather | solution.py:984
  156.3 36.0 %copy-start.68 = (bf16[100,800]{1,0:T(8,128)(2,1)S(1)}, bf16[100,800]{1,0:T(8,128)(2,1)}, u32[]{:S(2)}) copy-start(bf16[100,800]{1,0:T(8,128)(2,1)} %reshape.693) | copy-start | bytes 480004
  156.4 36.0 %copy-start.130 = (f32[800]{0:T(1024)S(1)}, f32[800]{0:T(1024)}, u32[]{:S(2)}) copy-start(f32[800]{0:T(1024)} %add.335) | copy-start | bytes 9604
  195.9 131.1 %reduce-scatter.5.cloned.1.call-start = ((), (), s32[]{:S(2)}) async-start(), calls=%async_computation.7 | async-start | bytes 4096000 | tf_op jit(solution)/shard_map/reduce_scatter | solution.py:997
  265.0 132.8 %all-gather.9.cloned.1.call-start = ((), (), s32[]{:S(2)}) async-start(), calls=%async_computation.8 | async-start | bytes 4096000 | tf_op jit(solution)/shard_map/all_gather | solution.py:1009
  272.6 55.8 %copy-start.133 = (f32[256]{0:T(256)}, f32[256]{0:T(256)S(1)}, u32[]{:S(2)}) copy-start(f32[256]{0:T(256)S(1)} %add_rsqrt_fusion.4) | copy-start | bytes 3076
  330.6 175.6 %copy-start.5 = (f32[256,1600]{0,1:T(8,128)}, f32[256,1600]{0,1:T(8,128)S(1)}, u32[]{:S(2)}) copy-start(f32[256,1600]{0,1:T(8,128)S(1)} %get-tuple-element.176) | copy-start | bytes 4915204
  330.6 29.0 %copy-start.131 = (f32[256]{0:T(256)}, f32[256]{0:T(256)S(1)}, u32[]{:S(2)}) copy-start(f32[256]{0:T(256)S(1)} %add_rsqrt_fusion.2) | copy-start | bytes 3076
  332.1 171.5 %reduce-scatter.7.cloned.1.call-start = ((), (), s32[]{:S(2)}) async-start(), calls=%async_computation.9 | async-start | bytes 4096000 | tf_op jit(solution)/shard_map/reduce_scatter | solution.py:1020
  397.8 10.3 %slice-start.4 = ((s8[4505600]{0:T(1024)(128)(4,1)}), s8[311296]{0:T(1024)(128)(4,1)S(1)}, s32[]{:S(2)}) async-start(s8[4505600]{0:T(1024)(128)(4,1)} %bitcast.453), calls=%async_computation.18 | async-start | bytes 622592
  397.8 10.3 %slice-start.5 = ((s8[4505600]{0:T(1024)(128)(4,1)}), s8[4194304]{0:T(1024)(128)(4,1)S(1)}, s32[]{:S(2)}) async-start(s8[4505600]{0:T(1024)(128)(4,1)} %bitcast.453), calls=%async_computation.19 | async-start | bytes 8388608
  397.8 10.3 %copy-start.50 = (bf16[1600,1024]{1,0:T(8,128)(2,1)S(1)}, bf16[1600,1024]{1,0:T(8,128)(2,1)}, u32[]{:S(2)}) copy-start(bf16[1600,1024]{1,0:T(8,128)(2,1)} %tie.14) | copy-start | bytes 9830404
  397.8 30.5 %slice-start.6 = ((s8[4505600]{0:T(1024)(128)(4,1)}), s8[4194304]{0:T(1024)(128)(4,1)S(1)}, s32[]{:S(2)}) async-start(s8[4505600]{0:T(1024)(128)(4,1)} %bitcast.515), calls=%async_computation.20 | async-start | bytes 8388608
  408.0 20.2 %slice-start.7 = ((s8[4505600]{0:T(1024)(128)(4,1)}), s8[311296]{0:T(1024)(128)(4,1)S(1)}, s32[]{:S(2)}) async-start(s8[4505600]{0:T(1024)(128)(4,1)} %bitcast.515), calls=%async_computation.21 | async-start | bytes 622592
  420.9 7.4 copy-start.157
  435.4 155.2 %all-gather.11.cloned.1.call-start = ((), (), s32[]{:S(2)}) async-start(), calls=%async_computation.10 | async-start | bytes 4096000 | tf_op jit(solution)/shard_map/all_gather | solution.py:1034
  487.4 9.3 copy-start.51
  487.4 9.3 copy-start.158
  509.8 6.6 slice-start
  527.6 154.2 %reduce-scatter.9.cloned.1.call-start = ((), (), s32[]{:S(2)}) async-start(), calls=%async_computation.11 | async-start | bytes 4096000 | tf_op jit(solution)/shard_map/reduce_scatter | solution.py:1060
  529.3 7.3 slice-start.2
  600.2 150.3 %all-reduce.13.cloned.1.call-start = ((), (), s32[]{:S(2)}) async-start(), calls=%async_computation.13 | async-start | bytes 3276800 | tf_op jit(solution)/shard_map/psum | solution.py:1092
  681.7 242.6 %reduce-scatter.11.cloned.1.call-start = ((), (), s32[]{:S(2)}) async-start(), calls=%async_computation.12 | async-start | bytes 4096000 | tf_op jit(solution)/shard_map/reduce_scatter | solution.py:1108
  746.0 34.3 %copy-start.65 = (bf16[800,132]{0,1:T(8,128)(2,1)S(1)}, bf16[800,132]{0,1:T(8,128)(2,1)}, u32[]{:S(2)}) copy-start(bf16[800,132]{0,1:T(8,128)(2,1)} %copy-done.64) | copy-start | bytes 633604
  746.0 34.3 %copy-start.136 = (pred[1024]{0:T(1024)(128)(4,1)S(1)}, pred[1024]{0:T(1024)(128)(4,1)}, u32[]{:S(2)}) copy-start(pred[1024]{0:T(1024)(128)(4,1)} %copy-done.135) | copy-start | bytes 3076
  746.1 34.3 %copy-start.138 = (pred[1024]{0:T(1024)(128)(4,1)S(1)}, pred[1024]{0:T(1024)(128)(4,1)}, u32[]{:S(2)}) copy-start(pred[1024]{0:T(1024)(128)(4,1)} %copy-done.137) | copy-start | bytes 3076
  746.1 34.3 %copy-start.140 = (pred[1024]{0:T(1024)(128)(4,1)S(1)}, pred[1024]{0:T(1024)(128)(4,1)}, u32[]{:S(2)}) copy-start(pred[1024]{0:T(1024)(128)(4,1)} %copy-done.139) | copy-start | bytes 3076
  780.3 13.4 %copy-start.60 = (bf16[1024,132]{0,1:T(8,128)(2,1)}, bf16[1024,132]{0,1:T(8,128)(2,1)S(1)}, u32[]{:S(2)}) copy-start(bf16[1024,132]{0,1:T(8,128)(2,1)S(1)} %all-reduce.14) | copy-start | bytes 811012
  822.9 5.8 copy-start.33
  829.9 7.8 copy-start.59
  837.8 6.0 copy-start.41
  838.9 6.4 copy-start.112
  839.0 6.4 copy-start.113
  839.0 6.4 copy-start.146
  839.0 6.5 copy-start.61
  844.1 6.5 copy-start.114
  844.2 6.5 copy-start.115
  844.2 6.5 copy-start.116
  866.8 56.5 %copy-start.6 = (f32[256,1600]{0,1:T(8,128)S(1)}, f32[256,1600]{0,1:T(8,128)}, u32[]{:S(2)}) copy-start(f32[256,1600]{0,1:T(8,128)} %copy-done.5) | copy-start | bytes 4915204
  866.8 56.5 %copy-start.74 = (bf16[256,1600]{0,1:T(8,128)(2,1)S(1)}, bf16[256,1600]{0,1:T(8,128)(2,1)}, u32[]{:S(2)}) copy-start(bf16[256,1600]{0,1:T(8,128)(2,1)} %reduce-scatter.9.cloned.1.call-done) | copy-start | bytes 2457604
  916.2 8.2 copy-start.9
  916.2 8.2 copy-start.122
  (113 other events, 327.8 us)
Sparse Core Ops, SparseCore 0:
  9.6 68.2 all-gather.4
  156.0 36.2 all-reduce.10
  196.0 67.6 all-gather.6
  265.9 61.0 reduce-scatter.4
  332.2 65.5 all-gather.8
  435.5 60.6 reduce-scatter.6
  527.8 62.7 all-gather.10
  600.3 60.6 reduce-scatter.8
  681.9 68.5 all-reduce.12
  818.9 60.5 reduce-scatter.10

commit v3 on v2

--- a/solution.py
+++ b/solution.py
@@ -248,6 +248,7 @@
         sems = pltpu.SemaphoreType.DMA((self.count, 9))
         self.scratch = [sems, sems, pltpu.SemaphoreType.DMA((self.count,))]
         self.sent = sum(math.prod(array.shape) for array in arrays) * 2
+        self.peered = False
         self.results = lambda outs: [out.reshape(-1, out.shape[2]) for out in outs]
 
     def bind(self, ins, outs, scratch):
@@ -298,7 +299,6 @@
             return remote(i, 7 + half, piece, piece, CORE)
 
         def begin():
-            greet()
             for i in range(self.count):
                 for k in range(3):
                     own(i, k).start()
@@ -353,6 +353,7 @@
         self.in_specs = [pl.BlockSpec(memory_space=pl.ANY)] * self.count
         self.out_specs = [pl.BlockSpec(memory_space=pltpu.VMEM)] * len(self.out_shape)
         self.shared = shared
+        self.peered = shared > 0
         vm = pltpu.VMEM
         self.scratch = [vm((4,) + s, LOW) for s in self.sizes] * 1
         self.scratch += [vm((4,) + s, LOW) for s in self.sizes]
@@ -438,7 +439,6 @@
             return remote(i, 9, self.mine[i].at[2 * row + 1 - col, cut(1, i)], self.lasts[i].at[cut(1, i)], FIRST)
 
         def begin():
-            greet(self.shared > 0)
             for i in range(self.count):
                 for k in range(4):
                     cross(i, k).start()
@@ -502,6 +502,72 @@
         return begin, forward, last, finish
 
 
+class Exchange:
+    def __init__(self, part):
+        rows, width = part.shape
+        self.block = rows // 4
+        self.arrays = [part]
+        self.in_specs = [pl.BlockSpec(memory_space=pltpu.VMEM)]
+        self.out_specs = [pl.BlockSpec(memory_space=pltpu.VMEM)]
+        self.out_shape = [jax.ShapeDtypeStruct((rows, width), LOW)]
+        sems = pltpu.SemaphoreType.DMA((6,))
+        self.scratch = [pltpu.VMEM((3, self.block, width), LOW), sems, sems]
+        self.sent = 0
+        self.peered = True
+        self.results = list
+
+    def bind(self, ins, outs, scratch):
+        (self.part,), (self.out,) = ins, outs
+        self.peers, self.send, self.recv = scratch
+
+    def stages(self):
+        place = lax.axis_index("tensor")
+        rows = lambda who: pl.ds(pl.multiple_of(who * self.block, self.block), self.block)
+
+        def copy(turn, k):
+            other = jnp.bitwise_xor(place, k)
+            mine = self.out.at[rows(place)]
+            source, target = (self.part.at[rows(other)], self.peers.at[k - 1]) if turn == 0 else (mine, mine)
+            return pltpu.make_async_remote_copy(
+                src_ref=source,
+                dst_ref=target,
+                send_sem=self.send.at[3 * turn + k - 1],
+                recv_sem=self.recv.at[3 * turn + k - 1],
+                device_id={"tensor": other},
+                device_id_type=MESH_ID,
+            )
+
+        def begin():
+            for k in (2, 3, 1):
+                copy(0, k).start()
+
+        def middle():
+            for k in range(1, 4):
+                copy(0, k).wait_recv()
+
+            def add(n, carry):
+                at = pl.multiple_of(n * 16, 16)
+                here = pl.ds(pl.multiple_of(place * self.block + at, 16), 16)
+                total = self.part[here, :].astype(jnp.float32)
+                for k in range(3):
+                    total = total + self.peers[k, pl.ds(at, 16), :].astype(jnp.float32)
+                self.out[here, :] = total.astype(LOW)
+                return carry
+
+            lax.fori_loop(0, self.block // 16, add, 0)
+            for k in (2, 3, 1):
+                copy(1, k).start()
+
+        def finish():
+            for k in range(1, 4):
+                copy(1, k).wait_recv()
+            for turn in range(2):
+                for k in range(1, 4):
+                    copy(turn, k).wait_send()
+
+        return begin, middle, finish
+
+
 def tie_kernel(*refs):
     pass
 
@@ -518,32 +584,48 @@
     )(value, *others)
 
 
-def comm_kernel(move, n_others, *refs):
-    a = len(move.arrays)
+def comm_kernel(moves, n_others, *refs):
+    a = sum(len(move.arrays) for move in moves)
     b = a + n_others
-    c = b + len(move.out_shape)
-    move.bind(refs[:a], refs[b:c], refs[c:])
-    begin, forward, last, finish = move.stages()
-    begin()
-    for i in range(move.count):
+    c = b + sum(len(move.out_shape) for move in moves)
+    i, o, s = 0, b, c
+    for move in moves:
+        n_in, n_out, n_scr = len(move.arrays), len(move.out_shape), len(move.scratch)
+        move.bind(refs[i : i + n_in], refs[o : o + n_out], refs[s : s + n_scr])
+        i, o, s = i + n_in, o + n_out, s + n_scr
+    stages = [move.stages() for move in moves]
+    greet(any(move.peered for move in moves))
+    for begin, *_ in stages[::-1]:
+        begin()
+    for _, middle, _ in stages[1:]:
+        middle()
+    _, forward, last, finish = stages[0]
+    for i in range(moves[0].count):
         forward(i)
-    for i in range(move.count):
+    for i in range(moves[0].count):
         last(i)
     finish()
-
-
-def comm_call(move, ident, name, others=()):
+    for _, _, end in stages[1:]:
+        end()
+
+
+def comm_call(moves, ident, name, others=()):
     outs = pl.pallas_call(
-        functools.partial(comm_kernel, move, len(others)),
-        out_shape=move.out_shape,
-        in_specs=move.in_specs + [pl.BlockSpec(memory_space=pl.ANY)] * len(others),
-        out_specs=move.out_specs,
-        scratch_shapes=move.scratch,
+        functools.partial(comm_kernel, moves, len(others)),
+        out_shape=[shape for move in moves for shape in move.out_shape],
+        in_specs=[spec for move in moves for spec in move.in_specs] + [pl.BlockSpec(memory_space=pl.ANY)] * len(others),
+        out_specs=[spec for move in moves for spec in move.out_specs],
+        scratch_shapes=[scratch for move in moves for scratch in move.scratch],
         compiler_params=pltpu.CompilerParams(collective_id=ident, has_side_effects=True),
-        cost_estimate=pl.CostEstimate(flops=0, bytes_accessed=100 * move.sent, transcendentals=0),
+        cost_estimate=pl.CostEstimate(flops=0, bytes_accessed=100 * sum(move.sent for move in moves), transcendentals=0),
         name=f"{name}_{ident}",
-    )(*move.arrays, *others)
-    return move.results(outs)
+    )(*[array for move in moves for array in move.arrays], *others)
+    results, start = [], 0
+    for move in moves:
+        count = len(move.out_shape)
+        results.append(move.results(outs[start : start + count]))
+        start += count
+    return results
 
 
 def product_kernel(former_ref, latter_ref, out_ref):
@@ -564,6 +646,70 @@
     )(former, latter)
 
 
+def conv_back_kernel(taps_at, part_ref, proj_ref, xproj_ref, mamba_ref, reach_ref, vec_ref, gin_ref, gtaps_ref, gxproj_ref):
+    length, width = mamba_ref.shape
+    taps = CONV
+
+    @pl.when(pl.program_id(0) == 0)
+    def _():
+        gtaps_ref[...] = jnp.zeros_like(gtaps_ref)
+        gxproj_ref[...] = jnp.zeros_like(gxproj_ref)
+
+    reach = reach_ref[...]
+    proj = proj_ref[...]
+    for at in range(0, width, 256):
+        lanes = pl.ds(at, min(256, width - at))
+        tap = lambda k: vec_ref[pl.ds(taps_at + k, 1), lanes]
+        rows = mamba_ref[:, lanes]
+        conv = tap(taps) + tap(0) * rows
+        lagged = []
+        for k in range(1, taps):
+            lagged.append(jnp.where(reach >= k, pltpu.roll(rows, k, 0), 0.0))
+            conv = conv + tap(k) * lagged[-1]
+        sig = sigmoid(conv)
+        feed_low = (conv * sig).astype(LOW)
+        weight = xproj_ref[lanes, :]
+        back = part_ref[:, lanes] + lax.dot_general(
+            proj, weight, (((1,), (1,)), ((), ())), preferred_element_type=jnp.float32
+        )
+        back = back * (sig * (1.0 + conv * (1.0 - sig)))
+        total = tap(0) * back
+        grads = [jnp.sum(back * rows, axis=0, keepdims=True)]
+        for k in range(1, taps):
+            grads.append(jnp.sum(back * lagged[k - 1], axis=0, keepdims=True))
+            total = total + tap(k) * pltpu.roll(jnp.where(reach >= k, back, 0.0), length - k, 0)
+        grads.append(jnp.sum(back, axis=0, keepdims=True))
+        for k, grad in enumerate(grads):
+            gtaps_ref[pl.ds(k, 1), lanes] += grad
+        gin_ref[:, lanes] = total.astype(gin_ref.dtype)
+        gxproj_ref[lanes, :] += lax.dot_general(
+            feed_low, proj, (((0,), (0,)), ((), ())), preferred_element_type=jnp.float32
+        )
+
+
+def conv_back(part, proj, xproj, mamba, reach, vectors, taps_at, seq_len):
+    rows, width = mamba.shape
+    wide = pl.BlockSpec((seq_len, width), lambda s: (s, 0))
+    fixed = lambda array: pl.BlockSpec(array.shape, lambda s: (0, 0))
+    shape = jax.ShapeDtypeStruct
+    return pl.pallas_call(
+        functools.partial(conv_back_kernel, taps_at),
+        grid=(rows // seq_len,),
+        in_specs=[
+            wide,
+            pl.BlockSpec((seq_len, proj.shape[1]), lambda s: (s, 0)),
+            fixed(xproj),
+            wide,
+            pl.BlockSpec((seq_len, 1), lambda s: (s, 0)),
+            fixed(vectors),
+        ],
+        out_specs=[wide, pl.BlockSpec((8, width), lambda s: (0, 0)), fixed(xproj)],
+        out_shape=[shape((rows, width), LOW), shape((8, width), jnp.float32), shape(xproj.shape, jnp.float32)],
+        cost_estimate=pl.CostEstimate(flops=0, bytes_accessed=40_000_000, transcendentals=0),
+        name="conv_backward",
+    )(part, proj, xproj, mamba, reach, vectors)
+
+
 def softplus(v):
     return jnp.maximum(v, 0.0) + jnp.log1p(jnp.exp(-jnp.abs(v)))
 
@@ -572,29 +718,59 @@
     return 1.0 / (1.0 + jnp.exp(-v))
 
 
-def scan_fwd_body(feed_ref, sraw_ref, gate_ref, keep_ref, b_ref, c_ref, rate_ref, skip_ref, low_ref, comb_ref, starts_ref, h_scr, y_scr):
+WIDE = 128
+def lane_chunks(width):
+    return [(at, min(WIDE, width - at)) for at in range(0, width, WIDE)]
+
+def spread_columns(mat, out_ref):
+    for j in range(BLK):
+        out_ref[j] = jnp.broadcast_to(mat[:, j:j+1], out_ref.shape[1:])
+
+def tile_to(mat, width):
+    if width <= 128:
+        return mat[:, :width]
+    return jnp.concatenate([mat] * (width // 128), axis=1)
+
+def step_inputs(proj_ref, dtproj_ref, dtb_ref):
+    ranks = dtproj_ref.shape[0]
+    sraw = jnp.dot(proj_ref[:, :ranks], dtproj_ref[...], preferred_element_type=jnp.float32)
+    return sraw + dtb_ref[...]
+
+
+def scan_columns(proj_ref, rows, states):
+    tail = proj_ref[rows, :].astype(jnp.float32)[:, proj_ref.shape[1] - 2 * states :]
+    turned = tail.T
+    return turned[:states], turned[states:]
+
+
+def scan_fwd_body(feed_ref, proj_ref, gate_ref, keep_ref, dtproj_ref, dtb_ref, rate_ref, skip_ref, low_ref, comb_ref, starts_ref, h_scr, y_scr, reach_scr, drive_scr, sraw_scr, b_scr, c_scr):
     blocks = feed_ref.shape[0] // BLK
-    rate2 = rate_ref[...] * LOG2E
 
     @pl.when(pl.program_id(1) == 0)
     def _():
         h_scr[...] = jnp.zeros_like(h_scr)
 
+    sraw_scr[...] = step_inputs(proj_ref, dtproj_ref, dtb_ref)
+
     def body(n, carry):
         rows = pl.ds(pl.multiple_of(n * BLK, BLK), BLK)
         feed = feed_ref[rows, :]
-        step = softplus(sraw_ref[rows, :])
-        reach = jnp.where(keep_ref[rows, :] > 0.0, step, FAR)
-        drive = step * feed
-        bm = b_ref[0, n]
-        cm = c_ref[0, n]
-        h = h_scr[...]
-        starts_ref[0, n] = h
-        for j in range(BLK):
-            a = jnp.exp2(reach[j : j + 1, :] * rate2)
-            h = a * h + drive[j : j + 1, :] * bm[:, j : j + 1]
-            y_scr[j : j + 1, :] = jnp.sum(h * cm[:, j : j + 1], axis=0, keepdims=True)
-        h_scr[...] = h
+        step = softplus(sraw_scr[rows, :])
+        reach_scr[...] = jnp.where(keep_ref[rows, :] > 0.0, step, FAR)
+        drive_scr[...] = step * feed
+        bm, cm = scan_columns(proj_ref, rows, rate_ref.shape[0])
+        spread_columns(bm, b_scr)
+        spread_columns(cm, c_scr)
+        starts_ref[0, n] = h_scr[...]
+        for at, size in lane_chunks(feed_ref.shape[1]):
+            lanes = pl.ds(at, size)
+            rate2 = rate_ref[:, lanes] * LOG2E
+            h = h_scr[:, lanes]
+            for j in range(BLK):
+                a = jnp.exp2(reach_scr[pl.ds(j, 1), lanes] * rate2)
+                h = a * h + drive_scr[pl.ds(j, 1), lanes] * tile_to(b_scr[j], size)
+                y_scr[pl.ds(j, 1), lanes] = jnp.sum(h * tile_to(c_scr[j], size), axis=0, keepdims=True)
+            h_scr[:, lanes] = h
         combined = y_scr[...] + skip_ref[...] * feed
         comb_ref[rows, :] = combined
         gate = gate_ref[rows, :]
@@ -605,14 +781,14 @@
 
 
 def scan_bwd_body(
-    gg_ref, gate_ref, comb_ref, feed_ref, sraw_ref, keep_ref, b_ref, c_ref, starts_ref, rate_ref, skip_ref,
-    ggate_ref, gfeed_ref, gstep_ref, db_ref, dc_ref, drate_ref, dskip_ref, dbias_ref,
-    dh_scr, h_scr, a_scr, du_scr, ds_scr,
+    gg_ref, gate_ref, comb_ref, feed_ref, proj_ref, keep_ref, starts_ref, dtproj_ref, dtb_ref, rate_ref, skip_ref,
+    ggate_ref, gfeed_ref, gstep_ref, gproj_ref, drate_ref, dskip_ref, dbias_ref,
+    dh_scr, h_scr, a_scr, du_scr, ds_scr, step_scr, reach_scr, drive_scr, gcomb_scr, sraw_scr, mats_scr, b_scr, c_scr, db_scr, dc_scr,
 ):
     blocks = feed_ref.shape[0] // BLK
-    rate = rate_ref[...]
-    rate2 = rate * LOG2E
-    lane = lax.broadcasted_iota(jnp.int32, (b_ref.shape[2], BLK), 1)
+    states = rate_ref.shape[0]
+    lane = lax.broadcasted_iota(jnp.int32, (2 * states, BLK), 1)
+    sraw_scr[...] = step_inputs(proj_ref, dtproj_ref, dtb_ref)
 
     @pl.when((pl.program_id(0) == 0) & (pl.program_id(1) == 0))
     def _():
@@ -628,66 +804,103 @@
         n = blocks - 1 - i
         rows = pl.ds(pl.multiple_of(n * BLK, BLK), BLK)
         feed = feed_ref[rows, :]
-        sraw = sraw_ref[rows, :]
-        step = softplus(sraw)
-        reach = jnp.where(keep_ref[rows, :] > 0.0, step, FAR)
-        drive = step * feed
+        step = softplus(sraw_scr[rows, :])
+        step_scr[...] = step
+        reach_scr[...] = jnp.where(keep_ref[rows, :] > 0.0, step, FAR)
+        drive_scr[...] = step * feed
         gate = gate_ref[rows, :]
         sig = sigmoid(gate)
         gg = gg_ref[rows, :]
         gcomb = gg * (gate * sig)
+        gcomb_scr[...] = gcomb
         ggate_ref[rows, :] = (gg * comb_ref[rows, :] * (sig * (1.0 + gate * (1.0 - sig)))).astype(ggate_ref.dtype)
         dskip_ref[...] += jnp.sum(gcomb * feed, axis=0, keepdims=True)
-        bm = b_ref[0, n]
-        cm = c_ref[0, n]
-        h = starts_ref[0, n]
+        bm, cm = scan_columns(proj_ref, rows, rate_ref.shape[0])
+        spread_columns(bm, b_scr)
+        spread_columns(cm, c_scr)
+        def fold(v):
+            w = v.shape[1]
+            if w <= 128:
+                return v if w == 128 else jnp.pad(v, ((0, 0), (0, 128 - w)))
+            return sum(v[:, k * 128:(k + 1) * 128] for k in range(w // 128))
+        for index, (at, size) in enumerate(lane_chunks(feed_ref.shape[1])):
+            lanes = pl.ds(at, size)
+            rate = rate_ref[:, lanes]
+            rate2 = rate * LOG2E
+            h = starts_ref[0, n, :, lanes]
+            for j in range(BLK):
+                h_scr[j, :, pl.ds(0, size)] = h
+                a = jnp.exp2(reach_scr[pl.ds(j, 1), lanes] * rate2)
+                a_scr[j, :, pl.ds(0, size)] = a
+                h = a * h + drive_scr[pl.ds(j, 1), lanes] * tile_to(b_scr[j], size)
+            dh = dh_scr[:, lanes]
+            drate = drate_ref[:, lanes]
+            for j in reversed(range(BLK)):
+                gy = gcomb_scr[pl.ds(j, 1), lanes]
+                dh = dh + tile_to(c_scr[j], size) * gy
+                dc = fold(gy * h)
+                db = fold(dh * drive_scr[pl.ds(j, 1), lanes])
+                if index == 0:
+                    dc_scr[j], db_scr[j] = dc, db
+                else:
+                    dc_scr[j] += dc
+                    db_scr[j] += db
+                du_scr[pl.ds(j, 1), lanes] = jnp.sum(dh * tile_to(b_scr[j], size), axis=0, keepdims=True)
+                dh = dh * a_scr[j, :, pl.ds(0, size)]
+                h = h_scr[j, :, pl.ds(0, size)]
+                thru = dh * h
+                ds_scr[pl.ds(j, 1), lanes] = jnp.sum(thru * rate, axis=0, keepdims=True)
+                drate = drate + thru * step_scr[pl.ds(j, 1), lanes]
+            dh_scr[:, lanes] = dh
+            drate_ref[:, lanes] = drate
+        mats = jnp.zeros(lane.shape, jnp.float32)
         for j in range(BLK):
-            h_scr[j] = h
-            a = jnp.exp2(reach[j : j + 1, :] * rate2)
-            a_scr[j] = a
-            h = a * h + drive[j : j + 1, :] * bm[:, j : j + 1]
-        dh = dh_scr[...]
-        drate = drate_ref[...]
-        dbm = jnp.zeros(bm.shape, jnp.float32)
-        dcm = jnp.zeros(bm.shape, jnp.float32)
-        for j in reversed(range(BLK)):
-            gy = gcomb[j : j + 1, :]
-            dh = dh + cm[:, j : j + 1] * gy
-            dcm = jnp.where(lane == j, jnp.sum(gy * h, axis=1, keepdims=True), dcm)
-            dbm = jnp.where(lane == j, jnp.sum(dh * drive[j : j + 1, :], axis=1, keepdims=True), dbm)
-            du_scr[j : j + 1, :] = jnp.sum(dh * bm[:, j : j + 1], axis=0, keepdims=True)
-            dh = dh * a_scr[j]
-            h = h_scr[j]
-            thru = dh * h
-            ds_scr[j : j + 1, :] = jnp.sum(thru * rate, axis=0, keepdims=True)
-            drate = drate + thru * step[j : j + 1, :]
-        dh_scr[...] = dh
-        drate_ref[...] = drate
-        db_ref[0, n] = dbm
-        dc_ref[0, n] = dcm
+            both = jnp.concatenate([db_scr[j], dc_scr[j]], axis=0)
+            mats = jnp.where(lane == j, jnp.sum(both, axis=1, keepdims=True), mats)
+        mats_scr[rows, :] = mats.T
         du = du_scr[...]
-        gfeed_ref[rows, :] = gcomb * skip_ref[...] + du * step
-        gsraw = (du * feed + ds_scr[...]) * sigmoid(sraw)
+        gfeed_ref[rows, :] = gcomb_scr[...] * skip_ref[...] + du * step_scr[...]
+        gsraw = (du * feed_ref[rows, :] + ds_scr[...]) * sigmoid(sraw_scr[rows, :])
         dbias_ref[...] += jnp.sum(gsraw, axis=0, keepdims=True)
         gstep_ref[rows, :] = gsraw.astype(gstep_ref.dtype)
         return carry
 
     lax.fori_loop(0, blocks, body, 0)
-
-
-def fused_kernel(body, n_in, n_prior, n_out, n_scr, move, plan, *refs):
+    ranks = lax.dot_general(
+        gstep_ref[...], dtproj_ref[...], (((1,), (1,)), ((), ())), preferred_element_type=jnp.float32
+    )
+    gproj_ref[...] = jnp.concatenate([ranks, mats_scr[...]], axis=1).astype(gproj_ref.dtype)
+
+def fwd_scratch(states, width, chunk):
+    vm = lambda *shape: pltpu.VMEM(shape, jnp.float32)
+    return [vm(states, width)] + [vm(BLK, width)] * 3 + [vm(chunk, width)] + [vm(BLK, states, 128)] * 2
+
+
+def bwd_scratch(states, width, chunk):
+    vm = lambda *shape: pltpu.VMEM(shape, jnp.float32)
+    return (
+        [vm(states, width)]
+        + [vm(BLK, states, WIDE)] * 2
+        + [vm(BLK, width)] * 6
+        + [vm(chunk, width), vm(chunk, 2 * states)]
+        + [vm(BLK, states, 128)] * 4
+    )
+
+
+def fused_kernel(body, n_in, n_others, n_out, n_scr, move, plan, *refs):
     m_in, m_out = (len(move.arrays), len(move.out_shape)) if move else (0, 0)
-    a = n_in + n_prior + m_in
+    a = n_in + n_others + m_in
     b = a + n_out + m_out
     ins, outs, scr = refs[:n_in], refs[a : a + n_out], refs[b : b + n_scr]
     if move:
-        move.bind(refs[n_in + n_prior : a], refs[a + n_out : b], refs[b + n_scr :])
+        move.bind(refs[n_in + n_others : a], refs[a + n_out : b], refs[b + n_scr :])
         begin, forward, last, finish = move.stages()
         step = pl.program_id(0) * pl.num_programs(1) + pl.program_id(1)
         for at, acts in plan(move.count):
             def run(acts=acts):
                 for act, i in acts:
                     if act == "begin":
+                        greet(move.peered)
                         begin()
                     elif act == "forward":
                         forward(i)
@@ -700,24 +913,20 @@
         pl.when(step == pl.num_programs(0) * pl.num_programs(1) - 1)(finish)
 
 
-def scan_pieces(width, states, seq_len, chunk, back, base):
+def scan_pieces(width, states, seq_len, chunk, back):
     pieces = seq_len // chunk
     turn = (lambda t: pieces - 1 - t) if back else (lambda t: t)
-    wide = pl.BlockSpec((chunk, width), lambda s, t: ((s + base) * pieces + turn(t), 0))
-    keep = pl.BlockSpec((chunk, 1), lambda s, t: ((s + base) * pieces + turn(t), 0))
-    cols = pl.BlockSpec((1, chunk // BLK, states, BLK), lambda s, t: (s + base, turn(t), 0, 0))
-    starts = pl.BlockSpec((1, chunk // BLK, states, width), lambda s, t: (s + base, turn(t), 0, 0))
-    par = pl.BlockSpec((states, width), lambda s, t: (0, 0))
-    row = pl.BlockSpec((1, width), lambda s, t: (0, 0))
-    return wide, keep, cols, starts, par, row
-
-
-def fused_call(body, operands, in_specs, out_specs, out_shape, scratch, grid, move, plan, ident, name, prior=(), others=()):
+    rows = lambda columns: pl.BlockSpec((chunk, columns), lambda s, t: (s * pieces + turn(t), 0))
+    starts = pl.BlockSpec((1, chunk // BLK, states, width), lambda s, t: (s, turn(t), 0, 0))
+    fixed = lambda height: pl.BlockSpec((height, width), lambda s, t: (0, 0))
+    return rows, starts, fixed
+
+
+def fused_call(body, operands, in_specs, out_specs, out_shape, scratch, grid, move, plan, ident, name, others=()):
     n_in, n_out, n_scr = len(in_specs), len(out_specs), len(scratch)
     params = {}
-    aliases = {n_in + k: k for k in range(len(prior))}
-    operands = list(operands) + list(prior) + list(others)
-    in_specs = in_specs + [pl.BlockSpec(memory_space=pl.ANY)] * (len(prior) + len(others))
+    operands = list(operands) + list(others)
+    in_specs = in_specs + [pl.BlockSpec(memory_space=pl.ANY)] * len(others)
     if move:
         operands = operands + list(move.arrays)
         in_specs = in_specs + move.in_specs
@@ -726,13 +935,12 @@
         scratch = scratch + move.scratch
         params = dict(collective_id=ident, has_side_effects=True)
     outs = pl.pallas_call(
-        functools.partial(fused_kernel, body, n_in, len(prior) + len(others), n_out, n_scr, move, plan),
+        functools.partial(fused_kernel, body, n_in, len(others), n_out, n_scr, move, plan),
         grid=grid,
         in_specs=in_specs,
         out_specs=out_specs,
         out_shape=out_shape,
         scratch_shapes=scratch,
-        input_output_aliases=aliases,
         compiler_params=pltpu.CompilerParams(**params),
         cost_estimate=pl.CostEstimate(flops=0, bytes_accessed=150_000_000, transcendentals=0),
         name=name,
@@ -740,78 +948,63 @@
     return outs[:n_out], (move.results(outs[n_out:]) if move else None)
 
 
-def scan_fwd(feed, sraw, gate, keep, bcols, ccols, rate, skip, seq_len, move=None, plan=None, ident=None, chunk=128):
-    rows, width = feed.shape
-    seqs, states, nb = rows // seq_len, rate.shape[0], seq_len // BLK
-    wide, keeps, cols, starts, par, row = scan_pieces(width, states, seq_len, chunk, False, 0)
-    f32 = jnp.float32
+def scan_fwd(feed, proj, gate, keep, dtproj, dtb, rate, skip, seq_len, others=(), move=None, plan=None, ident=None, chunk=128):
+    height, width = feed.shape
+    seqs, states, nb = height // seq_len, rate.shape[0], seq_len // BLK
+    rows, starts, fixed = scan_pieces(width, states, seq_len, chunk, False)
+    wide = rows(width)
+    shape = jax.ShapeDtypeStruct
     return fused_call(
         scan_fwd_body,
-        (feed, sraw, gate, keep, bcols, ccols, rate, skip),
-        [wide, wide, wide, keeps, cols, cols, par, row],
+        (feed, proj, gate, keep, dtproj, dtb, rate, skip),
+        [wide, rows(proj.shape[1]), wide, rows(1), fixed(dtproj.shape[0]), fixed(1), fixed(states), fixed(1)],
         [wide, wide, starts],
         [
-            jax.ShapeDtypeStruct((rows, width), LOW),
-            jax.ShapeDtypeStruct((rows, width), f32),
-            jax.ShapeDtypeStruct((seqs, nb, states, width), f32),
+            shape((height, width), LOW),
+            shape((height, width), jnp.float32),
+            shape((seqs, nb, states, width), jnp.float32),
         ],
-        [pltpu.VMEM((states, width), f32), pltpu.VMEM((BLK, width), f32)],
+        fwd_scratch(states, width, chunk),
         (seqs, seq_len // chunk),
         move,
         plan,
         ident,
         "scan_forward",
+        others,
     )
 
 
 def scan_bwd(
-    gg, gate, comb, feed, sraw, keep, bcols, ccols, starts, rate, skip, seq_len,
-    part=0, parts=1, prior=(), others=(), move=None, plan=None, ident=None, chunk=128,
+    gg, gate, comb, feed, proj, keep, starts, dtproj, dtb, rate, skip, seq_len,
+    others=(), move=None, plan=None, ident=None, chunk=128,
 ):
-    rows, width = feed.shape
-    seqs, states, nb = rows // seq_len, rate.shape[0], seq_len // BLK
-    wide, keeps, cols, startb, par, row = scan_pieces(width, states, seq_len, chunk, True, part * (seqs // parts))
-    f32 = jnp.float32
+    height, width = feed.shape
+    seqs, states = height // seq_len, rate.shape[0]
+    rows, startb, fixed = scan_pieces(width, states, seq_len, chunk, True)
+    wide, narrow = rows(width), rows(proj.shape[1])
     shape = jax.ShapeDtypeStruct
     return fused_call(
         scan_bwd_body,
-        (gg, gate, comb, feed, sraw, keep, bcols, ccols, starts, rate, skip),
-        [wide, wide, wide, wide, wide, keeps, cols, cols, startb, par, row],
-        [wide, wide, wide, cols, cols, par, row, row],
+        (gg, gate, comb, feed, proj, keep, starts, dtproj, dtb, rate, skip),
+        [wide, wide, wide, wide, narrow, rows(1), startb, fixed(dtproj.shape[0]), fixed(1), fixed(states), fixed(1)],
+        [wide, wide, wide, narrow, fixed(states), fixed(1), fixed(1)],
         [
-            shape((rows, width), LOW),
-            shape((rows, width), f32),
-            shape((rows, width), LOW),
-            shape((seqs, nb, states, BLK), f32),
-            shape((seqs, nb, states, BLK), f32),
-            shape((states, width), f32),
-            shape((1, width), f32),
-            shape((1, width), f32),
+            shape((height, width), LOW),
+            shape((height, width), jnp.float32),
+            shape((height, width), LOW),
+            shape(proj.shape, LOW),
+            shape((states, width), jnp.float32),
+            shape((1, width), jnp.float32),
+            shape((1, width), jnp.float32),
         ],
-        [
-            pltpu.VMEM((states, width), f32),
-            pltpu.VMEM((BLK, states, width), f32),
-            pltpu.VMEM((BLK, states, width), f32),
-            pltpu.VMEM((BLK, width), f32),
-            pltpu.VMEM((BLK, width), f32),
-        ],
-        (seqs // parts, seq_len // chunk),
+        bwd_scratch(states, width, chunk),
+        (seqs, seq_len // chunk),
         move,
         plan,
         ident,
         "scan_backward",
-        prior,
         others,
     )
-
-
-def to_cols(mat, seq_len):
-    rows, states = mat.shape
-    return jnp.swapaxes(mat.reshape(rows // seq_len, seq_len // BLK, BLK, states), 2, 3)
-
-
-def from_cols(cols):
-    return jnp.swapaxes(cols, 2, 3).reshape(-1, cols.shape[2])
 
 
 def lag_masks(segments):
@@ -831,25 +1024,13 @@
     return totals
 
 
-def causal_conv_grad(cotangent, mamba_in, conv_taps, masks):
-    back_input = conv_taps[0][None] * cotangent
-    tap_grads = [jnp.sum(cotangent * mamba_in, axis=0)]
-    for lag in range(1, CONV):
-        masked = jnp.where(masks[lag - 1], cotangent, 0.0)
-        padding = jnp.zeros((lag, mamba_in.shape[1]), mamba_in.dtype)
-        lagged = jnp.concatenate([padding, mamba_in[:-lag]])
-        tap_grads.append(jnp.sum(masked * lagged, axis=0))
-        back_input = back_input + conv_taps[lag][None] * jnp.concatenate([masked[lag:], padding])
-    return back_input, jnp.stack(tap_grads), jnp.sum(cotangent, axis=0)
-
-
 def fits():
     return lax.axis_size("dp") == 8 and lax.axis_size("tensor") == 4
 
 
 def gather_rows(shards, ident, *others):
     if fits():
-        return comm_call(Gather(shards), ident, "gather", others)
+        return comm_call([Gather(shards)], ident, "gather", others)[0]
     planes = [plane for shard in shards for plane in ([shard] if shard.ndim == 2 else list(shard))]
     return [lax.all_gather(plane, "dp", axis=0, tiled=True) for plane in planes]
 
@@ -867,9 +1048,9 @@
     return results
 
 
-def scatter_rows(groups, ident, shared=0):
+def scatter_rows(groups, ident, *others, shared=0):
     if fits():
-        return comm_call(Scatter(groups, shared), ident, "scatter")
+        return comm_call([Scatter(groups, shared)], ident, "scatter", others)[0]
     return scatter_plain(groups, shared)
 
 
@@ -888,10 +1069,8 @@
 
 
 def scatter_plan(count):
-    return [
-        (0, [("begin", 0)]),
-        (1, [("forward", i) for i in range(count)]),
-        (3, [("last", i) for i in range(count)]),
+    return [(0, [("begin", 0)]), (1, [("forward", i) for i in range(count)])] + [
+        (min(3 + i, 7), [("last", i)]) for i in range(count)
     ]
 
 
@@ -961,33 +1140,35 @@
     allowed = segment_mask(own_segments)
 
     masks = lag_masks(segment_ids)
-    keep_state = masks[0].astype(jnp.float32)
+    keep_state = sum(mask.astype(jnp.float32) for mask in masks)
     mamba_in = plain_dot(normed_all, in_first)
     gate_raw = plain_dot(normed_all, in_second)
     conv_raw = causal_conv(mamba_in, conv_taps, conv_shift, masks)
     feed_rows = jax.nn.silu(conv_raw)
     feed_low = feed_rows.astype(jnp.bfloat16)
-    projected_part = plain_dot(feed_low, xproj_weight)
-    projected = lax.psum(projected_part, "tensor")
-    query_weight, key_weight, value_weight = gather_rows((w_query, w_keyval), 2, edge(projected_part))
+    projected_part = plain_dot(feed_low, xproj_weight).astype(LOW)
+    if fits():
+        (query_weight, key_weight, value_weight), (projected,) = comm_call(
+            [Gather((w_query, w_keyval)), Exchange(projected_part)], 2, "gather"
+        )
+    else:
+        query_weight, key_weight, value_weight = gather_rows((w_query, w_keyval), 2)
+        projected = lax.psum(projected_part, "tensor")
 
     query_low, key_low, value_low, meta_keys, meta_values = attention_inputs(
         normed_low, meta_low, query_weight, key_weight, value_weight, cosine_table, sine_table
     )
     attended, log_total = attention_forward(query_low, key_low, value_low, meta_keys, meta_values, allowed)
 
-    projected = hold(projected, edge(attended), edge(gate_raw))
-    rank_low = projected[:, :DTR].astype(jnp.bfloat16)
-    step_raw = plain_dot(rank_low, dtproj_weight) + dt_shift
-    input_cols = to_cols(projected[:, DTR : DTR + STATE], SEQ_LEN)
-    output_cols = to_cols(projected[:, DTR + STATE :], SEQ_LEN)
-    grad_all = lax.all_gather(tie(out_grad, step_raw), "tensor", axis=0, tiled=True)
+    grad_all = lax.all_gather(tie(out_grad, projected), "tensor", axis=0, tiled=True)
     scan_args = (
-        feed_rows, step_raw, gate_raw, keep_state, input_cols, output_cols, decay_rate, skip_weight[None], SEQ_LEN
+        feed_rows, projected, gate_raw, keep_state, dtproj_weight, dt_shift[None], decay_rate, skip_weight[None], SEQ_LEN
     )
     out_shards = (w_output, out_proj.T)
     if fits():
-        (mamba_low, combined, starts), moved = scan_fwd(*scan_args, move=Gather(out_shards), plan=gather_plan, ident=3)
+        (mamba_low, combined, starts), moved = scan_fwd(
+            *scan_args, move=Gather(out_shards), plan=gather_plan, ident=3
+        )
     else:
         (mamba_low, combined, starts), _ = scan_fwd(*scan_args)
         moved = gather_rows(out_shards, 3)
@@ -995,7 +1176,7 @@
     mamba_part = contract_cols(mamba_low, out_turned).astype(jnp.bfloat16)
     mamba_part = hold(mamba_part, edge(grad_all))
     mamba_out = lax.psum_scatter(mamba_part, "tensor", scatter_dimension=0, tiled=True)
-    gate_weight, up_weight = gather_rows((gate_up,), 4, edge(mamba_part))
+    (gate_weight,) = gather_rows((gate_up[0],), 4, edge(mamba_part))
     attn_out = plain_dot(attended, output_weight)
     mamba_out = hold(mamba_out, gate_weight, edge(attn_out)).astype(jnp.float32)
     attn_scale = inverse_rms(attn_out)
@@ -1007,7 +1188,7 @@
     normed_two = mixed_rows * scale_two
     ffn_low = (normed_two * gain_rows[3]).astype(jnp.bfloat16)
     ffn_all = lax.all_gather(ffn_low, "tensor", axis=0, tiled=True)
-    (down_turned,) = gather_rows((w_down.T,), 5, edge(ffn_low))
+    up_weight, down_turned = gather_rows((gate_up[1], w_down.T), 5, edge(ffn_low))
     g_hidden = plain_dot(grad_all, down_turned)
     ffn_all = hold(ffn_all, edge(g_hidden))
     gate_pre = plain_dot(ffn_all, gate_weight)
@@ -1055,58 +1236,53 @@
     key_side = contract_cols(g_key_low, key_weight) + contract_cols(g_value_low, value_weight)
     attention_side = query_side + key_side
     g_key, g_value = g_key.astype(jnp.bfloat16), g_value.astype(jnp.bfloat16)
-    g_mamba_all = hold(g_mamba_all, g_query, g_output, g_key, g_value, edge(attention_side))
+    (r_up,) = scatter_rows(([d_up],), 10, edge(g_mamba_low))
+    g_mamba_all = hold(g_mamba_all, g_query, g_output, g_key, g_value, edge(attention_side), r_up)
     g_gated = plain_dot(g_mamba_all, out_turned)
     ffn_out = lax.psum_scatter(hold(ffn_part, g_gated), "tensor", scatter_dimension=0, tiled=True)
     block_out = (mixed_rows + ffn_out.astype(jnp.float32)).astype(jnp.bfloat16)
     attention_groups = ([g_query], [g_output], [g_key, g_value])
-    ffn_groups = ([d_gate, d_up],)
     scan_args = (
         g_gated,
         gate_raw,
         combined,
         feed_rows,
-        step_raw,
+        projected,
         keep_state,
-        input_cols,
-        output_cols,
         starts,
+        dtproj_weight,
+        dt_shift[None],
         decay_rate,
         skip_weight[None],
         SEQ_LEN,
     )
+    moved_groups = attention_groups + ([d_gate],)
     if fits():
-        first, attention_shares = scan_bwd(
-            *scan_args, part=0, parts=2, move=Scatter(attention_groups), plan=scatter_plan, ident=7
+        scanned, moved = scan_bwd(*scan_args, move=Scatter(moved_groups), plan=scatter_plan, ident=7)
+    else:
+        scanned, _ = scan_bwd(*scan_args)
+        moved = scatter_plain(moved_groups)
+    g_gate_raw_low, g_feed_part, g_step_low, g_projected, g_rate, g_skip, g_dt_shift = scanned
+    s_query, s_output, s_keyval = lax.psum(tuple(item.astype(jnp.bfloat16) for item in moved[:3]), "tensor")
+    r_gate = moved[3]
+    rank_low = projected[:, :DTR]
+    g_out = product(g_mamba_all.T, mamba_low)
+    g_dtproj = low_rows(g_step_low, rank_low)
+    d_second = product(normed_all.T, g_gate_raw_low)
+    if fits():
+        (r_second, r_out), (g_projected_low,) = comm_call(
+            [Scatter(([d_second], [g_out])), Exchange(g_projected)], 11, "scatter", (edge(ffn_out),)
         )
-        second, ffn_shares = scan_bwd(
-            *scan_args, part=1, parts=2, prior=first[:5], others=(edge(ffn_out),), move=Scatter(ffn_groups), plan=scatter_plan, ident=8
-        )
-        g_gate_raw_low, g_feed_part, g_step_low, g_input_cols, g_output_cols = second[:5]
-        g_rate, g_skip, g_dt_shift = [former + latter for former, latter in zip(first[5:], second[5:])]
     else:
-        (g_gate_raw_low, g_feed_part, g_step_low, g_input_cols, g_output_cols, g_rate, g_skip, g_dt_shift), _ = scan_bwd(
-            *scan_args
-        )
-        attention_shares, ffn_shares = scatter_plain(attention_groups), scatter_plain(ffn_groups)
-    s_query, s_output, s_keyval = lax.psum(tuple(item.astype(jnp.bfloat16) for item in attention_shares), "tensor")
-    (r_gateup,) = ffn_shares
-    g_projected = jnp.concatenate(
-        [contract_cols(g_step_low, dtproj_weight), from_cols(g_input_cols), from_cols(g_output_cols)], axis=1
-    )
-    g_projected = lax.psum(hold(g_projected, s_query), "tensor")
-    g_dtproj = low_rows(g_step_low, rank_low)
-    g_out = product(g_mamba_all.T, mamba_low)
-    g_projected_low = g_projected.astype(jnp.bfloat16)
-    g_feed = g_feed_part + contract_cols(g_projected_low, xproj_weight)
-    g_conv_raw = g_feed * swish_slope(conv_raw)
-    g_mamba_in, g_conv_taps, g_conv_shift = causal_conv_grad(g_conv_raw, mamba_in, conv_taps, masks)
-    g_in_low = g_mamba_in.astype(jnp.bfloat16)
+        r_second, r_out = scatter_plain(([d_second], [g_out]))
+        g_projected_low = lax.psum(g_projected, "tensor")
+    g_in_low, g_taps, g_xproj = conv_back(
+        g_feed_part, g_projected_low, xproj_weight, mamba_in, keep_state, vectors, states, SEQ_LEN
+    )
     g_normed_part = contract_cols(g_in_low, in_first) + contract_cols(g_gate_raw_low, in_second)
     g_gain_in = jnp.sum(g_normed_part * (residual_all * scale_all), axis=0)
     g_normed_part = g_normed_part.astype(jnp.bfloat16)
     g_normed = lax.psum_scatter(g_normed_part, "tensor", scatter_dimension=0, tiled=True)
-    g_xproj = low_rows(feed_low, g_projected_low)
     key_float = key_weight.astype(jnp.float32)
     value_float = value_weight.astype(jnp.float32)
     g_meta_normed = contract_cols_exact(g_meta_key, key_float) + contract_cols_exact(g_meta_value, value_float)
@@ -1116,25 +1292,26 @@
     g_meta = norm_backward(g_meta_normed * gain_rows[0], meta_normed, meta_scale)
     g_gains = jnp.stack([g_gain_in, g_gain_attn, g_gain_mamba, g_gain_ffn])
     g_vectors = jnp.concatenate(
-        [g_rate * decay_rate, g_conv_taps, g_conv_shift[None], g_dt_shift, g_skip], axis=0
+        [g_rate * decay_rate, g_taps[: taps + 1], g_dt_shift, g_skip], axis=0
     ).astype(LOW)
-    s_meta, s_gains, r_xproj, r_dtproj, r_vectors, r_inproj, r_out = scatter_rows(
+    r_xproj, r_dtproj, r_vectors, r_first = scatter_rows(
         (
-            [g_meta.astype(LOW)],
-            [spread(g_gains.astype(LOW), 1, dp_count)],
-            [g_xproj],
+            [g_xproj.astype(LOW)],
             [g_dtproj],
             [spread(g_vectors, 1, dp_count)],
-            [product(normed_all.T, g_in_low), product(normed_all.T, g_gate_raw_low)],
-            [g_out],
+            [product(normed_all.T, g_in_low)],
         ),
         9,
-        shared=2,
+        s_output,
+    )
+    r_inproj, r_gateup = jnp.stack([r_first, r_second]), jnp.stack([r_gate, r_up])
+    s_meta, s_gains = scatter_rows(
+        ([g_meta.astype(LOW)], [spread(g_gains.astype(LOW), 1, dp_count)]), 12, r_inproj, r_gateup, shared=2
     )
     r_vectors = r_vectors.reshape(-1, conv_bias.shape[1])
     r_alog, r_conv = r_vectors[:states], r_vectors[states : states + taps]
     r_convbias, r_dtbias, r_skip = (r_vectors[states + taps + k][None] for k in range(3))
-    g_normed = hold(g_normed, r_out).astype(jnp.float32) + attention_side
+    g_normed = hold(g_normed, s_meta).astype(jnp.float32) + attention_side
     tokens_grad = g_mixed + norm_backward(g_normed * gain_rows[0], normed_one, scale_one)
     wide = lambda item: item.astype(jnp.float32)
     return (

time: 952 us -> 865 us (0.909)
  waiting for transfers between devices: 116 us -> 25.3 us
  Pallas kernels: 434 us -> 490 us
  blocking collectives: 29.9 us -> 0 us
  matrix products: 198 us -> 180 us
    pallas_call x9 -> x12, Pallas kernels: 405 us -> 461 us  [the longest x9 312 us: comm_call(): pl.pallas_call(functools.partial(comm_kernel, moves, len(others)), out_sh...]
    all_gather x1, waiting for transfers between devices: 31.7 us -> 0.01 us  [per_device(): g_mamba_all = lax.all_gather(g_mamba_low, 'tensor', axis=0, tiled=True)]
    psum x1 -> x0, blocking collectives: 29.9 us -> none  [per_device(): g_projected = lax.psum(hold(g_projected, s_query), 'tensor')]
    psum x2 -> x1, waiting for transfers between devices: 28.9 us -> 0.24 us  [per_device(): lax.psum(tuple((item.astype(jnp.bfloat16) for item in moved[:3])), 'tensor')]
    all_gather x1, waiting for transfers between devices: 26 us -> 3.66 us  [per_device(): ffn_all = lax.all_gather(ffn_low, 'tensor', axis=0, tiled=True)]
    dot_general x12 -> x10, matrix products: 66.3 us -> 50.6 us  [contract_cols(): lax.dot_general(former, latter, (((1,), (1,)), ((), ())), preferred_eleme...]
    all_gather x1, waiting for transfers between devices: 8.47 us -> 19.5 us  [per_device(): tokens_all = lax.all_gather(tokens, 'tensor', axis=0, tiled=True)]
    reduce_scatter x1, waiting for transfers between devices: 9.81 us -> 0.02 us  [per_device(): lax.psum_scatter(mamba_part, 'tensor', scatter_dimension=0, tiled=True)]
  transfers between devices with their start and end apart: 10 -> 9, of which waited for: 7 -> 4; matrix products, arithmetic and copies ran while one was open for 18% -> 24% of each run, Pallas kernels for 41% -> 53%
where the time goes in v3:
time: 865 us; the launch traced here: 855 us
  Pallas kernels  490 us (57%)
  matrix products  180 us (21%)
  local copies, waits for them, and re-layouts  80.5 us (9%)
  other arithmetic  62.2 us (7%)
  waiting for transfers between devices  25.3 us (3%)
  between operations  15.8 us (2%)
    pallas_call x9, Pallas kernels, comm_call(): pl.pallas_call(functools.partial(comm_kernel, moves, len(others)), out_sh...  312 us
    pallas_call x2, Pallas kernels, fused_call(): pl.pallas_call(functools.partial(fused_kernel, body, n_in, len(others), n...  138 us
    dot_general x12, matrix products, plain_dot(): return jnp.dot(former, latter, preferred_element_type=jnp.float32)  62.6 us
    dot_general x10, matrix products, contract_cols(): lax.dot_general(former, latter, (((1,), (1,)), ((), ())), preferred_eleme...  50.6 us
    dot_general x8, matrix products, contract_rows(): lax.dot_general(former, latter, (((0,), (0,)), ((), ())), preferred_eleme...  40.7 us
    unnamed x272, local copies, waits for them, and re-layouts  31.5 us
    pallas_call x4, Pallas kernels, product(): pl.pallas_call(product_kernel, grid=(rows // block,), in_specs=[pl.BlockS...  29.2 us
    dot_general x12, matrix products, mix_sum(): jnp.einsum(pattern, former, latter, preferred_element_type=jnp.float32)  19.7 us
  transfers between devices with their start and end apart: 9, of which 4 were waited for; matrix products, arithmetic and copies ran while one was open for 24% of the time, Pallas kernels for 53%

profile of v3, /device:TPU:0, one launch (start us, length us, event | category | flops | bytes accessed | tf_op | source)
XLA Modules:
  0.0 855.1 jit_solution(16237574026276093907)
XLA Ops:
  12.1 2.6 concatenate.62.refs_2_
  14.6 37.8 %gather_1.1 = (bf16[8,100,132]{2,1,0:T(8,128)(2,1)}, bf16[8,100,100]{2,1,0:T(8,128)(2,1)}, bf16[8,23,100]{2,1,0:T(8,128)(2,1)}, bf16[8,16,1600]{2,1,0:T(8,128)(2...) custom-call(bf16[100,132]{1,0:T(8,128)(2,1)} %bitcast.470, ...), custom_call_target="tpu_custom_call" | custom-call | bytes 74380000 | tf_op jit(solution)/shard_map/gather_1/pallas_call | solution.py:613
  58.3 19.5 %all-gather.5.cloned.1.call-done = bf16[1024,1600]{0,1:T(8,128)(2,1)} async-done(((bf16[256,1600]{0,1:T(8,128)(2,1)}), bf16[1024,1600]{0,1:T(8,128)(2,1)}) %all-gather.5.cloned.1.call-update) | async-done | bytes 3276816 | tf_op jit(solution)/shard_map/all_gather | solution.py:1114
  77.9 2.8 fusion.4
  80.8 6.1 fusion.101.mamba_ref
  86.9 4.2 divide_multiply_fusion.refs_0_.refs_3_
  91.1 1.8 copy-done.2
  94.8 39.3 %gather_2.1 = (bf16[8,200,1600]{2,1,0:T(8,128)(2,1)}, bf16[8,200,320]{2,1,0:T(8,128)(2,1)}, bf16[8,200,320]{2,1,0:T(8,128)(2,1)}, bf16[1024,132]{1,0:T(8,128)(2,1)}) custom-call(bf16[200,1600]{1,0:T(8,128)(2,1)} %refs_0_.2, bf16[2,200,320]{2,1,0:T(8,128)(2,1)} %refs_1_.1, bf16[1024,132]{1,0:T(8,128)(2,1)} %copy.162.refs_2_), custom_call_target="tpu_custom_call" | custom-call | bytes 89600000 | tf_op jit(solution)/shard_map/gather_2/pallas_call | solution.py:613
  140.7 8.1 fusion.99.refs_2_.refs_1_
  148.8 43.6 %scan_forward.1 = (bf16[1024,800]{1,0:T(8,128)(2,1)}, f32[1024,800]{1,0:T(8,128)}, f32[4,16,16,800]{3,2,1,0:T(8,128)}, bf16[8,200,1600]{2,1,0:T(8,128)(2,1)}, bf16[8,200,800]{2,1,0:T(8,128)(2,1)}) custom-call(f32[1024,800]{1,0:T(8,128)} %copy-done.2, bf16[1024,132]{1,0:T(8,128)(2,1)} %get-tuple-element.67.refs_1_.refs_4_, ...), custom_call_target="tpu_custom_call" | custom-call | bytes 150000000 | tf_op jit(solution)/shard_map/scan_forward/pallas_call | solution.py:937
  192.4 7.7 convolution_convert_fusion.6.refs_0_
  207.6 5.9 product.4
  213.5 2.7 copy.164
  216.2 2.6 copy.165
  218.8 1.8 fusion.65
  230.8 2.9 multiply_reduce_fusion.3
  241.0 26.3 %gather_4.1 = bf16[8,200,1376]{2,1,0:T(8,128)(2,1)} custom-call(bf16[200,1376]{1,0:T(8,128)(2,1)} %get-tuple-element.197.refs_0_, bf16[8,128]{1,0:T(8,128)(2,1)} %copy.173.refs_1_), custom_call_target="tpu_custom_call" | custom-call | bytes 55040000 | tf_op jit(solution)/shard_map/gather_4/pallas_call | solution.py:613
  269.3 2.3 multiply_reduce_fusion.2
  277.0 43.0 %gather_5.1 = (bf16[8,200,1376]{2,1,0:T(8,128)(2,1)}, bf16[8,200,1376]{2,1,0:T(8,128)(2,1)}) custom-call(bf16[200,1376]{1,0:T(8,128)(2,1)} %get-tuple-element.196.refs_0_, bf16[200,1376]{1,0:T(8,128)(2,1)} %bitcast.467, bf16[8,128]{1,0:T(8,128)(2,1)} %copy.175.refs_2_), custom_call_target="tpu_custom_call" | custom-call | bytes 110080000 | tf_op jit(solution)/shard_map/gather_5/pallas_call | solution.py:613
  320.0 9.0 %fusion.108 = f32[1024,1376]{0,1:T(8,128)S(1)} fusion(bf16[1024,1600]{1,0:T(8,128)(2,1)} %all-gather.7.cloned.1.call-done, bf16[1600,1376]{1,0:T(8,128)(2,1)} %bitcast.486), kind=kOutput, calls=%fused_computation.217 | convolution fusion | flops 4508876800 | bytes 13316096 | tf_op jit(solution)/shard_map/dot_general | solution.py:26
  329.0 2.5 copy-done.112
  333.6 3.7 all-gather.9.cloned.1.call-done
  337.3 10.0 %fusion.109 = f32[1024,1376]{0,1:T(8,128)} fusion(bf16[1600,1024]{1,0:T(8,128)(2,1)} %tie.11, bf16[1600,1376]{1,0:T(8,128)(2,1)} %bitcast.488), kind=kOutput, calls=%fused_computation.218 | convolution fusion | flops 4508876800 | bytes 13316096 | tf_op jit(solution)/shard_map/dot_general | solution.py:26
  347.4 14.1 %multiply_convert_fusion = (bf16[1024,1376]{0,1:T(8,128)(2,1)}, bf16[1024,1376]{0,1:T(8,128)(2,1)}, bf16[1024,1376]{0,1:T(8,128)(2,1)}) fusion(f32[1024,1376]{0,1:T(8,128)} %copy-done.112, f32[1024,1376]{0,1:T(8,128)} %fusion.109, bf16[1600,1024]{1,0:T(8,128)(2,1)S(1)} %copy-done.48, bf16[1600,1376]{1,0:T(8,128)(2,1)} %bitcast.396), kind=kOutput, calls=%fused_computation.22 | convolution fusion | flops 4530012160 | bytes 27406336 | tf_op jit(solution)/shard_map/dot_general | solution.py:26
  361.5 7.4 fusion.116
  369.0 6.9 add_convert_fusion
  378.5 11.0 %convolution_convert_fusion.2 = bf16[1600,1376]{1,0:T(8,128)(2,1)} fusion(bf16[1024,1600]{1,0:T(8,128)(2,1)} %all-gather.7.cloned.1.call-done, bf16[1024,1376]{0,1:T(8,128)(2,1)} %get-tuple-element.187), kind=kOutput, calls=%fused_computation.6 | convolution fusion | flops 4511078400 | bytes 10498048 | tf_op jit(solution)/shard_map/dot_general | solution.py:30
  389.6 30.6 %scatter_6.1.refs_1_ = f32[200,1376]{1,0:T(8,128)} custom-call(bf16[8,200,1376]{2,1,0:T(8,128)(2,1)} %bitcast.430), custom_call_target="tpu_custom_call" | custom-call | bytes 55040000 | tf_op jit(solution)/shard_map/scatter_6/pallas_call | solution.py:613
  420.2 7.9 convolution_convert_fusion.5
  428.1 1.8 copy-done.22
  431.9 9.3 %convolution_convert_fusion.refs_4_ = bf16[1600,1376]{1,0:T(8,128)(2,1)} fusion(bf16[1600,1024]{1,0:T(8,128)(2,1)} %tie.11, bf16[1024,1376]{0,1:T(8,128)(2,1)} %get-tuple-element.185), kind=kOutput, calls=%fused_computation.4 | convolution fusion | flops 4511078400 | bytes 10498048 | tf_op jit(solution)/shard_map/dot_general | solution.py:30
  441.2 6.9 convolution_convert_fusion.1.refs_3_
  448.1 3.1 fusion.60
  451.4 4.3 multiply_reduce_fusion
  455.7 1.9 multiply_convert_fusion.3
  457.7 4.6 convolution_convert_fusion.7
  462.4 5.4 fusion.5
  467.7 3.2 fusion.14
  473.2 6.5 fusion.13
  493.4 30.9 %scatter_10.1.refs_6_ = f32[200,1376]{1,0:T(8,128)} custom-call(bf16[8,200,1376]{2,1,0:T(8,128)(2,1)} %bitcast.394, bf16[8,128]{1,0:T(8,128)(2,1)} %copy.188.refs_1_), custom_call_target="tpu_custom_call" | custom-call | bytes 55040000 | tf_op jit(solution)/shard_map/scatter_10/pallas_call | solution.py:613
  524.4 2.4 fusion.96
  533.6 4.1 convolution_convert_fusion.3.refs_2_
  537.7 4.1 convolution_convert_fusion.4.refs_1_
  541.7 1.8 copy-done.115
  543.5 7.7 fusion.113.refs_1_.refs_0_
  551.6 1.7 copy.195
  555.9 2.5 fusion.98.former_ref
  558.4 94.5 %scan_backward.1 = (bf16[1024,800]{1,0:T(8,128)(2,1)}, f32[1024,800]{1,0:T(8,128)}, bf16[1024,800]{1,0:T(8,128)(2,1)}, bf16[1024,132]{1,0:T(8,128)(2,1)}, f32[16...) custom-call(f32[1024,800]{1,0:T(8,128)} %fusion.113.refs_1_.refs_0_,, ...), custom_call_target="tpu_custom_call" | custom-call | bytes 150000000 | tf_op jit(solution)/shard_map/scan_backward/pallas_call | solution.py:937
  652.9 2.4 convert_element_type.405
  656.9 7.7 product.6
  664.6 7.7 product.5
  673.8 50.8 %scatter_11.1 = (f32[200,800]{1,0:T(8,128)}, f32[200,800]{1,0:T(8,128)}, bf16[1024,132]{1,0:T(8,128)(2,1)}) custom-call(bf16[8,200,800]{2,1,0:T(8,128)(2,1)} %bitcast.445, bf16[8,200,800]{2,1,0:T(8,128)(2,1)} %bitcast.444, bf16[1024,132]{1,0:T(8,128)(2,1)} %get-tuple-element.79.refs_2_, bf16[8,128]{1,0:T(8,128)(2,1)} %copy.194.refs_3_), custom_call_target="tpu_custom_call" | custom-call | bytes 64000000 | tf_op jit(solution)/shard_map/scatter_11/pallas_call | solution.py:613
  724.7 11.2 %conv_backward.1 = (bf16[1024,800]{1,0:T(8,128)(2,1)}, f32[8,800]{1,0:T(8,128)}, f32[800,132]{1,0:T(8,128)}) custom-call(f32[1024,800]{1,0:T(8,128)} %get-tuple-element.77.part_ref, bf16[1024,132]{1,0:T(8,128)(2,1)} %get-tuple-element.80.proj_ref, bf16[800,132]{1,0:T(8,128)(2,1)} %copy.196.xproj_ref, f32[1024,800]{1,0:T(8,128)} %copy-done.1, ...), custom_call_target="tpu_custom_call" | custom-call | bytes 40000000 | tf_op jit(solution)/shard_map/conv_backward/pallas_call | solution.py:695
  735.9 6.2 fusion.114
  742.1 6.9 fusion.3
  751.8 2.1 fusion.115
  753.9 2.1 multiply_reduce_fusion.5
  757.7 2.0 convolution_convert_fusion.8
  762.6 2.3 convert_element_type.409
  764.9 2.2 convert_element_type.412
  769.7 8.0 product.7
  777.7 24.7 %scatter_9.1 = (f32[100,132]{1,0:T(8,128)}, f32[100,100]{1,0:T(8,128)}, f32[23,100]{1,0:T(8,128)}, f32[200,800]{1,0:T(8,128)}) custom-call(bf16[8,100,132]{2,1,0:T(8,128)(2,1)} %reshape.706.refs_0_, bf16[8,100,100]{2,1,0:T(8,128)(2,1)} %copy.211.refs_1_, bf16[8,23,100]{2,1,0:T(8,128)(2,1)} %maximum_bitcast_fusion.3.refs_2_, bf16[8,200,800]{2,1,0:T(8,128)(2,1)} %bitcast.446, ...), custom_call_target="tpu_custom_call" | custom-call | bytes 37100000 | tf_op jit(solution)/shard_map/scatter_9/pallas_call | solution.py:613
  805.7 2.4 pad_maximum_fusion.1.refs_2_
  808.0 28.3 %scatter_12.1 = (f32[16,1600]{1,0:T(8,128)}, f32[4,200]{1,0:T(4,128)}) custom-call(bf16[8,16,1600]{2,1,0:T(8,128)(2,1)} %bitcast.447, bf16[8,4,200]{2,1,0:T(4,128)(2,1)} %maximum_bitcast_fusion.4.refs_1_, f32[2,200,800]{2,1,0:T(8,128)} %pad_maximum_fusion.1.refs_2_, f32[2,200,1376]{2,1,0:T(8,128)} %pad_maximum_fusion.refs_3_), custom_call_target="tpu_custom_call" | custom-call | bytes 5280000 | tf_op jit(solution)/shard_map/scatter_12/pallas_call | solution.py:613
  (444 shorter events, 111.5 us)
Async XLA Ops:
  7.2 50.4 %copy-start.87 = (s32[1024]{0:T(1024)S(1)}, s32[1024]{0:T(1024)}, u32[]{:S(2)}) copy-start(s32[1024]{0:T(1024)} %param.20) | copy-start | bytes 12292
  7.2 49.0 %copy-start.50 = (bf16[256,1600]{0,1:T(8,128)(2,1)S(1)}, bf16[256,1600]{0,1:T(8,128)(2,1)}, u32[]{:S(2)}) copy-start(bf16[256,1600]{0,1:T(8,128)(2,1)} %param.21) | copy-start | bytes 2457604
  7.2 70.7 %all-gather.5.cloned.1.call-start = ((), (), s32[]{:S(2)}) async-start(), calls=%async_computation.4 | async-start | bytes 4096000 | tf_op jit(solution)/shard_map/all_gather | solution.py:1114
  7.9 193.2 %all-gather.7.cloned.1.call-start = ((), (), s32[]{:S(2)}) async-start(), calls=%async_computation.5 | async-start | bytes 4259840 | tf_op jit(solution)/shard_map/all_gather | solution.py:1163
  53.4 152.9 %copy-start.76 = (f32[1600]{0:T(1024)}, f32[1600]{0:T(1024)S(1)}, u32[]{:S(2)}) copy-start(f32[1600]{0:T(1024)S(1)} %mul.690) | copy-start | bytes 19204
  54.2 81.5 %copy-start.64 = (f32[23,8,100]{2,0,1:T(8,128)}, f32[23,8,100]{2,0,1:T(8,128)S(1)}, u32[]{:S(2)}) copy-start(f32[23,8,100]{2,0,1:T(8,128)S(1)} %convert_bitcast_fusion) | copy-start | bytes 220804
  56.3 34.9 %copy-start.55 = (bf16[800,132]{0,1:T(8,128)(2,1)}, bf16[800,132]{0,1:T(8,128)(2,1)S(1)}, u32[]{:S(2)}) copy-start(bf16[800,132]{0,1:T(8,128)(2,1)S(1)} %reshape.659) | copy-start | bytes 633604
  80.7 58.5 %copy-start.102 = (f32[1024]{0:T(1024)}, f32[1024]{0:T(1024)S(1)}, u32[]{:S(2)}) copy-start(f32[1024]{0:T(1024)S(1)} %add_rsqrt_fusion) | copy-start | bytes 12292
  93.8 42.7 %copy-start.85 = (bf16[8,100,100]{2,1,0:T(8,128)(2,1)S(1)}, bf16[8,100,100]{2,1,0:T(8,128)(2,1)}, u32[]{:S(2)}) copy-start(bf16[8,100,100]{2,1,0:T(8,128)(2,1)} %get-tuple-element.69) | copy-start | bytes 480004
  94.8 43.7 %copy-start.43 = (bf16[8,16,1600]{2,1,0:T(8,128)(2,1)S(1)}, bf16[8,16,1600]{2,1,0:T(8,128)(2,1)}, u32[]{:S(2)}) copy-start(bf16[8,16,1600]{2,1,0:T(8,128)(2,1)} %get-tuple-element.59) | copy-start | bytes 1228804
  134.1 4.5 copy-start.6
  134.1 133.2 %reduce-scatter.5.cloned.1.call-start = ((), (), s32[]{:S(2)}) async-start(), calls=%async_computation.6 | async-start | bytes 4096000 | tf_op jit(solution)/shard_map/reduce_scatter | solution.py:1178
  138.9 9.9 %copy-start.94 = (f32[256]{0:T(256)}, f32[256]{0:T(256)S(1)}, u32[]{:S(2)}) copy-start(f32[256]{0:T(256)S(1)} %add_rsqrt_fusion.5) | copy-start | bytes 3076
  138.9 67.3 %copy-start.92 = (f32[8,16]{1,0:T(8,128)}, f32[8,16]{1,0:T(8,128)S(1)}, u32[]{:S(2)}) copy-start(f32[8,16]{1,0:T(8,128)S(1)} %add_rsqrt_fusion.1) | copy-start | bytes 1540
  139.2 79.5 %copy-start.9 = (bf16[256,1600]{0,1:T(8,128)(2,1)}, bf16[256,1600]{0,1:T(8,128)(2,1)S(1)}, u32[]{:S(2)}) copy-start(bf16[256,1600]{0,1:T(8,128)(2,1)S(1)} %fusion.45) | copy-start | bytes 2457604
  202.4 134.9 %all-gather.9.cloned.1.call-start = ((), (), s32[]{:S(2)}) async-start(), calls=%async_computation.7 | async-start | bytes 4096000 | tf_op jit(solution)/shard_map/all_gather | solution.py:1190
  206.3 14.4 %copy-start.65 = (f32[256,32]{0,1:T(8,128)}, f32[256,32]{0,1:T(8,128)S(1)}, u32[]{:S(2)}) copy-start(f32[256,32]{0,1:T(8,128)S(1)} %get-tuple-element.207) | copy-start | bytes 98308
  206.4 14.5 %copy-start.29 = (bf16[8,16,1600]{2,1,0:T(8,128)(2,1)}, bf16[8,16,1600]{2,1,0:T(8,128)(2,1)S(1)}, u32[]{:S(2)}) copy-start(bf16[8,16,1600]{2,1,0:T(8,128)(2,1)S(1)} %multiply_convert_fusion.5) | copy-start | bytes 1228804
  223.4 5.4 copy-start
  274.0 174.1 %reduce-scatter.7.cloned.1.call-start = ((), (), s32[]{:S(2)}) async-start(), calls=%async_computation.8 | async-start | bytes 4096000 | tf_op jit(solution)/shard_map/reduce_scatter | solution.py:1201
  337.3 10.1 %copy-start.48 = (bf16[1600,1024]{1,0:T(8,128)(2,1)S(1)}, bf16[1600,1024]{1,0:T(8,128)(2,1)}, u32[]{:S(2)}) copy-start(bf16[1600,1024]{1,0:T(8,128)(2,1)} %tie.11) | copy-start | bytes 9830404
  337.3 24.2 %slice-start.4 = ((s8[4505600]{0:T(1024)(128)(4,1)}), s8[4194304]{0:T(1024)(128)(4,1)S(1)}, s32[]{:S(2)}) async-start(s8[4505600]{0:T(1024)(128)(4,1)} %bitcast.397), calls=%async_computation.17 | async-start | bytes 8388608
  337.3 31.6 %slice-start.10 = ((s8[4505600]{0:T(1024)(128)(4,1)}), s8[4194304]{0:T(1024)(128)(4,1)S(1)}, s32[]{:S(2)}) async-start(s8[4505600]{0:T(1024)(128)(4,1)} %bitcast.489), calls=%async_computation.23 | async-start | bytes 8388608
  347.4 14.1 %slice-start.5 = ((s8[4505600]{0:T(1024)(128)(4,1)}), s8[311296]{0:T(1024)(128)(4,1)S(1)}, s32[]{:S(2)}) async-start(s8[4505600]{0:T(1024)(128)(4,1)} %bitcast.397), calls=%async_computation.18 | async-start | bytes 622592
  347.4 21.6 %slice-start.11 = ((s8[4505600]{0:T(1024)(128)(4,1)}), s8[311296]{0:T(1024)(128)(4,1)S(1)}, s32[]{:S(2)}) async-start(s8[4505600]{0:T(1024)(128)(4,1)} %bitcast.489), calls=%async_computation.24 | async-start | bytes 622592
  361.5 7.4 copy-start.117
  375.9 165.9 %all-gather.11.cloned.1.call-start = ((), (), s32[]{:S(2)}) async-start(), calls=%async_computation.9 | async-start | bytes 4096000 | tf_op jit(solution)/shard_map/all_gather | solution.py:1215
  431.9 9.3 %copy-start.49 = (bf16[1600,1024]{1,0:T(8,128)(2,1)S(1)}, bf16[1600,1024]{1,0:T(8,128)(2,1)}, u32[]{:S(2)}) copy-start(bf16[1600,1024]{1,0:T(8,128)(2,1)} %tie.11) | copy-start | bytes 9830404
  431.9 9.3 %copy-start.118 = (bf16[1024,1376]{0,1:T(8,128)(2,1)S(1)}, bf16[1024,1376]{0,1:T(8,128)(2,1)}, u32[]{:S(2)}) copy-start(bf16[1024,1376]{0,1:T(8,128)(2,1)} %get-tuple-element.186) | copy-start | bytes 8454148
  451.3 4.3 copy-start.19
  451.3 4.3 copy-start.88
  451.3 4.3 copy-start.89
  451.3 4.3 copy-start.98
  451.3 4.3 copy-start.105
  455.7 6.7 slice-start
  457.6 4.7 copy-start.53
  457.6 4.7 slice-start.1
  457.6 4.7 copy-start.72
  462.3 5.4 copy-start.35
  471.7 200.7 %reduce-scatter.9.cloned.1.call-start = ((), (), s32[]{:S(2)}) async-start(), calls=%async_computation.10 | async-start | bytes 4096000 | tf_op jit(solution)/shard_map/reduce_scatter | solution.py:1242
  473.2 6.6 copy-start.45
  473.2 6.6 copy-start.47
  481.8 5.4 slice-start.6
  551.3 4.6 copy-start.25
  551.3 4.6 copy-start.77
  551.3 4.6 copy-start.103
  551.3 211.3 %all-reduce.6.cloned.1.call-start = ((), (), s32[]{:S(2)}) async-start(), calls=%async_computation.12 | async-start | bytes 3276800 | tf_op jit(solution)/shard_map/psum | solution.py:1266
  672.3 167.9 %reduce-scatter.11.cloned.1.call-start = ((), (), s32[]{:S(2)}) async-start(), calls=%async_computation.11 | async-start | bytes 4096000 | tf_op jit(solution)/shard_map/reduce_scatter | solution.py:1285
  735.9 6.2 copy-start.114
  735.9 6.2 copy-start.116
  749.0 4.9 copy-start.28
  749.0 4.9 copy-start.58
  751.7 4.3 copy-start.108
  756.0 4.8 copy-start.32
  756.3 4.5 copy-start.61
  762.4 5.7 copy-start.107
  762.4 5.8 copy-start.67
  762.6 4.5 copy-start.83
  777.7 27.2 %copy-start.106 = (f32[1600]{0:T(1024)S(1)}, f32[1600]{0:T(1024)}, u32[]{:S(2)}) copy-start(f32[1600]{0:T(1024)} %get-tuple-element.188) | copy-start | bytes 19204
  777.7 28.0 %copy-start.69 = (f32[200,800]{1,0:T(8,128)S(1)}, f32[200,800]{1,0:T(8,128)}, u32[]{:S(2)}) copy-start(f32[200,800]{1,0:T(8,128)} %get-tuple-element.90) | copy-start | bytes 1920004
  805.7 30.7 %copy-start.86 = (f32[100,132]{1,0:T(8,128)S(1)}, f32[100,132]{1,0:T(8,128)}, u32[]{:S(2)}) copy-start(f32[100,132]{1,0:T(8,128)} %get-tuple-element.96) | copy-start | bytes 158404
  808.0 29.1 %copy-start.91 = (f32[100,100]{1,0:T(8,128)S(1)}, f32[100,100]{1,0:T(8,128)}, u32[]{:S(2)}) copy-start(f32[100,100]{1,0:T(8,128)} %get-tuple-element.97) | copy-start | bytes 120004
  808.0 31.1 %copy-start.5 = (f32[256,1600]{0,1:T(8,128)S(1)}, f32[256,1600]{0,1:T(8,128)}, u32[]{:S(2)}) copy-start(f32[256,1600]{0,1:T(8,128)} %copy-done.3) | copy-start | bytes 4915204
  808.0 31.1 %copy-start.63 = (bf16[256,1600]{0,1:T(8,128)(2,1)S(1)}, bf16[256,1600]{0,1:T(8,128)(2,1)}, u32[]{:S(2)}) copy-start(bf16[256,1600]{0,1:T(8,128)(2,1)} %reduce-scatter.9.cloned.1.call-done) | copy-start | bytes 2457604
  (76 other events, 165.4 us)
Sparse Core Ops, SparseCore 0:
  9.6 68.2 all-gather.4
  134.3 66.8 all-gather.6
  203.4 61.0 reduce-scatter.4
  274.1 63.1 all-gather.8
  376.0 60.6 reduce-scatter.6
  471.8 62.6 all-gather.10
  551.4 59.6 reduce-scatter.8
  672.5 90.1 all-reduce.5
  765.0 61.4 reduce-scatter.10
